TPU v7x, 512 devices: a whole 4x4x16 slice. The times are simulated.
512 devices in a mesh: patch: 128 (over y, z, core), rep: 4 (over x).
Axes of the slice: x: 4, y: 4, z: 16, core: 2. Of those that a mesh axis runs over, the one named last changes fastest.
Arguments:
- nodes: bfloat16 [4, 65536, 256], P('rep', 'patch'), may hold values from -6 to 6
- edges: bfloat16 [4, 196608, 256], P('rep', 'patch'), may hold values from -6 to 6
- edge_ends: int32 [196608, 2], P('patch'), may hold values from 0 to 543, as said below
- edge_count: int32 [128], P('patch'), may hold values from 768 to 1536, as said below
- send_rows: int32 [256, 16], P('patch'), may hold values from 0 to 511, as said below
- cotangent: bfloat16 [4, 65536, 256], P('rep', 'patch'), may hold values from -6 to 6
- edge_first: bfloat16 [768, 256], replicated, may hold values from -0.21875 to 0.21875
- edge_second: bfloat16 [256, 256], replicated, may hold values from -0.375 to 0.375
- node_first: bfloat16 [512, 256], replicated, may hold values from -0.25 to 0.25
- node_second: bfloat16 [256, 256], replicated, may hold values from -0.375 to 0.375
Outputs:
- new_nodes: bfloat16 [4, 65536, 256], P('rep', 'patch')
- grad_nodes: bfloat16 [4, 65536, 256], P('rep', 'patch')
- grad_edges: bfloat16 [4, 196608, 256], P('rep', 'patch')
- grad_edge_first: bfloat16 [768, 256], replicated
- grad_edge_second: bfloat16 [256, 256], replicated
- grad_node_first: bfloat16 [512, 256], replicated
- grad_node_second: bfloat16 [256, 256], replicated
Inputs may be any that keep to these rules, and one draw needn't show every extreme that they name: `edge_ends`: in patch p's block, row j gives edge slot j: column 0 is a vertex of p; column 1 is a vertex of p, or 512 + h * 16 + s with h < 2, which names the vertex in slot s of row h of the send_rows block of patch (p + h + 1) mod 128. Padding slots hold ends of the same form. `edge_count`: live edge slots of each patch; slots at or beyond it are padding. Some patch has all 1536 live. `send_rows`: each patch's block has 2 rows of 16 distinct vertices of that patch, in its own numbering.
All inputs are finite; a program needn't handle non-finite values.
Results may differ from a plain program's by a relative error of at most 0.0084.
Values may be sent and summed in bfloat16 or wider, within the bound.
No kernel may reach another device: no remote copies, remote signals or barrier semaphores. Data moves between devices by JAX's collectives and lax.ppermute only.
A program may use at most 64 MiB of HBM per device.

v0:
```python
import jax
import jax.numpy as jnp
from jax import lax
from jax.sharding import PartitionSpec as P

EPS = 1e-05


def passed_along(block, axis, distance):
    devices = range(lax.axis_size(axis))
    route = [((i - distance) % len(devices), i) for i in devices]
    return lax.ppermute(block, axis, route)


def normalize(values):
    average = jnp.mean(values, axis=-1, keepdims=True)
    centred = values - average
    inv_scale = lax.rsqrt(jnp.mean(centred * centred, axis=-1, keepdims=True) + EPS)
    return (centred * inv_scale, inv_scale)


def norm_back(upstream, normed, inv_scale):
    return inv_scale * (
        upstream
        - jnp.mean(upstream, axis=-1, keepdims=True)
        - normed * jnp.mean(upstream * normed, axis=-1, keepdims=True)
    )


def silu_slope(pre):
    sigma = jax.nn.sigmoid(pre)
    return sigma * (1.0 + pre * (1.0 - sigma))


def matmul(left, right):
    return jnp.dot(left, right, preferred_element_type=jnp.float32)


def outer_sum(left, right):
    return lax.dot_general(
        left, right, (((0,), (0,)), ((), ())), preferred_element_type=jnp.float32
    )


def fetch_seam(outgoing):
    peer_count = outgoing.shape[0]
    pieces = [
        passed_along(outgoing[offset], "patch", -(offset + 1)) for offset in range(peer_count)
    ]
    return jnp.stack(pieces)


def return_seam(totals):
    peer_count = totals.shape[0]
    pieces = [passed_along(totals[offset], "patch", offset + 1) for offset in range(peer_count)]
    return jnp.stack(pieces)


def gather_ends(local_rows, send_rows, first_end, second_end):
    halo = fetch_seam(local_rows[send_rows])
    table = jnp.concatenate([local_rows, halo.reshape(-1, local_rows.shape[1])], axis=0)
    return (local_rows[first_end], table[second_end])


def scatter_ends(first_terms, second_terms, send_rows, first_end, second_end, verts):
    seam_total = send_rows.shape[0] * send_rows.shape[1]
    totals = jax.ops.segment_sum(first_terms, first_end, verts + seam_total) + jax.ops.segment_sum(
        second_terms, second_end, verts + seam_total
    )
    features = totals.shape[1]
    returned = return_seam(totals[verts:].reshape(send_rows.shape + (features,)))
    return totals[:verts].at[send_rows.reshape(-1)].add(returned.reshape(-1, features))


def local(
    nodes,
    edges,
    edge_ends,
    edge_count,
    send_rows,
    cotangent,
    edge_first,
    edge_second,
    node_first,
    node_second,
):
    node_rows = nodes[0]
    edge_rows = edges[0]
    cot_wide = cotangent[0].astype(jnp.float32)
    verts, features = node_rows.shape
    first_end = edge_ends[:, 0]
    second_end = edge_ends[:, 1]
    alive = (jnp.arange(edge_rows.shape[0], dtype=jnp.int32) < edge_count[0]).astype(jnp.float32)[
        :, None
    ]
    first_rows, second_rows = gather_ends(node_rows, send_rows, first_end, second_end)
    edge_pre = (
        matmul(edge_rows, edge_first[:features])
        + matmul(first_rows, edge_first[features : 2 * features])
        + matmul(second_rows, edge_first[2 * features :])
    )
    edge_hidden = jax.nn.silu(edge_pre).astype(jnp.bfloat16)
    edge_normed, edge_inv = normalize(matmul(edge_hidden, edge_second))
    new_edge = ((edge_rows.astype(jnp.float32) + edge_normed) * alive).astype(jnp.bfloat16)
    new_wide = lax.optimization_barrier(new_edge).astype(jnp.float32)
    aggregate = scatter_ends(new_wide, new_wide, send_rows, first_end, second_end, verts).astype(
        jnp.bfloat16
    )
    node_pre = matmul(node_rows, node_first[:features]) + matmul(aggregate, node_first[features:])
    node_hidden = jax.nn.silu(node_pre).astype(jnp.bfloat16)
    node_normed, node_inv = normalize(matmul(node_hidden, node_second))
    new_nodes = (node_rows.astype(jnp.float32) + node_normed).astype(jnp.bfloat16)
    d_node_out = norm_back(cot_wide, node_normed, node_inv).astype(jnp.bfloat16)
    grad_ns = outer_sum(node_hidden, d_node_out)
    d_node_pre = (matmul(d_node_out, node_second.T) * silu_slope(node_pre)).astype(jnp.bfloat16)
    grad_nf = jnp.concatenate(
        [outer_sum(node_rows, d_node_pre), outer_sum(aggregate, d_node_pre)], axis=0
    )
    d_direct = matmul(d_node_pre, node_first[:features].T)
    d_aggregate = matmul(d_node_pre, node_first[features:].T).astype(jnp.bfloat16)
    d_first_rows, d_second_rows = gather_ends(d_aggregate, send_rows, first_end, second_end)
    d_new_edge = alive * (d_first_rows.astype(jnp.float32) + d_second_rows.astype(jnp.float32))
    d_edge_out = norm_back(d_new_edge, edge_normed, edge_inv).astype(jnp.bfloat16)
    grad_es = outer_sum(edge_hidden, d_edge_out)
    d_edge_pre = (matmul(d_edge_out, edge_second.T) * silu_slope(edge_pre)).astype(jnp.bfloat16)
    grad_ef = jnp.concatenate(
        [
            outer_sum(edge_rows, d_edge_pre),
            outer_sum(first_rows, d_edge_pre),
            outer_sum(second_rows, d_edge_pre),
        ],
        axis=0,
    )
    grad_edges = (d_new_edge + matmul(d_edge_pre, edge_first[:features].T)).astype(jnp.bfloat16)
    d_first_end = matmul(d_edge_pre, edge_first[features : 2 * features].T)
    d_second_end = matmul(d_edge_pre, edge_first[2 * features :].T)
    end_terms = scatter_ends(d_first_end, d_second_end, send_rows, first_end, second_end, verts)
    grad_nodes = (cot_wide + d_direct + end_terms).astype(jnp.bfloat16)
    grad_ef, grad_es, grad_nf, grad_ns = lax.psum(
        (grad_ef, grad_es, grad_nf, grad_ns), ("patch", "rep")
    )
    return (
        new_nodes[None],
        grad_nodes[None],
        grad_edges[None],
        grad_ef.astype(jnp.bfloat16),
        grad_es.astype(jnp.bfloat16),
        grad_nf.astype(jnp.bfloat16),
        grad_ns.astype(jnp.bfloat16),
    )


def solution(mesh):
    placed = (
        P("rep", "patch", None),
        P("rep", "patch", None),
        P("patch", None),
        P("patch"),
        P("patch", None),
        P("rep", "patch", None),
        P(),
        P(),
        P(),
        P(),
    )
    return jax.shard_map(
        local,
        mesh=mesh,
        in_specs=placed,
        out_specs=(
            P("rep", "patch", None),
            P("rep", "patch", None),
            P("rep", "patch", None),
            P(),
            P(),
            P(),
            P(),
        ),
        check_vma=False,
    )
```

profile of v0, /device:TPU:1, one launch (start us, length us, event | category | flops | bytes accessed | tf_op | source)
XLA Modules:
  0.0 271.1 jit_solution(1852937462430202631)
XLA Ops:
  1.5 1.6 gather_fusion.1
  3.1 8.7 %collective-permute-start = (bf16[16,256]{1,0:T(8,128)(2,1)S(1)}, bf16[16,256]{1,0:T(8,128)(2,1)S(1)}, u32[]{:S(2)}, u32[]{:S(2)}) collective-permute-start(bf16[16,256]{1,0:T(8,128)(2,1)S(1)} %get-tuple-element.46), channel_id=1, source_target_pairs={{4,0},{8,4},{12,8},{16,12},{20,16},{24,20},{28,24},{32,28},{36,32}... | collective-permute-start | bytes 24584 | tf_op jit(solution)/shard_map/ppermute | solution.py:12
  11.8 8.2 %collective-permute-start.1 = (bf16[16,256]{1,0:T(8,128)(2,1)S(1)}, bf16[16,256]{1,0:T(8,128)(2,1)S(1)}, u32[]{:S(2)}, u32[]{:S(2)}) collective-permute-start(bf16[16,256]{1,0:T(8,128)(2,1)S(1)} %get-tuple-element.47), channel_id=1, source_target_pairs={{8,0},{12,4},{16,8},{20,12},{24,16},{28,20},{32,24},{36,28},{40,32... | collective-permute-start | bytes 24584 | tf_op jit(solution)/shard_map/ppermute | solution.py:12
  23.9 2.0 fusion.38
  26.0 5.4 %gather_fusion = bf16[1536,256]{1,0:T(8,128)(2,1)} fusion(bf16[512,256]{1,0:T(8,128)(2,1)S(1)} %bitcast.87, s32[2048]{0:T(1024)S(1)} %get-tuple-element.57), kind=kCustom, calls=%fused_computation | custom fusion | bytes 1579008 | tf_op jit(solution)/shard_map/gather | solution.py:62
  37.0 5.4 %gather_fusion.2 = bf16[1536,256]{1,0:T(8,128)(2,1)} fusion(bf16[544,256]{1,0:T(8,128)(2,1)S(1)} %copy.58, s32[2048]{0:T(1024)S(1)} %get-tuple-element.56), kind=kCustom, calls=%fused_computation.2 | custom fusion | bytes 1579008 | tf_op jit(solution)/shard_map/gather | solution.py:62
  42.3 2.8 %multiply_convert_fusion.2 = (bf16[1536,256]{1,0:T(8,128)(2,1)S(1)}, f32[1536,256]{1,0:T(8,128)}) fusion(f32[1536,256]{1,0:T(8,128)S(1)} %copy-done.14, bf16[1536,256]{1,0:T(8,128)(2,1)} %gather_fusion.2, bf16[768,256]{1,0:T(8,128)(2,1)} %param.16), kind=kOutput, calls=%fused_computation.24 | convolution fusion | flops 203685888 | bytes 4849664 | tf_op jit(solution)/shard_map/dot_general | solution.py:36
  48.6 9.4 %scatter_custom_fusion.1 = f32[544,256]{1,0:T(8,128)S(1)} fusion(s32[1536]{0:T(1024)} %get-tuple-element.30, f32[1536,256]{1,0:T(8,128)} %copy.59, f32[]{:T(128)} %constant.10.clone.1), kind=kCustom, calls=%fused_computation.60 | custom fusion | flops 393216 | bytes 557568 | tf_op jit(solution)/shard_map/scatter-add | solution.py:67
  58.0 10.1 %scatter_custom_fusion = f32[544,256]{1,0:T(8,128)} fusion(s32[1536]{0:T(1024)} %get-tuple-element.33, f32[1536,256]{1,0:T(8,128)} %copy.59, f32[]{:T(128)} %constant.10.clone.1), kind=kCustom, calls=%fused_computation.62 | custom fusion | flops 393216 | bytes 557568 | tf_op jit(solution)/shard_map/scatter-add | solution.py:67
  69.2 3.3 %collective-permute-start.2 = (f32[16,256]{1,0:T(8,128)S(1)}, f32[16,256]{1,0:T(8,128)S(1)}, u32[]{:S(2)}, u32[]{:S(2)}) collective-permute-start(f32[16,256]{1,0:T(8,128)S(1)} %get-tuple-element.40), channel_id=1, source_target_pairs={{508,0},{0,4},{4,8},{8,12},{12,16},{16,20},{20,24},{24,28},{28,32}... | collective-permute-start | bytes 49160 | tf_op jit(solution)/shard_map/ppermute | solution.py:12
  72.5 1.9 collective-permute-start.3
  74.5 5.9 %collective-permute-done.3 = f32[16,256]{1,0:T(8,128)S(1)} collective-permute-done((f32[16,256]{1,0:T(8,128)S(1)}, f32[16,256]{1,0:T(8,128)S(1)}, u32[]{:S(2)}, u32[]{:S(2)}) %collective-permute-start.3) | collective-permute-done | bytes 16416 | tf_op jit(solution)/shard_map/ppermute | solution.py:12
  88.7 2.3 collective-permute-start.4
  91.0 2.1 collective-permute-start.5
  94.0 5.4 %gather_fusion.3 = bf16[1536,256]{1,0:T(8,128)(2,1)} fusion(bf16[512,256]{1,0:T(8,128)(2,1)S(1)} %convolution_convert_fusion, s32[2048]{0:T(1024)S(1)} %copy-done.36), kind=kCustom, calls=%fused_computation.3 | custom fusion | bytes 1579008 | tf_op jit(solution)/shard_map/gather | solution.py:62
  102.3 5.5 %gather_fusion.5 = bf16[1536,256]{1,0:T(8,128)(2,1)} fusion(bf16[544,256]{1,0:T(8,128)(2,1)S(1)} %pad_maximum_fusion.3, s32[2048]{0:T(1024)} %copy-done.34), kind=kCustom, calls=%fused_computation.5 | custom fusion | bytes 1579008 | tf_op jit(solution)/shard_map/gather | solution.py:62
  117.7 1.6 fusion.29
  119.3 1.6 fusion.32
  120.8 9.6 %scatter_custom_fusion.4 = f32[544,256]{1,0:T(8,128)S(1)} fusion(s32[1536]{0:T(1024)} %get-tuple-element.30, f32[1536,256]{1,0:T(8,128)} %fusion.29, f32[]{:T(128)} %constant.10.clone.1), kind=kCustom, calls=%fused_computation.56 | custom fusion | flops 393216 | bytes 557568 | tf_op jit(solution)/shard_map/scatter-add | solution.py:67
  131.5 10.1 %scatter_custom_fusion.3 = f32[544,256]{1,0:T(8,128)} fusion(s32[1536]{0:T(1024)} %get-tuple-element.33, f32[1536,256]{1,0:T(8,128)} %fusion.32, f32[]{:T(128)} %constant.10.clone.1), kind=kCustom, calls=%fused_computation.58 | custom fusion | flops 393216 | bytes 557568 | tf_op jit(solution)/shard_map/scatter-add | solution.py:67
  141.6 2.2 copy.65
  147.1 3.9 %collective-permute-start.6 = (f32[16,256]{0,1:T(8,128)}, f32[16,256]{0,1:T(8,128)}, u32[]{:S(2)}, u32[]{:S(2)}) collective-permute-start(f32[16,256]{0,1:T(8,128)} %get-tuple-element.38), channel_id=1, source_target_pairs={{508,0},{0,4},{4,8},{8,12},{12,16},{16,20},{20,24},{24,28},{28,32}... | collective-permute-start | bytes 49160 | tf_op jit(solution)/shard_map/ppermute | solution.py:12
  151.0 2.8 %collective-permute-start.7 = (f32[16,256]{0,1:T(8,128)}, f32[16,256]{0,1:T(8,128)}, u32[]{:S(2)}, u32[]{:S(2)}) collective-permute-start(f32[16,256]{0,1:T(8,128)} %get-tuple-element.39), channel_id=1, source_target_pairs={{504,0},{508,4},{0,8},{4,12},{8,16},{12,20},{16,24},{20,28},{24,32... | collective-permute-start | bytes 49160 | tf_op jit(solution)/shard_map/ppermute | solution.py:12
  153.8 110.8 %all-reduce.2 = (bf16[768,256]{1,0:T(8,128)(2,1)}, bf16[256,256]{1,0:T(8,128)(2,1)}, bf16[512,256]{1,0:T(8,128)(2,1)}, bf16[256,256]{1,0:T(8,128)(2,1)}) all-reduce(f32[768,256]{1,0:T(8,128)S(1)} %pad_maximum_fusion, f32[256,256]{1,0:T(8,128)} %fusion.54, ...), channel_id=1, replica_groups=mesh['patch'=128,'rep'=4] {'patch','rep'}, use_global_device_ids=true, to_apply=%region_14.15 | all-reduce | flops 458752 | bytes 2752512 | tf_op jit(solution)/shard_map/psum | solution.py:139
  (169 shorter events, 46.7 us)
Async XLA Ops:
  0.6 44.5 %copy-start = (bf16[256,256]{1,0:T(8,128)(2,1)S(1)}, bf16[256,256]{1,0:T(8,128)(2,1)}, u32[]{:S(2)}) copy-start(bf16[256,256]{1,0:T(8,128)(2,1)} %param.17) | copy-start | bytes 393220
  0.6 25.4 %copy-start.1 = (bf16[1,512,256]{2,1,0:T(8,128)(2,1)S(1)}, bf16[1,512,256]{2,1,0:T(8,128)(2,1)}, u32[]{:S(2)}) copy-start(bf16[1,512,256]{2,1,0:T(8,128)(2,1)} %param.10) | copy-start | bytes 786436
  1.5 24.5 %copy-start.37 = (s32[1024]{0:T(1024)}, s32[1024]{0:T(1024)S(1)}, u32[]{:S(2)}) copy-start(s32[1024]{0:T(1024)S(1)} %pad_clamp_fusion.2) | copy-start | bytes 12292
  3.1 33.5 %collective-permute-start = (bf16[16,256]{1,0:T(8,128)(2,1)S(1)}, bf16[16,256]{1,0:T(8,128)(2,1)S(1)}, u32[]{:S(2)}, u32[]{:S(2)}) collective-permute-start(bf16[16,256]{1,0:T(8,128)(2,1)S(1)} %get-tuple-element.46), channel_id=1, source_target_pairs={{4,0},{8,4},{12,8},{16,12},{20,16},{24,20},{28,24},{32,28},{36,32}... | collective-permute-start | bytes 24584 | tf_op jit(solution)/shard_map/ppermute | solution.py:12
  11.8 24.8 %collective-permute-start.1 = (bf16[16,256]{1,0:T(8,128)(2,1)S(1)}, bf16[16,256]{1,0:T(8,128)(2,1)S(1)}, u32[]{:S(2)}, u32[]{:S(2)}) collective-permute-start(bf16[16,256]{1,0:T(8,128)(2,1)S(1)} %get-tuple-element.47), channel_id=1, source_target_pairs={{8,0},{12,4},{16,8},{20,12},{24,16},{28,20},{32,24},{36,28},{40,32... | collective-permute-start | bytes 24584 | tf_op jit(solution)/shard_map/ppermute | solution.py:12
  26.0 5.4 %copy-start.35 = (s32[2048]{0:T(1024)}, s32[2048]{0:T(1024)S(1)}, u32[]{:S(2)}) copy-start(s32[2048]{0:T(1024)S(1)} %get-tuple-element.57) | copy-start | bytes 24580
  26.0 10.9 %copy-start.34 = (s32[2048]{0:T(1024)}, s32[2048]{0:T(1024)S(1)}, u32[]{:S(2)}) copy-start(s32[2048]{0:T(1024)S(1)} %get-tuple-element.56) | copy-start | bytes 24580
  26.0 5.4 %copy-start.6 = (bf16[1,1536,256]{2,1,0:T(8,128)(2,1)S(1)}, bf16[1,1536,256]{2,1,0:T(8,128)(2,1)}, u32[]{:S(2)}) copy-start(bf16[1,1536,256]{2,1,0:T(8,128)(2,1)} %param.11) | copy-start | bytes 2359300
  26.0 5.4 %copy-start.15 = (bf16[768,256]{1,0:T(8,128)(2,1)S(1)}, bf16[768,256]{1,0:T(8,128)(2,1)}, u32[]{:S(2)}) copy-start(bf16[768,256]{1,0:T(8,128)(2,1)} %param.16) | copy-start | bytes 1179652
  37.0 5.4 %copy-start.14 = (f32[1536,256]{1,0:T(8,128)S(1)}, f32[1536,256]{1,0:T(8,128)}, u32[]{:S(2)}) copy-start(f32[1536,256]{1,0:T(8,128)} %convolution_add_fusion.2) | copy-start | bytes 4718596
  48.6 25.8 %copy-start.42 = (s32[32,1]{0,1:T(1,128)S(1)}, s32[32,1]{0,1:T(1,128)}, u32[]{:S(2)}) copy-start(s32[32,1]{0,1:T(1,128)} %reshape.115) | copy-start | bytes 388
  68.0 13.6 %copy-start.20 = (bf16[512,256]{1,0:T(8,128)(2,1)S(1)}, bf16[512,256]{1,0:T(8,128)(2,1)}, u32[]{:S(2)}) copy-start(bf16[512,256]{1,0:T(8,128)(2,1)} %param.18) | copy-start | bytes 786436
  69.2 5.3 %collective-permute-start.2 = (f32[16,256]{1,0:T(8,128)S(1)}, f32[16,256]{1,0:T(8,128)S(1)}, u32[]{:S(2)}, u32[]{:S(2)}) collective-permute-start(f32[16,256]{1,0:T(8,128)S(1)} %get-tuple-element.40), channel_id=1, source_target_pairs={{508,0},{0,4},{4,8},{8,12},{12,16},{16,20},{20,24},{24,28},{28,32}... | collective-permute-start | bytes 49160 | tf_op jit(solution)/shard_map/ppermute | solution.py:12
  72.5 7.9 %collective-permute-start.3 = (f32[16,256]{1,0:T(8,128)S(1)}, f32[16,256]{1,0:T(8,128)S(1)}, u32[]{:S(2)}, u32[]{:S(2)}) collective-permute-start(f32[16,256]{1,0:T(8,128)S(1)} %get-tuple-element.41), channel_id=1, source_target_pairs={{504,0},{508,4},{0,8},{4,12},{8,16},{12,20},{16,24},{20,28},{24,32... | collective-permute-start | bytes 49160 | tf_op jit(solution)/shard_map/ppermute | solution.py:12
  74.4 7.2 %copy-start.39 = (s32[32]{0:T(128)}, s32[32]{0:T(128)S(1)}, u32[]{:S(2)}) copy-start(s32[32]{0:T(128)S(1)} %fusion.43) | copy-start | bytes 388
  86.2 7.8 %copy-start.2 = (bf16[512,256]{1,0:T(8,128)(2,1)}, bf16[512,256]{1,0:T(8,128)(2,1)S(1)}, u32[]{:S(2)}) copy-start(bf16[512,256]{1,0:T(8,128)(2,1)S(1)} %fusion.4) | copy-start | bytes 786436
  86.8 7.2 %copy-start.36 = (s32[2048]{0:T(1024)S(1)}, s32[2048]{0:T(1024)}, u32[]{:S(2)}) copy-start(s32[2048]{0:T(1024)} %copy-done.35) | copy-start | bytes 24580
  88.7 12.9 %collective-permute-start.4 = (bf16[16,256]{1,0:T(8,128)(2,1)}, bf16[16,256]{1,0:T(8,128)(2,1)}, u32[]{:S(2)}, u32[]{:S(2)}) collective-permute-start(bf16[16,256]{1,0:T(8,128)(2,1)} %get-tuple-element.44), channel_id=1, source_target_pairs={{4,0},{8,4},{12,8},{16,12},{20,16},{24,20},{28,24},{32,28},{36,32}... | collective-permute-start | bytes 24584 | tf_op jit(solution)/shard_map/ppermute | solution.py:12
  91.0 10.6 %collective-permute-start.5 = (bf16[16,256]{1,0:T(8,128)(2,1)S(1)}, bf16[16,256]{1,0:T(8,128)(2,1)}, u32[]{:S(2)}, u32[]{:S(2)}) collective-permute-start(bf16[16,256]{1,0:T(8,128)(2,1)S(1)} %get-tuple-element.45), channel_id=1, source_target_pairs={{8,0},{12,4},{16,8},{20,12},{24,16},{28,20},{32,24},{36,28},{40,32... | collective-permute-start | bytes 24584 | tf_op jit(solution)/shard_map/ppermute | solution.py:12
  94.0 5.4 %copy-start.18 = (bf16[1,512,256]{1,2,0:T(8,128)(2,1)S(1)}, bf16[1,512,256]{1,2,0:T(8,128)(2,1)}, u32[]{:S(2)}) copy-start(bf16[1,512,256]{1,2,0:T(8,128)(2,1)} %get-tuple-element.43) | copy-start | bytes 786436
  146.2 7.6 %copy-start.17 = (f32[256,256]{1,0:T(8,128)S(1)}, f32[256,256]{1,0:T(8,128)}, u32[]{:S(2)}) copy-start(f32[256,256]{1,0:T(8,128)} %fusion.55) | copy-start | bytes 786436
  147.0 117.6 %copy-start.28 = (f32[1536]{0:T(1024)S(1)}, f32[1536]{0:T(1024)}, u32[]{:S(2)}) copy-start(f32[1536]{0:T(1024)} %fusion.40) | copy-start | bytes 18436
  147.1 120.3 %collective-permute-start.6 = (f32[16,256]{0,1:T(8,128)}, f32[16,256]{0,1:T(8,128)}, u32[]{:S(2)}, u32[]{:S(2)}) collective-permute-start(f32[16,256]{0,1:T(8,128)} %get-tuple-element.38), channel_id=1, source_target_pairs={{508,0},{0,4},{4,8},{8,12},{12,16},{16,20},{20,24},{24,28},{28,32}... | collective-permute-start | bytes 49160 | tf_op jit(solution)/shard_map/ppermute | solution.py:12
  151.0 117.3 %collective-permute-start.7 = (f32[16,256]{0,1:T(8,128)}, f32[16,256]{0,1:T(8,128)}, u32[]{:S(2)}, u32[]{:S(2)}) collective-permute-start(f32[16,256]{0,1:T(8,128)} %get-tuple-element.39), channel_id=1, source_target_pairs={{504,0},{508,4},{0,8},{4,12},{8,16},{12,20},{16,24},{20,28},{24,32... | collective-permute-start | bytes 49160 | tf_op jit(solution)/shard_map/ppermute | solution.py:12
  (28 other events, 45.4 us)
where the time goes:
time: 272 us; the launch traced here: 271 us
  blocking collectives  111 us (41%)
  other arithmetic  53 us (19%)
  local copies, waits for them, and re-layouts  44.4 us (16%)
  starting transfers between devices  33.3 us (12%)
  matrix products  21.6 us (8%)
  waiting for transfers between devices  5.94 us (2%)
    psum x1, blocking collectives, local(): lax.psum((grad_ef, grad_es, grad_nf, grad_ns), ('patch', 'rep'))  111 us
    ppermute x8, starting transfers between devices, passed_along(): return lax.ppermute(block, axis, route)  33.3 us
    gather x6, local copies, waits for them, and re-layouts, gather_ends(): return (local_rows[first_end], table[second_end])  24.4 us
    scatter-add x2, other arithmetic, scatter_ends(): jax.ops.segment_sum(first_terms, first_end, verts + seam_total)  20.1 us
    scatter-add x2, other arithmetic, scatter_ends(): jax.ops.segment_sum(second_terms, second_end, verts + seam_total)  19 us
    dot_general x14, matrix products, matmul(): return jnp.dot(left, right, preferred_element_type=jnp.float32)  15.6 us
    unnamed x93, local copies, waits for them, and re-layouts  8.47 us
    dot_general x7, matrix products, outer_sum(): lax.dot_general(left, right, (((0,), (0,)), ((), ())), preferred_element_...  5.97 us
  transfers between devices with their start and end apart: 8, of which 1 were waited for; matrix products, arithmetic and copies ran while one was open for 10% of the time, Pallas kernels for 0%

commit v1 on v0

v1 whole, which is shorter than its diff:
```python
import jax
import jax.numpy as jnp
from jax import lax
from jax.experimental import pallas as pl
from jax.experimental.pallas import tpu as pltpu
from jax.sharding import Mesh, PartitionSpec as P

EPS = 1e-05
BF = jnp.bfloat16
F32 = jnp.float32
BLOCK = 512
PATCH_SPLIT = (4, 8, 2, 2)
PATCH = ("y", "zh", "zl", "c")
INNER = ("y", "zl", "c", "rep")
OUTER = ("zh",)


def dot(left, right):
    return jnp.dot(left, right, preferred_element_type=F32)


def dot_t(left, right):
    return lax.dot_general(left, right, (((1,), (1,)), ((), ())), preferred_element_type=F32)


def t_dot(left, right):
    return lax.dot_general(left, right, (((0,), (0,)), ((), ())), preferred_element_type=F32)


def split(values):
    high = values.astype(BF)
    return high, (values - high.astype(F32)).astype(BF)


def one_hot(index, shape, axis):
    return (index == lax.broadcasted_iota(jnp.int32, shape, axis)).astype(F32)


def normalize(values):
    centred = values - jnp.mean(values, axis=-1, keepdims=True)
    inv_scale = lax.rsqrt(jnp.mean(centred * centred, axis=-1, keepdims=True) + EPS)
    return centred * inv_scale, inv_scale


def norm_back(upstream, normed, inv_scale):
    return inv_scale * (
        upstream
        - jnp.mean(upstream, axis=-1, keepdims=True)
        - normed * jnp.mean(upstream * normed, axis=-1, keepdims=True)
    )


def sigmoid(pre):
    return 1.0 / (1.0 + jnp.exp(-pre))


def slope(pre):
    sigma = sigmoid(pre)
    return sigma * (1.0 + pre * (1.0 - sigma))


def live_row(ends_ref, row, start, count, offset=0):
    index = ends_ref[row : row + 1, pl.ds(start, BLOCK)]
    slot = start + lax.broadcasted_iota(jnp.int32, (1, BLOCK), 1)
    return jnp.where(slot < count, index - offset, -1)


def loop(total, body):
    def step(i, carry):
        body(pl.multiple_of(i * BLOCK, BLOCK))
        return carry

    lax.fori_loop(0, total // BLOCK, step, 0)


def seam_pick(send_ref, hop, table):
    verts = table.shape[0]
    slots = send_ref.shape[1]
    pick = one_hot(send_ref[hop : hop + 1, :], (verts, slots), 0).astype(BF)
    return t_dot(pick, table).astype(BF)


def seam_spread(send_ref, hop, verts, rows):
    slots = send_ref.shape[1]
    pick = one_hot(send_ref[hop : hop + 1, :], (verts, slots), 0)
    return jnp.dot(pick, rows, preferred_element_type=F32, precision=lax.Precision.HIGHEST)


def seam_kernel(send_ref, nodes_ref, out0_ref, out1_ref):
    table = nodes_ref[...]
    out0_ref[...] = seam_pick(send_ref, 0, table)
    out1_ref[...] = seam_pick(send_ref, 1, table)


def edge_local_kernel(
    count_ref, ends_ref, nodes_ref, edges_ref, ef_ref, pre_ref, pairs_ref, far_ref
):
    features = nodes_ref.shape[1]
    verts = nodes_ref.shape[0]
    seam = far_ref.shape[1]
    count = count_ref[0]

    def body(start):
        rows = pl.ds(start, BLOCK)
        first = live_row(ends_ref, 0, start, count)
        second = live_row(ends_ref, 1, start, count)
        both = jnp.concatenate([first, second, second, second, second, second, second, second], axis=0)
        cols = both.T
        first_col = cols[:, 0:1]
        second_col = cols[:, 1:2]
        pick_first = one_hot(first_col, (BLOCK, verts), 1)
        pick_second = one_hot(second_col, (BLOCK, verts), 1)
        far_ref[rows, :] = one_hot(second_col - verts, (BLOCK, seam), 1).astype(BF)
        pairs_ref[rows, :] = (pick_first + pick_second).astype(BF)
        table = nodes_ref[...]
        first_rows = dot(pick_first.astype(BF), table).astype(BF)
        second_rows = dot(pick_second.astype(BF), table).astype(BF)
        pre_ref[rows, :] = (
            dot(edges_ref[rows, :], ef_ref[:features, :])
            + dot(first_rows, ef_ref[features : 2 * features, :])
            + dot(second_rows, ef_ref[2 * features :, :])
        )

    loop(edges_ref.shape[0], body)


def edge_forward_kernel(
    count_ref,
    ends_ref,
    halo0_ref,
    halo1_ref,
    edges_ref,
    part_ref,
    far_ref,
    ef_ref,
    es_ref,
    pre_ref,
    hidden_ref,
    normed_ref,
    inv_ref,
    agg_ref,
    back0_ref,
    back1_ref,
    seam_ref,
):
    features = edges_ref.shape[1]
    verts = agg_ref.shape[0]
    slots = halo0_ref.shape[0]
    count = count_ref[0]
    halo = jnp.concatenate([halo0_ref[...], halo1_ref[...]], axis=0)
    agg_ref[...] = jnp.zeros_like(agg_ref)
    seam_ref[...] = jnp.zeros_like(seam_ref)

    def body(start):
        rows = pl.ds(start, BLOCK)
        far_rows = dot(far_ref[rows, :], halo).astype(BF)
        pre = part_ref[rows, :] + dot(far_rows, ef_ref[2 * features :, :])
        pre_ref[rows, :] = pre
        hidden = (pre * sigmoid(pre)).astype(BF)
        hidden_ref[rows, :] = hidden
        normed, inv = normalize(dot(hidden, es_ref[...]))
        normed_ref[rows, :] = normed
        inv_ref[rows, :] = inv
        new_edge = (edges_ref[rows, :].astype(F32) + normed).astype(BF)
        first = live_row(ends_ref, 0, start, count)
        second = live_row(ends_ref, 1, start, count)
        spread = one_hot(first, (verts, BLOCK), 0) + one_hot(second, (verts, BLOCK), 0)
        agg_ref[...] += dot(spread.astype(BF), new_edge)
        away = one_hot(second - verts, (2 * slots, BLOCK), 0).astype(BF)
        seam_ref[...] += dot(away, new_edge)

    loop(edges_ref.shape[0], body)
    back0_ref[...] = seam_ref[:slots, :]
    back1_ref[...] = seam_ref[slots:, :]


def node_kernel(
    send_ref,
    nodes_ref,
    cot_ref,
    agg_ref,
    got0_ref,
    got1_ref,
    nf_ref,
    ns_ref,
    new_ref,
    agg16_ref,
    hidden_ref,
    dout_ref,
    dpre_ref,
    dagg_ref,
    out0_ref,
    out1_ref,
):
    verts, features = nodes_ref.shape
    total = agg_ref[...] + seam_spread(send_ref, 0, verts, got0_ref[...])
    total = total + seam_spread(send_ref, 1, verts, got1_ref[...])
    aggregate = total.astype(BF)
    agg16_ref[...] = aggregate
    node_rows = nodes_ref[...]
    pre = dot(node_rows, nf_ref[:features, :]) + dot(aggregate, nf_ref[features:, :])
    sigma = sigmoid(pre)
    hidden = (pre * sigma).astype(BF)
    hidden_ref[...] = hidden
    normed, inv = normalize(dot(hidden, ns_ref[...]))
    new_ref[...] = (node_rows.astype(F32) + normed).astype(BF)
    d_out = norm_back(cot_ref[...].astype(F32), normed, inv).astype(BF)
    dout_ref[...] = d_out
    d_pre = (dot_t(d_out, ns_ref[...]) * (sigma * (1.0 + pre * (1.0 - sigma)))).astype(BF)
    dpre_ref[...] = d_pre
    d_agg = dot_t(d_pre, nf_ref[features:, :]).astype(BF)
    dagg_ref[...] = d_agg
    out0_ref[...] = seam_pick(send_ref, 0, d_agg)
    out1_ref[...] = seam_pick(send_ref, 1, d_agg)


def fill_kernel(
    nodes_ref,
    cot_ref,
    agg16_ref,
    hidden_ref,
    dout_ref,
    dpre_ref,
    dagg_ref,
    nf_ref,
    pairs_ref,
    grad_ref,
    part_ref,
    up_ref,
):
    features = nodes_ref.shape[1]
    d_pre = dpre_ref[...]

    def body(start):
        rows = pl.ds(start, BLOCK)
        up_ref[rows, :] = dot(pairs_ref[rows, :], dagg_ref[...])

    loop(pairs_ref.shape[0], body)
    grad_ref[:features, :] = t_dot(nodes_ref[...], d_pre).astype(BF)
    grad_ref[features : 2 * features, :] = t_dot(agg16_ref[...], d_pre).astype(BF)
    grad_ref[2 * features :, :] = t_dot(hidden_ref[...], dout_ref[...]).astype(BF)
    part_ref[...] = cot_ref[...].astype(F32) + dot_t(d_pre, nf_ref[:features, :])


def edge_backward_kernel(
    count_ref,
    ends_ref,
    nodes_ref,
    halo0_ref,
    halo1_ref,
    edges_ref,
    up_ref,
    far_ref,
    dhalo0_ref,
    dhalo1_ref,
    pre_ref,
    hidden_ref,
    normed_ref,
    inv_ref,
    ef_ref,
    es_ref,
    nodegrad_ref,
    part_ref,
    gedges_ref,
    pack_ref,
    partout_ref,
    back0_ref,
    back1_ref,
    first_ref,
    second_ref,
    seam_ref,
    ges_ref,
    ge1_ref,
):
    features = edges_ref.shape[1]
    half = features // 2
    verts = nodes_ref.shape[0]
    slots = halo0_ref.shape[0]
    count = count_ref[0]
    d_halo = jnp.concatenate([dhalo0_ref[...], dhalo1_ref[...]], axis=0)
    for ref in (first_ref, second_ref, seam_ref, ges_ref, ge1_ref):
        ref[...] = jnp.zeros_like(ref)

    def body(start):
        rows = pl.ds(start, BLOCK)
        up = up_ref[rows, :] + dot(far_ref[rows, :], d_halo)
        d_out = norm_back(up, normed_ref[rows, :], inv_ref[rows, :]).astype(BF)
        ges_ref[...] += t_dot(hidden_ref[rows, :], d_out)
        d_pre = (dot_t(d_out, es_ref[...]) * slope(pre_ref[rows, :])).astype(BF)
        first = live_row(ends_ref, 0, start, count)
        second = live_row(ends_ref, 1, start, count)
        seam_ref[...] += dot(one_hot(second - verts, (2 * slots, BLOCK), 0).astype(BF), d_pre)
        first_ref[...] += dot(one_hot(first, (verts, BLOCK), 0).astype(BF), d_pre)
        second_ref[...] += dot(one_hot(second, (verts, BLOCK), 0).astype(BF), d_pre)
        ge1_ref[...] += t_dot(edges_ref[rows, :], d_pre)
        gedges_ref[rows, :] = (up + dot_t(d_pre, ef_ref[:features, :])).astype(BF)

    loop(edges_ref.shape[0], body)
    back0_ref[...] = seam_ref[:slots, :]
    back1_ref[...] = seam_ref[slots:, :]
    total = pack_ref.shape[0] // 2

    def put(begin, grad):
        grad = grad.astype(BF)
        size = grad.shape[0]
        pack_ref[begin : begin + size, :] = grad[:, :half]
        pack_ref[total + begin : total + begin + size, :] = grad[:, half:]

    node_rows = nodes_ref[...]
    first_high, first_low = split(first_ref[...])
    second_high, second_low = split(second_ref[...])
    far_high, far_low = split(seam_ref[...])
    halo = jnp.concatenate([halo0_ref[...], halo1_ref[...]], axis=0)
    put(0, ge1_ref[...])
    put(features, t_dot(node_rows, first_high) + t_dot(node_rows, first_low))
    put(
        2 * features,
        t_dot(node_rows, second_high)
        + t_dot(node_rows, second_low)
        + t_dot(halo, far_high)
        + t_dot(halo, far_low),
    )
    put(3 * features, ges_ref[...])
    put(4 * features, nodegrad_ref[...])
    middle = ef_ref[features : 2 * features, :]
    last = ef_ref[2 * features :, :]
    partout_ref[...] = (
        part_ref[...]
        + (dot_t(first_high, middle) + dot_t(first_low, middle))
        + (dot_t(second_high, last) + dot_t(second_low, last))
    )


def finish_kernel(send_ref, part_ref, got0_ref, got1_ref, ef_ref, out_ref):
    verts, features = part_ref.shape
    last = ef_ref[2 * features :, :]
    total = part_ref[...]
    for hop, ref in enumerate((got0_ref, got1_ref)):
        high, low = split(ref[...])
        total = total + seam_spread(send_ref, hop, verts, dot_t(high, last) + dot_t(low, last))
    out_ref[...] = total.astype(BF)


def unpack_kernel(pack_ref, gef_ref, ges_ref, gnf_ref, gns_ref):
    total = pack_ref.shape[0] // 2
    half = pack_ref.shape[1]
    begin = 0
    for ref in (gef_ref, ges_ref, gnf_ref, gns_ref):
        size = ref.shape[0]
        ref[:, :half] = pack_ref[begin : begin + size, :]
        ref[:, half:] = pack_ref[total + begin : total + begin + size, :]
        begin += size


def call(kernel, outs, args, scalars=0, scratch=(), flops=0, name=None):
    return pl.pallas_call(
        kernel,
        out_shape=[jax.ShapeDtypeStruct(shape, kind) for shape, kind in outs],
        in_specs=[
            pl.BlockSpec(memory_space=pltpu.SMEM if i < scalars else pltpu.VMEM)
            for i in range(len(args))
        ],
        out_specs=[pl.BlockSpec(memory_space=pltpu.VMEM) for _ in outs],
        scratch_shapes=[pltpu.VMEM(shape, F32) for shape in scratch],
        cost_estimate=pl.CostEstimate(flops=flops, transcendentals=0, bytes_accessed=flops // 1000),
        name=name,
    )(*args)


def shift(block, distance):
    count = lax.axis_size(PATCH)
    return lax.ppermute(block, PATCH, [((i - distance) % count, i) for i in range(count)])


def group_size(axes):
    return lax.axis_size(axes)


def sum_everywhere(pack):
    inner = group_size(INNER)
    outer = group_size(OUTER)
    rows, lanes = pack.shape
    pieces = lax.all_to_all(pack.reshape(inner, rows // inner, lanes), INNER, 0, 0)
    mine = jnp.sum(pieces.astype(F32), axis=0).astype(BF)
    spread = jnp.broadcast_to(mine[None], (outer,) + mine.shape)
    pieces = lax.all_to_all(spread, OUTER, 0, 0)
    mine = jnp.sum(pieces.astype(F32), axis=0).astype(BF)
    spread = jnp.broadcast_to(mine[None], (inner,) + mine.shape)
    return lax.all_to_all(spread, INNER, 0, 0).reshape(rows, lanes)


def local(
    nodes,
    edges,
    edge_ends,
    edge_count,
    send_rows,
    cotangent,
    edge_first,
    edge_second,
    node_first,
    node_second,
):
    node_rows = nodes[0]
    edge_rows = edges[0]
    cot = cotangent[0]
    verts, features = node_rows.shape
    slots = edge_rows.shape[0]
    hops, seam = send_rows.shape
    assert hops == 2
    ends = edge_ends.T
    seam16 = ((seam, features), BF)
    seam32 = ((seam, features), F32)
    unit = 2 * features * features

    out0, out1 = call(seam_kernel, [seam16, seam16], (send_rows, node_rows), flops=10**8, name="seam")
    halo0 = shift(out0, -1)
    halo1 = shift(out1, -2)
    part, pairs, far = call(
        edge_local_kernel,
        [((slots, features), F32), ((slots, verts), BF), ((slots, hops * seam), BF)],
        (edge_count, ends, node_rows, edge_rows, edge_first),
        scalars=1,
        flops=7 * slots * unit,
        name="edge_local",
    )
    pre, hidden, normed, inv, agg, back0, back1 = call(
        edge_forward_kernel,
        [
            ((slots, features), F32),
            ((slots, features), BF),
            ((slots, features), F32),
            ((slots, 1), F32),
            ((verts, features), F32),
            seam32,
            seam32,
        ],
        (edge_count, ends, halo0, halo1, edge_rows, part, far, edge_first, edge_second),
        scalars=1,
        scratch=[(hops * seam, features)],
        flops=4 * slots * unit,
        name="edge_forward",
    )
    got0 = shift(back0, 1)
    got1 = shift(back1, 2)
    tall = (verts, features)
    new_nodes, agg16, node_hidden, d_out, d_pre, d_agg, out0, out1 = call(
        node_kernel,
        [(tall, BF)] * 6 + [seam16, seam16],
        (send_rows, node_rows, cot, agg, got0, got1, node_first, node_second),
        flops=8 * verts * unit,
        name="node",
    )
    d_halo0 = shift(out0, -1)
    d_halo1 = shift(out1, -2)
    node_grads, grad_part, up = call(
        fill_kernel,
        [((3 * features, features), BF), (tall, F32), ((slots, features), F32)],
        (node_rows, cot, agg16, node_hidden, d_out, d_pre, d_agg, node_first, pairs),
        flops=4 * slots * unit,
        name="fill",
    )
    grad_edges, pack, grad_part, back0, back1 = call(
        edge_backward_kernel,
        [
            ((slots, features), BF),
            ((2 * 7 * features, features // 2), BF),
            (tall, F32),
            seam32,
            seam32,
        ],
        (
            edge_count,
            ends,
            node_rows,
            halo0,
            halo1,
            edge_rows,
            up,
            far,
            d_halo0,
            d_halo1,
            pre,
            hidden,
            normed,
            inv,
            edge_first,
            edge_second,
            node_grads,
            grad_part,
        ),
        scalars=1,
        scratch=[tall, tall, (hops * seam, features), (features, features), (features, features)],
        flops=12 * slots * unit,
        name="edge_backward",
    )
    got0 = shift(back0, 1)
    got1 = shift(back1, 2)
    pack = sum_everywhere(pack)
    (grad_nodes,) = call(
        finish_kernel,
        [(tall, BF)],
        (send_rows, grad_part, got0, got1, edge_first),
        flops=verts * unit,
        name="finish",
    )
    grad_ef, grad_es, grad_nf, grad_ns = call(
        unpack_kernel,
        [
            ((3 * features, features), BF),
            ((features, features), BF),
            ((2 * features, features), BF),
            ((features, features), BF),
        ],
        (pack,),
        flops=1000,
        name="unpack",
    )
    return (
        new_nodes[None],
        grad_nodes[None],
        grad_edges[None],
        grad_ef,
        grad_es,
        grad_nf,
        grad_ns,
    )


def solution(mesh):
    fine = Mesh(mesh.devices.reshape(PATCH_SPLIT + (mesh.shape["rep"],)), PATCH + ("rep",))
    placed = (
        P("rep", PATCH, None),
        P("rep", PATCH, None),
        P(PATCH, None),
        P(PATCH),
        P(PATCH, None),
        P("rep", PATCH, None),
        P(),
        P(),
        P(),
        P(),
    )
    return jax.shard_map(
        local,
        mesh=fine,
        in_specs=placed,
        out_specs=(
            P("rep", PATCH, None),
            P("rep", PATCH, None),
            P("rep", PATCH, None),
            P(),
            P(),
            P(),
            P(),
        ),
        check_vma=False,
    )
```

time: 272 us -> 137 us (0.50)
  blocking collectives: 111 us -> 39 us
  other arithmetic: 53 us -> 0.18 us
  Pallas kernels: 0 us -> 40 us
  local copies, waits for them, and re-layouts: 44.4 us -> 4.43 us
  matrix products: 21.6 us -> 0 us
  waiting for transfers between devices: 5.94 us -> 12.4 us
  starting transfers between devices: 33.3 us -> 39.3 us
    psum x1 -> x0, blocking collectives: 111 us -> none  [local(): lax.psum((grad_ef, grad_es, grad_nf, grad_ns), ('patch', 'rep'))]
    scatter-add x6 -> x0, other arithmetic: 41.2 us -> none  [the longest x2 20.1 us: scatter_ends(): jax.ops.segment_sum(first_terms, first_end, verts + seam_total)]
    pallas_call x0 -> x8, Pallas kernels: none -> 40 us  [call(): pl.pallas_call(kernel, out_shape=[jax.ShapeDtypeStruct(shape, kind) for s...]
    all_to_all x0 -> x2, blocking collectives: none -> 39 us  [the longest x1 22.4 us: sum_everywhere(): lax.all_to_all(pack.reshape(inner, rows // inner, lanes), INNER, 0, 0)]
    gather x8 -> x0, local copies, waits for them, and re-layouts: 26.7 us -> none  [the longest x6 24.4 us: gather_ends(): return (local_rows[first_end], table[second_end])]
    dot_general x21 -> x0, matrix products: 21.6 us -> none  [the longest x14 15.6 us: matmul(): return jnp.dot(left, right, preferred_element_type=jnp.float32)]
    all_to_all x0 -> x1, starting transfers between devices: none -> 7.34 us  [sum_everywhere(): return lax.all_to_all(spread, INNER, 0, 0).reshape(rows, lanes)]
    ppermute x8, waiting for transfers between devices: 5.94 us -> 12.4 us  [shift(): lax.ppermute(block, PATCH, [((i - distance) % count, i) for i in range(co...]
  transfers between devices with their start and end apart: 8 -> 9, of which waited for: 1 -> 3; matrix products, arithmetic and copies ran while one was open for 10% -> 0% of each run, Pallas kernels for 0% -> 11%
where the time goes in v1:
time: 137 us
  Pallas kernels  40 us (29%)
  starting transfers between devices  39.3 us (29%)
  blocking collectives  39 us (28%)
  waiting for transfers between devices  12.4 us (9%)
  local copies, waits for them, and re-layouts  4.43 us (3%)
  between operations  1.46 us (1%)
    pallas_call x8, Pallas kernels, call(): pl.pallas_call(kernel, out_shape=[jax.ShapeDtypeStruct(shape, kind) for s...  40 us
    ppermute x8, starting transfers between devices, shift(): lax.ppermute(block, PATCH, [((i - distance) % count, i) for i in range(co...  32 us
    all_to_all x1, blocking collectives, sum_everywhere(): lax.all_to_all(pack.reshape(inner, rows // inner, lanes), INNER, 0, 0)  22.4 us
    all_to_all x1, blocking collectives, sum_everywhere(): pieces = lax.all_to_all(spread, OUTER, 0, 0)  16.6 us
    ppermute x8, waiting for transfers between devices, shift(): lax.ppermute(block, PATCH, [((i - distance) % count, i) for i in range(co...  12.4 us
    all_to_all x1, starting transfers between devices, sum_everywhere(): return lax.all_to_all(spread, INNER, 0, 0).reshape(rows, lanes)  7.34 us
    unnamed x22, local copies, waits for them, and re-layouts  3.35 us
  transfers between devices with their start and end apart: 9, of which 3 were waited for; matrix products, arithmetic and copies ran while one was open for 0% of the time, Pallas kernels for 11%

profile of v1, /device:TPU:1, one launch (start us, length us, event | category | flops | bytes accessed | tf_op | source)
XLA Modules:
  0.0 136.7 jit_solution(8092221146516125358)
XLA Ops:
  0.6 1.8 %seam.1 = (bf16[16,256]{1,0:T(8,128)(2,1)}, bf16[16,256]{1,0:T(8,128)(2,1)}) custom-call(s32[2,16]{1,0:T(2,128)} %send_ref.5, bf16[512,256]{1,0:T(8,128)(2,1)} %bitcast.13), custom_call_target="tpu_custom_call" | custom-call | flops 100000000 | bytes 100000 | tf_op jit(solution)/shard_map/seam/pallas_call | solution.py:356
  2.4 8.7 %collective-permute-start = (bf16[16,256]{1,0:T(8,128)(2,1)}, bf16[16,256]{1,0:T(8,128)(2,1)S(1)}, u32[]{:S(2)}, u32[]{:S(2)}) collective-permute-start(bf16[16,256]{1,0:T(8,128)(2,1)} %get-tuple-element.39), channel_id=1, source_target_pairs={{4,0},{8,4},{12,8},{16,12},{20,16},{24,20},{28,24},{32,28},{36,32}... | collective-permute-start | bytes 24584 | tf_op jit(solution)/shard_map/ppermute | solution.py:372
  11.2 8.2 %collective-permute-start.1 = (bf16[16,256]{1,0:T(8,128)(2,1)}, bf16[16,256]{1,0:T(8,128)(2,1)S(1)}, u32[]{:S(2)}, u32[]{:S(2)}) collective-permute-start(bf16[16,256]{1,0:T(8,128)(2,1)} %get-tuple-element.40), channel_id=1, source_target_pairs={{8,0},{12,4},{16,8},{20,12},{24,16},{28,20},{32,24},{36,28},{40,32... | collective-permute-start | bytes 24584 | tf_op jit(solution)/shard_map/ppermute | solution.py:372
  20.1 6.2 %edge_local.1 = (f32[1536,256]{1,0:T(8,128)}, bf16[1536,512]{1,0:T(8,128)(2,1)}, bf16[1536,32]{1,0:T(8,128)(2,1)}) custom-call(s32[1]{0:T(128)S(6)} %copy.17.count_ref, s32[2,1536]{1,0:T(2,128)} %bitcast.22, bf16[512,256]{1,0:T(8,128)(2,1)} %bitcast.14, bf16[1536,256]{1,0:T(8,128)(2,1)} %bitcast.10, bf16[768,256]{1,0:T(8,128)(2,1)} %ef_ref.7), custom_call_target="tpu_custom_call" | custom-call | flops 1409286144 | bytes 1409286 | tf_op jit(solution)/shard_map/edge_local/pallas_call | solution.py:356
  26.9 6.9 %edge_forward.1 = (f32[1536,256]{1,0:T(8,128)}, bf16[1536,256]{1,0:T(8,128)(2,1)}, f32[1536,256]{1,0:T(8,128)}, f32[1536,1]{1,0:T(8,128)}, f32[512,256]{1,0:T(8,...) custom-call(s32[1]{0:T(128)S(6)} %copy.17.count_ref, s32[2,1536]{1,0:T(2,128)} %bitcast.23, bf16[16,256]{1,0:T(8,128)(2,1)} %copy-done.1, ...), custom_call_target="tpu_custom_call" | custom-call | flops 805306368 | bytes 805306 | tf_op jit(solution)/shard_map/edge_forward/pallas_call | solution.py:356
  33.7 3.2 %collective-permute-start.2 = (f32[16,256]{1,0:T(8,128)}, f32[16,256]{1,0:T(8,128)S(1)}, u32[]{:S(2)}, u32[]{:S(2)}) collective-permute-start(f32[16,256]{1,0:T(8,128)} %get-tuple-element.44), channel_id=1, source_target_pairs={{508,0},{0,4},{4,8},{8,12},{12,16},{16,20},{20,24},{24,28},{28,32}... | collective-permute-start | bytes 49160 | tf_op jit(solution)/shard_map/ppermute | solution.py:372
  37.0 1.9 %collective-permute-start.3 = (f32[16,256]{1,0:T(8,128)}, f32[16,256]{1,0:T(8,128)S(1)}, u32[]{:S(2)}, u32[]{:S(2)}) collective-permute-start(f32[16,256]{1,0:T(8,128)} %get-tuple-element.45), channel_id=1, source_target_pairs={{504,0},{508,4},{0,8},{4,12},{8,16},{12,20},{16,24},{20,28},{24,32... | collective-permute-start | bytes 49160 | tf_op jit(solution)/shard_map/ppermute | solution.py:372
  39.0 6.2 %collective-permute-done.3.got1_ref = f32[16,256]{1,0:T(8,128)S(1)} collective-permute-done((f32[16,256]{1,0:T(8,128)}, f32[16,256]{1,0:T(8,128)S(1)}, u32[]{:S(2)}, u32[]{:S(2)}) %collective-permute-start.3) | collective-permute-done | bytes 16416 | tf_op jit(solution)/shard_map/ppermute | solution.py:372
  45.8 4.4 %node.1 = (bf16[512,256]{1,0:T(8,128)(2,1)}, bf16[512,256]{1,0:T(8,128)(2,1)}, bf16[512,256]{1,0:T(8,128)(2,1)}, bf16[512,256]{1,0:T(8,128)(2,1)}, bf16[512,256]...) custom-call(s32[2,16]{1,0:T(2,128)} %send_ref.5, ...), custom_call_target="tpu_custom_call" | custom-call | flops 536870912 | bytes 536870 | tf_op jit(solution)/shard_map/node/pallas_call | solution.py:356
  50.2 2.3 %collective-permute-start.4 = (bf16[16,256]{1,0:T(8,128)(2,1)}, bf16[16,256]{1,0:T(8,128)(2,1)S(1)}, u32[]{:S(2)}, u32[]{:S(2)}) collective-permute-start(bf16[16,256]{1,0:T(8,128)(2,1)} %get-tuple-element.54), channel_id=1, source_target_pairs={{4,0},{8,4},{12,8},{16,12},{20,16},{24,20},{28,24},{32,28},{36,32}... | collective-permute-start | bytes 24584 | tf_op jit(solution)/shard_map/ppermute | solution.py:372
  52.5 2.1 %collective-permute-start.5 = (bf16[16,256]{1,0:T(8,128)(2,1)}, bf16[16,256]{1,0:T(8,128)(2,1)S(1)}, u32[]{:S(2)}, u32[]{:S(2)}) collective-permute-start(bf16[16,256]{1,0:T(8,128)(2,1)} %get-tuple-element.55), channel_id=1, source_target_pairs={{8,0},{12,4},{16,8},{20,12},{24,16},{28,20},{32,24},{36,28},{40,32... | collective-permute-start | bytes 24584 | tf_op jit(solution)/shard_map/ppermute | solution.py:372
  54.6 5.0 %fill.1 = (bf16[768,256]{1,0:T(8,128)(2,1)}, f32[512,256]{1,0:T(8,128)}, f32[1536,256]{1,0:T(8,128)}) custom-call(bf16[512,256]{1,0:T(8,128)(2,1)} %bitcast.16, bf16[512,256]{1,0:T(8,128)(2,1)} %bitcast.20, bf16[512,256]{1,0:T(8,128)(2,1)} %get-tuple-element.47.agg16_ref, bf16[512,256]{1,0:T(8,128)(2,1)} %get-tuple-element.48.hidden_ref, ...), custom_call_target="tpu_custom_call" | custom-call | flops 805306368 | bytes 805306 | tf_op jit(solution)/shard_map/fill/pallas_call | solution.py:356
  60.2 9.5 %edge_backward.1 = (bf16[1536,256]{1,0:T(8,128)(2,1)}, bf16[3584,128]{1,0:T(8,128)(2,1)}, f32[512,256]{1,0:T(8,128)}, f32[16,256]{1,0:T(8,128)}, f32[16,256]{1,0:T(8,128)}) custom-call(s32[1]{0:T(128)S(6)} %copy.17.count_ref, s32[2,1536]{1,0:T(2,128)} %bitcast.24, bf16[512,256]{1,0:T(8,128)(2,1)} %bitcast.17, bf16[16,256]{1,0:T(8,128)(2,1)} %copy-done.1, ...), custom_call_target="tpu_custom_call" | custom-call | flops 2415919104 | bytes 2415919 | tf_op jit(solution)/shard_map/edge_backward/pallas_call | solution.py:356
  69.7 22.4 %all_to_all.15 = bf16[64,56,128]{2,1,0:T(8,128)(2,1)S(1)} all-to-all(bf16[64,56,128]{2,1,0:T(8,128)(2,1)} %bitcast.18), channel_id=1, replica_groups=mesh['y'=4,'zh'=8,'zl'=2,'c'=2,'rep'=4] {'y','zl','c','rep'}, dimensions={0} | all-to-all | bytes 1835008 | tf_op jit(solution)/shard_map/all_to_all | solution.py:383
  92.2 16.6 %all_to_all.16 = bf16[8,56,128]{2,1,0:T(8,128)(2,1)S(1)} all-to-all(bf16[8,56,128]{2,1,0:T(8,128)(2,1)S(1)} %broadcast_in_dim.24), channel_id=1, replica_groups=mesh['y'=4,'zh'=8,'zl'=2,'c'=2,'rep'=4] {'zh'}, dimensions={0} | all-to-all | bytes 229376 | tf_op jit(solution)/shard_map/all_to_all | solution.py:386
  108.9 1.1 broadcast_in_dim.25
  110.0 7.3 %all-to-all-start.2 = ((bf16[64,56,128]{2,1,0:T(8,128)(2,1)}), bf16[64,56,128]{2,1,0:T(8,128)(2,1)S(1)}, u32[]{:S(2)}, u32[]{:S(2)}) async-start(bf16[64,56,128]{2,1,0:T(8,128)(2,1)} %broadcast_in_dim.25), calls=%async_computation.2 | async-start | bytes 1835008 | tf_op jit(solution)/shard_map/all_to_all | solution.py:389
  117.3 3.5 %collective-permute-start.6 = (f32[16,256]{1,0:T(8,128)S(1)}, f32[16,256]{1,0:T(8,128)S(1)}, u32[]{:S(2)}, u32[]{:S(2)}) collective-permute-start(f32[16,256]{1,0:T(8,128)S(1)} %copy-done.8), channel_id=1, source_target_pairs={{508,0},{0,4},{4,8},{8,12},{12,16},{16,20},{20,24},{24,28},{28,32}... | collective-permute-start | bytes 49160 | tf_op jit(solution)/shard_map/ppermute | solution.py:372
  120.9 1.9 %collective-permute-start.7 = (f32[16,256]{1,0:T(8,128)S(1)}, f32[16,256]{1,0:T(8,128)S(1)}, u32[]{:S(2)}, u32[]{:S(2)}) collective-permute-start(f32[16,256]{1,0:T(8,128)S(1)} %copy-done.7), channel_id=1, source_target_pairs={{504,0},{508,4},{0,8},{4,12},{8,16},{12,20},{16,24},{20,28},{24,32... | collective-permute-start | bytes 49160 | tf_op jit(solution)/shard_map/ppermute | solution.py:372
  122.8 4.5 %collective-permute-done.6.got0_ref = f32[16,256]{1,0:T(8,128)S(1)} collective-permute-done((f32[16,256]{1,0:T(8,128)S(1)}, f32[16,256]{1,0:T(8,128)S(1)}, u32[]{:S(2)}, u32[]{:S(2)}) %collective-permute-start.6) | collective-permute-done | bytes 16416 | tf_op jit(solution)/shard_map/ppermute | solution.py:372
  127.3 1.6 %collective-permute-done.7.got1_ref = f32[16,256]{1,0:T(8,128)S(1)} collective-permute-done((f32[16,256]{1,0:T(8,128)S(1)}, f32[16,256]{1,0:T(8,128)S(1)}, u32[]{:S(2)}, u32[]{:S(2)}) %collective-permute-start.7) | collective-permute-done | bytes 16416 | tf_op jit(solution)/shard_map/ppermute | solution.py:372
  129.6 4.0 %finish.1 = bf16[512,256]{1,0:T(8,128)(2,1)} custom-call(s32[2,16]{1,0:T(2,128)} %send_ref.5, f32[512,256]{1,0:T(8,128)} %get-tuple-element.62.part_ref, f32[16,256]{1,0:T(8,128)} %copy-done.3, f32[16,256]{1,0:T(8,128)} %copy-done.4, bf16[768,256]{1,0:T(8,128)(2,1)} %ef_ref.7), custom_call_target="tpu_custom_call" | custom-call | flops 67108864 | bytes 67108 | tf_op jit(solution)/shard_map/finish/pallas_call | solution.py:356
  133.5 0.9 copy-done
  134.5 2.2 %unpack.1 = (bf16[768,256]{1,0:T(8,128)(2,1)}, bf16[256,256]{1,0:T(8,128)(2,1)}, bf16[512,256]{1,0:T(8,128)(2,1)}, bf16[256,256]{1,0:T(8,128)(2,1)}) custom-call(bf16[3584,128]{1,0:T(8,128)(2,1)} %bitcast.9), custom_call_target="tpu_custom_call" | custom-call | flops 1000 | bytes 1 | tf_op jit(solution)/shard_map/unpack/pallas_call | solution.py:356
  (30 shorter events, 2.6 us)
Async XLA Ops:
  2.4 23.8 %collective-permute-start = (bf16[16,256]{1,0:T(8,128)(2,1)}, bf16[16,256]{1,0:T(8,128)(2,1)S(1)}, u32[]{:S(2)}, u32[]{:S(2)}) collective-permute-start(bf16[16,256]{1,0:T(8,128)(2,1)} %get-tuple-element.39), channel_id=1, source_target_pairs={{4,0},{8,4},{12,8},{16,12},{20,16},{24,20},{28,24},{32,28},{36,32}... | collective-permute-start | bytes 24584 | tf_op jit(solution)/shard_map/ppermute | solution.py:372
  11.2 15.1 %collective-permute-start.1 = (bf16[16,256]{1,0:T(8,128)(2,1)}, bf16[16,256]{1,0:T(8,128)(2,1)S(1)}, u32[]{:S(2)}, u32[]{:S(2)}) collective-permute-start(bf16[16,256]{1,0:T(8,128)(2,1)} %get-tuple-element.40), channel_id=1, source_target_pairs={{8,0},{12,4},{16,8},{20,12},{24,16},{28,20},{32,24},{36,28},{40,32... | collective-permute-start | bytes 24584 | tf_op jit(solution)/shard_map/ppermute | solution.py:372
  26.3 0.6 copy-start.1
  26.3 0.6 copy-start.2
  33.7 5.2 %collective-permute-start.2 = (f32[16,256]{1,0:T(8,128)}, f32[16,256]{1,0:T(8,128)S(1)}, u32[]{:S(2)}, u32[]{:S(2)}) collective-permute-start(f32[16,256]{1,0:T(8,128)} %get-tuple-element.44), channel_id=1, source_target_pairs={{508,0},{0,4},{4,8},{8,12},{12,16},{16,20},{20,24},{24,28},{28,32}... | collective-permute-start | bytes 49160 | tf_op jit(solution)/shard_map/ppermute | solution.py:372
  37.0 8.2 %collective-permute-start.3 = (f32[16,256]{1,0:T(8,128)}, f32[16,256]{1,0:T(8,128)S(1)}, u32[]{:S(2)}, u32[]{:S(2)}) collective-permute-start(f32[16,256]{1,0:T(8,128)} %get-tuple-element.45), channel_id=1, source_target_pairs={{504,0},{508,4},{0,8},{4,12},{8,16},{12,20},{16,24},{20,28},{24,32... | collective-permute-start | bytes 49160 | tf_op jit(solution)/shard_map/ppermute | solution.py:372
  38.9 6.2 %copy-start.9 = (f32[16,256]{1,0:T(8,128)}, f32[16,256]{1,0:T(8,128)S(1)}, u32[]{:S(2)}) copy-start(f32[16,256]{1,0:T(8,128)S(1)} %collective-permute-done.2.got0_ref) | copy-start | bytes 49156
  45.2 0.6 copy-start.10
  50.2 9.4 %collective-permute-start.4 = (bf16[16,256]{1,0:T(8,128)(2,1)}, bf16[16,256]{1,0:T(8,128)(2,1)S(1)}, u32[]{:S(2)}, u32[]{:S(2)}) collective-permute-start(bf16[16,256]{1,0:T(8,128)(2,1)} %get-tuple-element.54), channel_id=1, source_target_pairs={{4,0},{8,4},{12,8},{16,12},{20,16},{24,20},{28,24},{32,28},{36,32}... | collective-permute-start | bytes 24584 | tf_op jit(solution)/shard_map/ppermute | solution.py:372
  52.5 7.1 %collective-permute-start.5 = (bf16[16,256]{1,0:T(8,128)(2,1)}, bf16[16,256]{1,0:T(8,128)(2,1)S(1)}, u32[]{:S(2)}, u32[]{:S(2)}) collective-permute-start(bf16[16,256]{1,0:T(8,128)(2,1)} %get-tuple-element.55), channel_id=1, source_target_pairs={{8,0},{12,4},{16,8},{20,12},{24,16},{28,20},{32,24},{36,28},{40,32... | collective-permute-start | bytes 24584 | tf_op jit(solution)/shard_map/ppermute | solution.py:372
  59.6 0.6 copy-start.5
  59.6 0.6 copy-start.6
  92.2 25.1 %copy-start.8 = (f32[16,256]{1,0:T(8,128)S(1)}, f32[16,256]{1,0:T(8,128)}, u32[]{:S(2)}) copy-start(f32[16,256]{1,0:T(8,128)} %get-tuple-element.63) | copy-start | bytes 49156
  92.2 28.6 %copy-start.7 = (f32[16,256]{1,0:T(8,128)S(1)}, f32[16,256]{1,0:T(8,128)}, u32[]{:S(2)}) copy-start(f32[16,256]{1,0:T(8,128)} %get-tuple-element.64) | copy-start | bytes 49156
  110.0 23.6 %all-to-all-start.2 = ((bf16[64,56,128]{2,1,0:T(8,128)(2,1)}), bf16[64,56,128]{2,1,0:T(8,128)(2,1)S(1)}, u32[]{:S(2)}, u32[]{:S(2)}) async-start(bf16[64,56,128]{2,1,0:T(8,128)(2,1)} %broadcast_in_dim.25), calls=%async_computation.2 | async-start | bytes 1835008 | tf_op jit(solution)/shard_map/all_to_all | solution.py:389
  117.3 10.0 %collective-permute-start.6 = (f32[16,256]{1,0:T(8,128)S(1)}, f32[16,256]{1,0:T(8,128)S(1)}, u32[]{:S(2)}, u32[]{:S(2)}) collective-permute-start(f32[16,256]{1,0:T(8,128)S(1)} %copy-done.8), channel_id=1, source_target_pairs={{508,0},{0,4},{4,8},{8,12},{12,16},{16,20},{20,24},{24,28},{28,32}... | collective-permute-start | bytes 49160 | tf_op jit(solution)/shard_map/ppermute | solution.py:372
  120.9 8.1 %collective-permute-start.7 = (f32[16,256]{1,0:T(8,128)S(1)}, f32[16,256]{1,0:T(8,128)S(1)}, u32[]{:S(2)}, u32[]{:S(2)}) collective-permute-start(f32[16,256]{1,0:T(8,128)S(1)} %copy-done.7), channel_id=1, source_target_pairs={{504,0},{508,4},{0,8},{4,12},{8,16},{12,20},{16,24},{20,28},{24,32... | collective-permute-start | bytes 49160 | tf_op jit(solution)/shard_map/ppermute | solution.py:372
  127.3 1.7 %copy-start.3 = (f32[16,256]{1,0:T(8,128)}, f32[16,256]{1,0:T(8,128)S(1)}, u32[]{:S(2)}) copy-start(f32[16,256]{1,0:T(8,128)S(1)} %collective-permute-done.6.got0_ref) | copy-start | bytes 49156
  129.0 0.6 copy-start.4
  133.5 0.9 copy-start

commit v2 on v1

--- a/solution.py
+++ b/solution.py
@@ -362,6 +362,7 @@
         ],
         out_specs=[pl.BlockSpec(memory_space=pltpu.VMEM) for _ in outs],
         scratch_shapes=[pltpu.VMEM(shape, F32) for shape in scratch],
+        compiler_params=pltpu.CompilerParams(vmem_limit_bytes=24 * 2**20),
         cost_estimate=pl.CostEstimate(flops=flops, transcendentals=0, bytes_accessed=flops // 1000),
         name=name,
     )(*args)

time: 137 us -> 123 us (0.90)
  Pallas kernels: 40 us -> 19.7 us
  local copies, waits for them, and re-layouts: 4.43 us -> 6.53 us
  waiting for transfers between devices: 12.4 us -> 14.3 us
  blocking collectives: 39 us -> 40.8 us
    pallas_call x8, Pallas kernels: 40 us -> 19.7 us  [call(): pl.pallas_call(kernel, out_shape=[jax.ShapeDtypeStruct(shape, kind) for s...]
    unnamed x22 -> x30, local copies, waits for them, and re-layouts: 3.35 us -> 5.45 us
    all_to_all x1, blocking collectives: 16.6 us -> 18.2 us  [sum_everywhere(): pieces = lax.all_to_all(spread, OUTER, 0, 0)]
  transfers between devices with their start and end apart: 9 -> 9, of which waited for: 3 -> 5; matrix products, arithmetic and copies ran while one was open for 0% -> 0% of each run, Pallas kernels for 11% -> 6%
where the time goes in v2:
time: 123 us; the launch traced here: 122 us
  blocking collectives  40.8 us (33%)
  starting transfers between devices  39.3 us (32%)
  Pallas kernels  19.7 us (16%)
  waiting for transfers between devices  14.3 us (12%)
  local copies, waits for them, and re-layouts  6.53 us (5%)
  between operations  1.53 us (1%)
    ppermute x8, starting transfers between devices, shift(): lax.ppermute(block, PATCH, [((i - distance) % count, i) for i in range(co...  32 us
    all_to_all x1, blocking collectives, sum_everywhere(): lax.all_to_all(pack.reshape(inner, rows // inner, lanes), INNER, 0, 0)  22.6 us
    pallas_call x8, Pallas kernels, call(): pl.pallas_call(kernel, out_shape=[jax.ShapeDtypeStruct(shape, kind) for s...  19.7 us
    all_to_all x1, blocking collectives, sum_everywhere(): pieces = lax.all_to_all(spread, OUTER, 0, 0)  18.2 us
    ppermute x8, waiting for transfers between devices, shift(): lax.ppermute(block, PATCH, [((i - distance) % count, i) for i in range(co...  13.1 us
    all_to_all x1, starting transfers between devices, sum_everywhere(): return lax.all_to_all(spread, INNER, 0, 0).reshape(rows, lanes)  7.34 us
    unnamed x30, local copies, waits for them, and re-layouts  5.45 us
  transfers between devices with their start and end apart: 9, of which 5 were waited for; matrix products, arithmetic and copies ran while one was open for 0% of the time, Pallas kernels for 6%

profile of v2, /device:TPU:1, one launch (start us, length us, event | category | flops | bytes accessed | tf_op | source)
XLA Modules:
  0.0 122.4 jit_solution(1077135976287302025)
XLA Ops:
  2.5 8.7 %collective-permute-start = (bf16[16,256]{1,0:T(8,128)(2,1)S(1)}, bf16[16,256]{1,0:T(8,128)(2,1)S(1)}, u32[]{:S(2)}, u32[]{:S(2)}) collective-permute-start(bf16[16,256]{1,0:T(8,128)(2,1)S(1)} %get-tuple-element.39), channel_id=1, source_target_pairs={{4,0},{8,4},{12,8},{16,12},{20,16},{24,20},{28,24},{32,28},{36,32}... | collective-permute-start | bytes 24584 | tf_op jit(solution)/shard_map/ppermute | solution.py:373
  11.2 8.2 %collective-permute-start.1 = (bf16[16,256]{1,0:T(8,128)(2,1)S(1)}, bf16[16,256]{1,0:T(8,128)(2,1)S(1)}, u32[]{:S(2)}, u32[]{:S(2)}) collective-permute-start(bf16[16,256]{1,0:T(8,128)(2,1)S(1)} %get-tuple-element.40), channel_id=1, source_target_pairs={{8,0},{12,4},{16,8},{20,12},{24,16},{28,20},{32,24},{36,28},{40,32... | collective-permute-start | bytes 24584 | tf_op jit(solution)/shard_map/ppermute | solution.py:373
  21.1 1.1 copy-done.2
  23.9 3.5 %edge_local.1 = (f32[1536,256]{1,0:T(8,128)S(1)}, bf16[1536,512]{1,0:T(8,128)(2,1)S(1)}, bf16[1536,32]{1,0:T(8,128)(2,1)S(1)}) custom-call(s32[1]{0:T(128)S(6)} %copy.17.count_ref, s32[2,1536]{1,0:T(2,128)S(1)} %bitcast.21, bf16[512,256]{1,0:T(8,128)(2,1)S(1)} %bitcast.14, bf16[1536,256]{1,0:T(8,128)(2,1)S(1)} %bitcast.10, bf16[768,256]{1,0:T(8,128)(2,1)S(1)} %copy-done), custom_call_target="tpu_custom_call" | custom-call | flops 1409286144 | bytes 1409286 | tf_op jit(solution)/shard_map/edge_local/pallas_call | solution.py:356
  27.5 3.2 %edge_forward.1 = (f32[1536,256]{1,0:T(8,128)S(1)}, bf16[1536,256]{1,0:T(8,128)(2,1)S(1)}, f32[1536,256]{1,0:T(8,128)S(1)}, f32[1536,1]{1,0:T(8,128)S(1)}, f32[5...) custom-call(s32[1]{0:T(128)S(6)} %copy.17.count_ref, s32[2,1536]{1,0:T(2,128)S(1)} %bitcast.22, ...), custom_call_target="tpu_custom_call" | custom-call | flops 805306368 | bytes 805306 | tf_op jit(solution)/shard_map/edge_forward/pallas_call | solution.py:356
  30.8 3.3 %collective-permute-start.2 = (f32[16,256]{1,0:T(8,128)S(1)}, f32[16,256]{1,0:T(8,128)S(1)}, u32[]{:S(2)}, u32[]{:S(2)}) collective-permute-start(f32[16,256]{1,0:T(8,128)S(1)} %get-tuple-element.44), channel_id=1, source_target_pairs={{508,0},{0,4},{4,8},{8,12},{12,16},{16,20},{20,24},{24,28},{28,32}... | collective-permute-start | bytes 49160 | tf_op jit(solution)/shard_map/ppermute | solution.py:373
  34.0 1.9 %collective-permute-start.3 = (f32[16,256]{1,0:T(8,128)S(1)}, f32[16,256]{1,0:T(8,128)S(1)}, u32[]{:S(2)}, u32[]{:S(2)}) collective-permute-start(f32[16,256]{1,0:T(8,128)S(1)} %get-tuple-element.45), channel_id=1, source_target_pairs={{504,0},{508,4},{0,8},{4,12},{8,16},{12,20},{16,24},{20,28},{24,32... | collective-permute-start | bytes 49160 | tf_op jit(solution)/shard_map/ppermute | solution.py:373
  36.0 6.0 %collective-permute-done.3.got1_ref = f32[16,256]{1,0:T(8,128)S(1)} collective-permute-done((f32[16,256]{1,0:T(8,128)S(1)}, f32[16,256]{1,0:T(8,128)S(1)}, u32[]{:S(2)}, u32[]{:S(2)}) %collective-permute-start.3) | collective-permute-done | bytes 16416 | tf_op jit(solution)/shard_map/ppermute | solution.py:373
  42.0 2.7 %node.1 = (bf16[512,256]{1,0:T(8,128)(2,1)}, bf16[512,256]{1,0:T(8,128)(2,1)S(1)}, bf16[512,256]{1,0:T(8,128)(2,1)S(1)}, bf16[512,256]{1,0:T(8,128)(2,1)S(1)}, b...) custom-call(s32[2,16]{1,0:T(2,128)S(1)} %copy-done.13, ...), custom_call_target="tpu_custom_call" | custom-call | flops 536870912 | bytes 536870 | tf_op jit(solution)/shard_map/node/pallas_call | solution.py:356
  44.7 2.3 %collective-permute-start.4 = (bf16[16,256]{1,0:T(8,128)(2,1)S(1)}, bf16[16,256]{1,0:T(8,128)(2,1)S(1)}, u32[]{:S(2)}, u32[]{:S(2)}) collective-permute-start(bf16[16,256]{1,0:T(8,128)(2,1)S(1)} %get-tuple-element.54), channel_id=1, source_target_pairs={{4,0},{8,4},{12,8},{16,12},{20,16},{24,20},{28,24},{32,28},{36,32}... | collective-permute-start | bytes 24584 | tf_op jit(solution)/shard_map/ppermute | solution.py:373
  47.0 2.1 %collective-permute-start.5 = (bf16[16,256]{1,0:T(8,128)(2,1)S(1)}, bf16[16,256]{1,0:T(8,128)(2,1)S(1)}, u32[]{:S(2)}, u32[]{:S(2)}) collective-permute-start(bf16[16,256]{1,0:T(8,128)(2,1)S(1)} %get-tuple-element.55), channel_id=1, source_target_pairs={{8,0},{12,4},{16,8},{20,12},{24,16},{28,20},{32,24},{36,28},{40,32... | collective-permute-start | bytes 24584 | tf_op jit(solution)/shard_map/ppermute | solution.py:373
  49.2 1.4 %fill.1 = (bf16[768,256]{1,0:T(8,128)(2,1)S(1)}, f32[512,256]{1,0:T(8,128)S(1)}, f32[1536,256]{1,0:T(8,128)S(1)}) custom-call(bf16[512,256]{1,0:T(8,128)(2,1)S(1)} %bitcast.16, bf16[512,256]{1,0:T(8,128)(2,1)S(1)} %bitcast.20, bf16[512,256]{1,0:T(8,128)(2,1)S(1)} %get-tuple-element.47.agg16_ref, bf16[512,256]{1,0:T(8,128)(2,1)S(1)} %get-tuple-element.48.hidden_ref, ...), custom_call_target="tpu_custom_call" | custom-call | flops 805306368 | bytes 805306 | tf_op jit(solution)/shard_map/fill/pallas_call | solution.py:356
  51.4 4.8 %edge_backward.1 = (bf16[1536,256]{1,0:T(8,128)(2,1)}, bf16[3584,128]{1,0:T(8,128)(2,1)S(1)}, f32[512,256]{1,0:T(8,128)S(1)}, f32[16,256]{1,0:T(8,128)S(1)}, f32[16,256]{1,0:T(8,128)S(1)}) custom-call(s32[1]{0:T(128)S(6)} %copy.17.count_ref, s32[2,1536]{1,0:T(2,128)S(1)} %bitcast.23, bf16[512,256]{1,0:T(8,128)(2,1)S(1)} %bitcast.17, ...), custom_call_target="tpu_custom_call" | custom-call | flops 2415919104 | bytes 2415919 | tf_op jit(solution)/shard_map/edge_backward/pallas_call | solution.py:356
  56.2 22.6 %all_to_all.15 = bf16[64,56,128]{2,1,0:T(8,128)(2,1)S(1)} all-to-all(bf16[64,56,128]{2,1,0:T(8,128)(2,1)S(1)} %bitcast.18), channel_id=1, replica_groups=mesh['y'=4,'zh'=8,'zl'=2,'c'=2,'rep'=4] {'y','zl','c','rep'}, dimensions={0} | all-to-all | bytes 1835008 | tf_op jit(solution)/shard_map/all_to_all | solution.py:384
  79.1 18.2 %all_to_all.16 = bf16[8,56,128]{2,1,0:T(8,128)(2,1)S(1)} all-to-all(bf16[8,56,128]{2,1,0:T(8,128)(2,1)S(1)} %broadcast_in_dim.24), channel_id=1, replica_groups=mesh['y'=4,'zh'=8,'zl'=2,'c'=2,'rep'=4] {'zh'}, dimensions={0} | all-to-all | bytes 229376 | tf_op jit(solution)/shard_map/all_to_all | solution.py:387
  97.3 1.1 broadcast_in_dim.25
  98.3 7.3 %all-to-all-start.2 = ((bf16[64,56,128]{2,1,0:T(8,128)(2,1)}), bf16[64,56,128]{2,1,0:T(8,128)(2,1)S(1)}, u32[]{:S(2)}, u32[]{:S(2)}) async-start(bf16[64,56,128]{2,1,0:T(8,128)(2,1)} %broadcast_in_dim.25), calls=%async_computation.2 | async-start | bytes 1835008 | tf_op jit(solution)/shard_map/all_to_all | solution.py:390
  105.7 3.5 %collective-permute-start.6 = (f32[16,256]{1,0:T(8,128)S(1)}, f32[16,256]{1,0:T(8,128)S(1)}, u32[]{:S(2)}, u32[]{:S(2)}) collective-permute-start(f32[16,256]{1,0:T(8,128)S(1)} %get-tuple-element.63), channel_id=1, source_target_pairs={{508,0},{0,4},{4,8},{8,12},{12,16},{16,20},{20,24},{24,28},{28,32}... | collective-permute-start | bytes 49160 | tf_op jit(solution)/shard_map/ppermute | solution.py:373
  109.2 1.9 %collective-permute-start.7 = (f32[16,256]{1,0:T(8,128)S(1)}, f32[16,256]{1,0:T(8,128)S(1)}, u32[]{:S(2)}, u32[]{:S(2)}) collective-permute-start(f32[16,256]{1,0:T(8,128)S(1)} %get-tuple-element.64), channel_id=1, source_target_pairs={{504,0},{508,4},{0,8},{4,12},{8,16},{12,20},{16,24},{20,28},{24,32... | collective-permute-start | bytes 49160 | tf_op jit(solution)/shard_map/ppermute | solution.py:373
  111.1 4.5 %collective-permute-done.6.got0_ref = f32[16,256]{1,0:T(8,128)S(1)} collective-permute-done((f32[16,256]{1,0:T(8,128)S(1)}, f32[16,256]{1,0:T(8,128)S(1)}, u32[]{:S(2)}, u32[]{:S(2)}) %collective-permute-start.6) | collective-permute-done | bytes 16416 | tf_op jit(solution)/shard_map/ppermute | solution.py:373
  115.7 1.6 %collective-permute-done.7.got1_ref = f32[16,256]{1,0:T(8,128)S(1)} collective-permute-done((f32[16,256]{1,0:T(8,128)S(1)}, f32[16,256]{1,0:T(8,128)S(1)}, u32[]{:S(2)}, u32[]{:S(2)}) %collective-permute-start.7) | collective-permute-done | bytes 16416 | tf_op jit(solution)/shard_map/ppermute | solution.py:373
  117.3 2.8 %finish.1 = bf16[512,256]{1,0:T(8,128)(2,1)} custom-call(s32[2,16]{1,0:T(2,128)S(1)} %copy-done.13, f32[512,256]{1,0:T(8,128)S(1)} %get-tuple-element.62.part_ref, f32[16,256]{1,0:T(8,128)S(1)} %collective-permute-done.6.got0_ref, f32[16,256]{1,0:T(8,128)S(1)} %collective-permute-done.7.got1_ref, bf16[768,256]{1,0:T(8,128)(2,1)S(1)} %copy-done.1), custom_call_target="tpu_custom_call" | custom-call | flops 67108864 | bytes 67108 | tf_op jit(solution)/shard_map/finish/pallas_call | solution.py:356
  120.1 1.3 %all-to-all-done.2 = bf16[64,56,128]{2,1,0:T(8,128)(2,1)S(1)} async-done(((bf16[64,56,128]{2,1,0:T(8,128)(2,1)}), bf16[64,56,128]{2,1,0:T(8,128)(2,1)S(1)}, u32[]{:S(2)}, u32[]{:S(2)}) %all-to-all-start.2) | async-done | bytes 917536 | tf_op jit(solution)/shard_map/all_to_all | solution.py:390
  121.3 1.1 unpack.1
  (38 shorter events, 5.6 us)
Async XLA Ops:
  0.6 1.0 copy-start.4
  1.6 0.7 copy-start.12
  2.5 24.9 %collective-permute-start = (bf16[16,256]{1,0:T(8,128)(2,1)S(1)}, bf16[16,256]{1,0:T(8,128)(2,1)S(1)}, u32[]{:S(2)}, u32[]{:S(2)}) collective-permute-start(bf16[16,256]{1,0:T(8,128)(2,1)S(1)} %get-tuple-element.39), channel_id=1, source_target_pairs={{4,0},{8,4},{12,8},{16,12},{20,16},{24,20},{28,24},{32,28},{36,32}... | collective-permute-start | bytes 24584 | tf_op jit(solution)/shard_map/ppermute | solution.py:373
  11.2 16.2 %collective-permute-start.1 = (bf16[16,256]{1,0:T(8,128)(2,1)S(1)}, bf16[16,256]{1,0:T(8,128)(2,1)S(1)}, u32[]{:S(2)}, u32[]{:S(2)}) collective-permute-start(bf16[16,256]{1,0:T(8,128)(2,1)S(1)} %get-tuple-element.40), channel_id=1, source_target_pairs={{8,0},{12,4},{16,8},{20,12},{24,16},{28,20},{32,24},{36,28},{40,32... | collective-permute-start | bytes 24584 | tf_op jit(solution)/shard_map/ppermute | solution.py:373
  20.1 1.0 copy-start
  21.1 1.1 copy-start.2
  22.2 0.9 copy-start.5
  23.2 0.7 copy-start.10
  23.9 3.5 %copy-start.1 = (bf16[768,256]{1,0:T(8,128)(2,1)S(1)}, bf16[768,256]{1,0:T(8,128)(2,1)}, u32[]{:S(2)}) copy-start(bf16[768,256]{1,0:T(8,128)(2,1)} %ef_ref.7) | copy-start | bytes 1179652
  23.9 3.5 %copy-start.7 = (bf16[256,256]{1,0:T(8,128)(2,1)S(1)}, bf16[256,256]{1,0:T(8,128)(2,1)}, u32[]{:S(2)}) copy-start(bf16[256,256]{1,0:T(8,128)(2,1)} %es_ref.3) | copy-start | bytes 393220
  27.5 14.5 %copy-start.6 = (bf16[1,512,256]{2,1,0:T(8,128)(2,1)S(1)}, bf16[1,512,256]{2,1,0:T(8,128)(2,1)}, u32[]{:S(2)}) copy-start(bf16[1,512,256]{2,1,0:T(8,128)(2,1)} %param.10) | copy-start | bytes 786436
  27.5 14.5 %copy-start.8 = (bf16[1,512,256]{2,1,0:T(8,128)(2,1)S(1)}, bf16[1,512,256]{2,1,0:T(8,128)(2,1)}, u32[]{:S(2)}) copy-start(bf16[1,512,256]{2,1,0:T(8,128)(2,1)} %param.15) | copy-start | bytes 786436
  27.5 14.5 %copy-start.9 = (bf16[512,256]{1,0:T(8,128)(2,1)S(1)}, bf16[512,256]{1,0:T(8,128)(2,1)}, u32[]{:S(2)}) copy-start(bf16[512,256]{1,0:T(8,128)(2,1)} %nf_ref.3) | copy-start | bytes 786436
  27.5 14.5 %copy-start.13 = (s32[2,16]{1,0:T(2,128)S(1)}, s32[2,16]{1,0:T(2,128)}, u32[]{:S(2)}) copy-start(s32[2,16]{1,0:T(2,128)} %send_ref.5) | copy-start | bytes 388
  27.5 14.5 %copy-start.14 = (bf16[256,256]{1,0:T(8,128)(2,1)S(1)}, bf16[256,256]{1,0:T(8,128)(2,1)}, u32[]{:S(2)}) copy-start(bf16[256,256]{1,0:T(8,128)(2,1)} %ns_ref.1) | copy-start | bytes 393220
  30.8 5.2 %collective-permute-start.2 = (f32[16,256]{1,0:T(8,128)S(1)}, f32[16,256]{1,0:T(8,128)S(1)}, u32[]{:S(2)}, u32[]{:S(2)}) collective-permute-start(f32[16,256]{1,0:T(8,128)S(1)} %get-tuple-element.44), channel_id=1, source_target_pairs={{508,0},{0,4},{4,8},{8,12},{12,16},{16,20},{20,24},{24,28},{28,32}... | collective-permute-start | bytes 49160 | tf_op jit(solution)/shard_map/ppermute | solution.py:373
  34.0 8.0 %collective-permute-start.3 = (f32[16,256]{1,0:T(8,128)S(1)}, f32[16,256]{1,0:T(8,128)S(1)}, u32[]{:S(2)}, u32[]{:S(2)}) collective-permute-start(f32[16,256]{1,0:T(8,128)S(1)} %get-tuple-element.45), channel_id=1, source_target_pairs={{504,0},{508,4},{0,8},{4,12},{8,16},{12,20},{16,24},{20,28},{24,32... | collective-permute-start | bytes 49160 | tf_op jit(solution)/shard_map/ppermute | solution.py:373
  44.7 5.8 %collective-permute-start.4 = (bf16[16,256]{1,0:T(8,128)(2,1)S(1)}, bf16[16,256]{1,0:T(8,128)(2,1)S(1)}, u32[]{:S(2)}, u32[]{:S(2)}) collective-permute-start(bf16[16,256]{1,0:T(8,128)(2,1)S(1)} %get-tuple-element.54), channel_id=1, source_target_pairs={{4,0},{8,4},{12,8},{16,12},{20,16},{24,20},{28,24},{32,28},{36,32}... | collective-permute-start | bytes 24584 | tf_op jit(solution)/shard_map/ppermute | solution.py:373
  47.0 4.4 %collective-permute-start.5 = (bf16[16,256]{1,0:T(8,128)(2,1)S(1)}, bf16[16,256]{1,0:T(8,128)(2,1)S(1)}, u32[]{:S(2)}, u32[]{:S(2)}) collective-permute-start(bf16[16,256]{1,0:T(8,128)(2,1)S(1)} %get-tuple-element.55), channel_id=1, source_target_pairs={{8,0},{12,4},{16,8},{20,12},{24,16},{28,20},{32,24},{36,28},{40,32... | collective-permute-start | bytes 24584 | tf_op jit(solution)/shard_map/ppermute | solution.py:373
  49.1 2.3 %copy-start.3 = (bf16[1,1536,256]{2,1,0:T(8,128)(2,1)S(1)}, bf16[1,1536,256]{2,1,0:T(8,128)(2,1)}, u32[]{:S(2)}) copy-start(bf16[1,1536,256]{2,1,0:T(8,128)(2,1)} %param.11) | copy-start | bytes 2359300
  49.1 2.3 %copy-start.11 = (s32[1536,2]{0,1:T(2,128)S(1)}, s32[1536,2]{0,1:T(2,128)}, u32[]{:S(2)}) copy-start(s32[1536,2]{0,1:T(2,128)} %param.12) | copy-start | bytes 36868
  98.3 23.0 %all-to-all-start.2 = ((bf16[64,56,128]{2,1,0:T(8,128)(2,1)}), bf16[64,56,128]{2,1,0:T(8,128)(2,1)S(1)}, u32[]{:S(2)}, u32[]{:S(2)}) async-start(bf16[64,56,128]{2,1,0:T(8,128)(2,1)} %broadcast_in_dim.25), calls=%async_computation.2 | async-start | bytes 1835008 | tf_op jit(solution)/shard_map/all_to_all | solution.py:390
  105.7 10.0 %collective-permute-start.6 = (f32[16,256]{1,0:T(8,128)S(1)}, f32[16,256]{1,0:T(8,128)S(1)}, u32[]{:S(2)}, u32[]{:S(2)}) collective-permute-start(f32[16,256]{1,0:T(8,128)S(1)} %get-tuple-element.63), channel_id=1, source_target_pairs={{508,0},{0,4},{4,8},{8,12},{12,16},{16,20},{20,24},{24,28},{28,32}... | collective-permute-start | bytes 49160 | tf_op jit(solution)/shard_map/ppermute | solution.py:373
  109.2 8.1 %collective-permute-start.7 = (f32[16,256]{1,0:T(8,128)S(1)}, f32[16,256]{1,0:T(8,128)S(1)}, u32[]{:S(2)}, u32[]{:S(2)}) collective-permute-start(f32[16,256]{1,0:T(8,128)S(1)} %get-tuple-element.64), channel_id=1, source_target_pairs={{504,0},{508,4},{0,8},{4,12},{8,16},{12,20},{16,24},{20,28},{24,32... | collective-permute-start | bytes 49160 | tf_op jit(solution)/shard_map/ppermute | solution.py:373

commit v3 on v2

--- a/solution.py
+++ b/solution.py
@@ -86,10 +86,51 @@
     return jnp.dot(pick, rows, preferred_element_type=F32, precision=lax.Precision.HIGHEST)
 
 
-def seam_kernel(send_ref, nodes_ref, out0_ref, out1_ref):
+def load_kernel(
+    send_hbm,
+    nodes_hbm,
+    ends_hbm,
+    ef_hbm,
+    edges_hbm,
+    out0_ref,
+    out1_ref,
+    send_ref,
+    nodes_ref,
+    ends_ref,
+    ef_ref,
+    edges_ref,
+    sems,
+):
+    sources = (send_hbm, nodes_hbm, ends_hbm, ef_hbm, edges_hbm)
+    targets = (send_ref, nodes_ref, ends_ref, ef_ref, edges_ref)
+    copies = [
+        pltpu.make_async_copy(source, target, sems.at[i])
+        for i, (source, target) in enumerate(zip(sources, targets))
+    ]
+    for copy in copies:
+        copy.start()
+    copies[0].wait()
+    copies[1].wait()
     table = nodes_ref[...]
     out0_ref[...] = seam_pick(send_ref, 0, table)
     out1_ref[...] = seam_pick(send_ref, 1, table)
+    for copy in copies[2:]:
+        copy.wait()
+
+
+def load(sources):
+    send, nodes = sources[:2]
+    seam = jax.ShapeDtypeStruct((send.shape[1], nodes.shape[1]), BF)
+    return pl.pallas_call(
+        load_kernel,
+        out_shape=[seam, seam] + [jax.ShapeDtypeStruct(x.shape, x.dtype) for x in sources],
+        in_specs=[pl.BlockSpec(memory_space=pltpu.HBM) for _ in sources],
+        out_specs=[pl.BlockSpec(memory_space=pltpu.VMEM) for _ in range(2 + len(sources))],
+        scratch_shapes=[pltpu.SemaphoreType.DMA((len(sources),))],
+        compiler_params=pltpu.CompilerParams(vmem_limit_bytes=24 * 2**20),
+        cost_estimate=pl.CostEstimate(flops=10**8, transcendentals=0, bytes_accessed=10**6),
+        name="load",
+    )(*[pltpu.with_memory_space_constraint(x, pltpu.HBM) for x in sources])
 
 
 def edge_local_kernel(
@@ -377,17 +418,39 @@
     return lax.axis_size(axes)
 
 
+def sum_kernel(pieces_ref, out_ref):
+    count = pieces_ref.shape[0]
+    copies = out_ref.shape[0]
+    total = lax.fori_loop(
+        1,
+        count,
+        lambda i, acc: acc + pieces_ref[i].astype(F32),
+        pieces_ref[0].astype(F32),
+        unroll=7,
+    ).astype(BF)
+
+    def store(i, carry):
+        out_ref[i] = total
+        return carry
+
+    lax.fori_loop(0, copies, store, 0, unroll=8)
+
+
+def sum_and_copy(pieces, copies, name):
+    (out,) = call(
+        sum_kernel, [((copies,) + pieces.shape[1:], BF)], (pieces,), flops=pieces.size, name=name
+    )
+    return out
+
+
 def sum_everywhere(pack):
     inner = group_size(INNER)
     outer = group_size(OUTER)
     rows, lanes = pack.shape
     pieces = lax.all_to_all(pack.reshape(inner, rows // inner, lanes), INNER, 0, 0)
-    mine = jnp.sum(pieces.astype(F32), axis=0).astype(BF)
-    spread = jnp.broadcast_to(mine[None], (outer,) + mine.shape)
-    pieces = lax.all_to_all(spread, OUTER, 0, 0)
-    mine = jnp.sum(pieces.astype(F32), axis=0).astype(BF)
-    spread = jnp.broadcast_to(mine[None], (inner,) + mine.shape)
-    return lax.all_to_all(spread, INNER, 0, 0).reshape(rows, lanes)
+    pieces = lax.all_to_all(sum_and_copy(pieces, outer, "inner_sum"), OUTER, 0, 0)
+    pieces = lax.all_to_all(sum_and_copy(pieces, inner, "outer_sum"), INNER, 0, 0)
+    return pieces.reshape(rows, lanes)
 
 
 def local(
@@ -414,7 +477,9 @@
     seam32 = ((seam, features), F32)
     unit = 2 * features * features
 
-    out0, out1 = call(seam_kernel, [seam16, seam16], (send_rows, node_rows), flops=10**8, name="seam")
+    out0, out1, send_rows, node_rows, ends, edge_first, edge_rows = load(
+        (send_rows, node_rows, ends, edge_first, edge_rows)
+    )
     halo0 = shift(out0, -1)
     halo1 = shift(out1, -2)
     part, pairs, far = call(

time: 123 us -> 119 us (0.967)
  local copies, waits for them, and re-layouts: 6.53 us -> 0.03 us
  Pallas kernels: 19.7 us -> 22.1 us
    unnamed x30 -> x8, local copies, waits for them, and re-layouts: 5.45 us -> 0.03 us
    pallas_call x0 -> x1, Pallas kernels: none -> 1.41 us  [load(): pl.pallas_call(load_kernel, out_shape=[seam, seam] + [jax.ShapeDtypeStruc...]
    pallas_call x8 -> x9, Pallas kernels: 19.7 us -> 20.7 us  [call(): pl.pallas_call(kernel, out_shape=[jax.ShapeDtypeStruct(shape, kind) for s...]
where the time goes in v3:
time: 119 us; the launch traced here: 118 us
  blocking collectives  40.8 us (34%)
  starting transfers between devices  39.3 us (33%)
  Pallas kernels  22.1 us (19%)
  waiting for transfers between devices  14.4 us (12%)
  between operations  1.47 us (1%)
    ppermute x8, starting transfers between devices, shift(): lax.ppermute(block, PATCH, [((i - distance) % count, i) for i in range(co...  32 us
    all_to_all x1, blocking collectives, sum_everywhere(): lax.all_to_all(pack.reshape(inner, rows // inner, lanes), INNER, 0, 0)  22.6 us
    pallas_call x9, Pallas kernels, call(): pl.pallas_call(kernel, out_shape=[jax.ShapeDtypeStruct(shape, kind) for s...  20.7 us
    all_to_all x1, blocking collectives, sum_everywhere(): lax.all_to_all(sum_and_copy(pieces, outer, 'inner_sum'), OUTER, 0, 0)  18.2 us
    ppermute x8, waiting for transfers between devices, shift(): lax.ppermute(block, PATCH, [((i - distance) % count, i) for i in range(co...  13.1 us
    all_to_all x1, starting transfers between devices, sum_everywhere(): lax.all_to_all(sum_and_copy(pieces, inner, 'outer_sum'), INNER, 0, 0)  7.34 us
  transfers between devices with their start and end apart: 9, of which 5 were waited for; matrix products, arithmetic and copies ran while one was open for 0% of the time, Pallas kernels for 6%

profile of v3, /device:TPU:1, one launch (start us, length us, event | category | flops | bytes accessed | tf_op | source)
XLA Modules:
  0.0 118.1 jit_solution(13426878131045322657)
XLA Ops:
  0.6 1.4 %load.1 = (bf16[16,256]{1,0:T(8,128)(2,1)S(1)}, bf16[16,256]{1,0:T(8,128)(2,1)S(1)}, s32[2,16]{1,0:T(2,128)S(1)}, bf16[512,256]{1,0:T(8,128)(2,1)S(1)}, s32[2,15...) custom-call(s32[2,16]{1,0:T(2,128)} %send_hbm.1, bf16[512,256]{1,0:T(8,128)(2,1)} %bitcast.14, ...), custom_call_target="tpu_custom_call" | custom-call | flops 100000000 | bytes 1000000 | tf_op jit(solution)/shard_map/load/pallas_call | solution.py:124
  2.1 8.7 %collective-permute-start = (bf16[16,256]{1,0:T(8,128)(2,1)S(1)}, bf16[16,256]{1,0:T(8,128)(2,1)S(1)}, u32[]{:S(2)}, u32[]{:S(2)}) collective-permute-start(bf16[16,256]{1,0:T(8,128)(2,1)S(1)} %get-tuple-element.47), channel_id=1, source_target_pairs={{4,0},{8,4},{12,8},{16,12},{20,16},{24,20},{28,24},{32,28},{36,32}... | collective-permute-start | bytes 24584 | tf_op jit(solution)/shard_map/ppermute | solution.py:414
  10.8 8.2 %collective-permute-start.1 = (bf16[16,256]{1,0:T(8,128)(2,1)S(1)}, bf16[16,256]{1,0:T(8,128)(2,1)S(1)}, u32[]{:S(2)}, u32[]{:S(2)}) collective-permute-start(bf16[16,256]{1,0:T(8,128)(2,1)S(1)} %get-tuple-element.48), channel_id=1, source_target_pairs={{8,0},{12,4},{16,8},{20,12},{24,16},{28,20},{32,24},{36,28},{40,32... | collective-permute-start | bytes 24584 | tf_op jit(solution)/shard_map/ppermute | solution.py:414
  19.7 3.5 %edge_local.1 = (f32[1536,256]{1,0:T(8,128)S(1)}, bf16[1536,512]{1,0:T(8,128)(2,1)S(1)}, bf16[1536,32]{1,0:T(8,128)(2,1)S(1)}) custom-call(s32[1]{0:T(128)S(6)} %copy.17.count_ref, s32[2,1536]{1,0:T(2,128)S(1)} %get-tuple-element.46.ends_ref, bf16[512,256]{1,0:T(8,128)(2,1)S(1)} %get-tuple-element.45.nodes_ref, ...), custom_call_target="tpu_custom_call" | custom-call | flops 1409286144 | bytes 1409286 | tf_op jit(solution)/shard_map/edge_local/pallas_call | solution.py:397
  23.3 3.2 %edge_forward.1 = (f32[1536,256]{1,0:T(8,128)S(1)}, bf16[1536,256]{1,0:T(8,128)(2,1)S(1)}, f32[1536,256]{1,0:T(8,128)S(1)}, f32[1536,1]{1,0:T(8,128)S(1)}, f32[5...) custom-call(s32[1]{0:T(128)S(6)} %copy.17.count_ref, s32[2,1536]{1,0:T(2,128)S(1)} %get-tuple-element.46.ends_ref, ...), custom_call_target="tpu_custom_call" | custom-call | flops 805306368 | bytes 805306 | tf_op jit(solution)/shard_map/edge_forward/pallas_call | solution.py:397
  26.5 3.3 %collective-permute-start.2 = (f32[16,256]{1,0:T(8,128)S(1)}, f32[16,256]{1,0:T(8,128)S(1)}, u32[]{:S(2)}, u32[]{:S(2)}) collective-permute-start(f32[16,256]{1,0:T(8,128)S(1)} %get-tuple-element.54), channel_id=1, source_target_pairs={{508,0},{0,4},{4,8},{8,12},{12,16},{16,20},{20,24},{24,28},{28,32}... | collective-permute-start | bytes 49160 | tf_op jit(solution)/shard_map/ppermute | solution.py:414
  29.8 1.9 %collective-permute-start.3 = (f32[16,256]{1,0:T(8,128)S(1)}, f32[16,256]{1,0:T(8,128)S(1)}, u32[]{:S(2)}, u32[]{:S(2)}) collective-permute-start(f32[16,256]{1,0:T(8,128)S(1)} %get-tuple-element.55), channel_id=1, source_target_pairs={{504,0},{508,4},{0,8},{4,12},{8,16},{12,20},{16,24},{20,28},{24,32... | collective-permute-start | bytes 49160 | tf_op jit(solution)/shard_map/ppermute | solution.py:414
  31.8 6.0 %collective-permute-done.3.got1_ref = f32[16,256]{1,0:T(8,128)S(1)} collective-permute-done((f32[16,256]{1,0:T(8,128)S(1)}, f32[16,256]{1,0:T(8,128)S(1)}, u32[]{:S(2)}, u32[]{:S(2)}) %collective-permute-start.3) | collective-permute-done | bytes 16416 | tf_op jit(solution)/shard_map/ppermute | solution.py:414
  37.8 2.7 %node.1 = (bf16[512,256]{1,0:T(8,128)(2,1)}, bf16[512,256]{1,0:T(8,128)(2,1)S(1)}, bf16[512,256]{1,0:T(8,128)(2,1)S(1)}, bf16[512,256]{1,0:T(8,128)(2,1)S(1)}, b...) custom-call(s32[2,16]{1,0:T(2,128)S(1)} %get-tuple-element.44.send_r, ...), custom_call_target="tpu_custom_call" | custom-call | flops 536870912 | bytes 536870 | tf_op jit(solution)/shard_map/node/pallas_call | solution.py:397
  40.5 2.3 %collective-permute-start.4 = (bf16[16,256]{1,0:T(8,128)(2,1)S(1)}, bf16[16,256]{1,0:T(8,128)(2,1)S(1)}, u32[]{:S(2)}, u32[]{:S(2)}) collective-permute-start(bf16[16,256]{1,0:T(8,128)(2,1)S(1)} %get-tuple-element.64), channel_id=1, source_target_pairs={{4,0},{8,4},{12,8},{16,12},{20,16},{24,20},{28,24},{32,28},{36,32}... | collective-permute-start | bytes 24584 | tf_op jit(solution)/shard_map/ppermute | solution.py:414
  42.8 2.1 %collective-permute-start.5 = (bf16[16,256]{1,0:T(8,128)(2,1)S(1)}, bf16[16,256]{1,0:T(8,128)(2,1)S(1)}, u32[]{:S(2)}, u32[]{:S(2)}) collective-permute-start(bf16[16,256]{1,0:T(8,128)(2,1)S(1)} %get-tuple-element.65), channel_id=1, source_target_pairs={{8,0},{12,4},{16,8},{20,12},{24,16},{28,20},{32,24},{36,28},{40,32... | collective-permute-start | bytes 24584 | tf_op jit(solution)/shard_map/ppermute | solution.py:414
  44.9 1.4 %fill.1 = (bf16[768,256]{1,0:T(8,128)(2,1)S(1)}, f32[512,256]{1,0:T(8,128)S(1)}, f32[1536,256]{1,0:T(8,128)S(1)}) custom-call(bf16[512,256]{1,0:T(8,128)(2,1)S(1)} %get-tuple-element.45.nodes_ref, bf16[512,256]{1,0:T(8,128)(2,1)S(1)} %bitcast.12, bf16[512,256]{1,0:T(8,128)(2,1)S(1)} %get-tuple-element.57.agg16_ref, ...), custom_call_target="tpu_custom_call" | custom-call | flops 805306368 | bytes 805306 | tf_op jit(solution)/shard_map/fill/pallas_call | solution.py:397
  47.2 4.8 %edge_backward.1 = (bf16[1536,256]{1,0:T(8,128)(2,1)}, bf16[3584,128]{1,0:T(8,128)(2,1)S(1)}, f32[512,256]{1,0:T(8,128)S(1)}, f32[16,256]{1,0:T(8,128)S(1)}, f32[16,256]{1,0:T(8,128)S(1)}) custom-call(s32[1]{0:T(128)S(6)} %copy.17.count_ref, s32[2,1536]{1,0:T(2,128)S(1)} %get-tuple-element.46.ends_ref, bf16[512,256]{1,0:T(8,128)(2,1)S(1)} %get-tuple-element.45.nodes_ref, ...), custom_call_target="tpu_custom_call" | custom-call | flops 2415919104 | bytes 2415919 | tf_op jit(solution)/shard_map/edge_backward/pallas_call | solution.py:397
  52.0 22.6 %all_to_all.15.pieces_ref = bf16[64,56,128]{2,1,0:T(8,128)(2,1)S(1)} all-to-all(bf16[64,56,128]{2,1,0:T(8,128)(2,1)S(1)} %bitcast.10), channel_id=1, replica_groups=mesh['y'=4,'zh'=8,'zl'=2,'c'=2,'rep'=4] {'y','zl','c','rep'}, dimensions={0} | all-to-all | bytes 1835008 | tf_op jit(solution)/shard_map/all_to_all | solution.py:450
  74.8 18.2 %all_to_all.16.pieces_ref = bf16[8,56,128]{2,1,0:T(8,128)(2,1)S(1)} all-to-all(bf16[8,56,128]{2,1,0:T(8,128)(2,1)S(1)} %inner_sum.1), channel_id=1, replica_groups=mesh['y'=4,'zh'=8,'zl'=2,'c'=2,'rep'=4] {'zh'}, dimensions={0} | all-to-all | bytes 229376 | tf_op jit(solution)/shard_map/all_to_all | solution.py:451
  92.9 1.0 outer_sum.1
  94.0 7.3 %all-to-all-start.2 = ((bf16[64,56,128]{2,1,0:T(8,128)(2,1)}), bf16[64,56,128]{2,1,0:T(8,128)(2,1)S(1)}, u32[]{:S(2)}, u32[]{:S(2)}) async-start(bf16[64,56,128]{2,1,0:T(8,128)(2,1)} %outer_sum.1), calls=%async_computation.2 | async-start | bytes 1835008 | tf_op jit(solution)/shard_map/all_to_all | solution.py:452
  101.3 3.5 %collective-permute-start.6 = (f32[16,256]{1,0:T(8,128)S(1)}, f32[16,256]{1,0:T(8,128)S(1)}, u32[]{:S(2)}, u32[]{:S(2)}) collective-permute-start(f32[16,256]{1,0:T(8,128)S(1)} %get-tuple-element.73), channel_id=1, source_target_pairs={{508,0},{0,4},{4,8},{8,12},{12,16},{16,20},{20,24},{24,28},{28,32}... | collective-permute-start | bytes 49160 | tf_op jit(solution)/shard_map/ppermute | solution.py:414
  104.9 1.9 %collective-permute-start.7 = (f32[16,256]{1,0:T(8,128)S(1)}, f32[16,256]{1,0:T(8,128)S(1)}, u32[]{:S(2)}, u32[]{:S(2)}) collective-permute-start(f32[16,256]{1,0:T(8,128)S(1)} %get-tuple-element.74), channel_id=1, source_target_pairs={{504,0},{508,4},{0,8},{4,12},{8,16},{12,20},{16,24},{20,28},{24,32... | collective-permute-start | bytes 49160 | tf_op jit(solution)/shard_map/ppermute | solution.py:414
  106.8 4.5 %collective-permute-done.6.got0_ref = f32[16,256]{1,0:T(8,128)S(1)} collective-permute-done((f32[16,256]{1,0:T(8,128)S(1)}, f32[16,256]{1,0:T(8,128)S(1)}, u32[]{:S(2)}, u32[]{:S(2)}) %collective-permute-start.6) | collective-permute-done | bytes 16416 | tf_op jit(solution)/shard_map/ppermute | solution.py:414
  111.3 1.6 %collective-permute-done.7.got1_ref = f32[16,256]{1,0:T(8,128)S(1)} collective-permute-done((f32[16,256]{1,0:T(8,128)S(1)}, f32[16,256]{1,0:T(8,128)S(1)}, u32[]{:S(2)}, u32[]{:S(2)}) %collective-permute-start.7) | collective-permute-done | bytes 16416 | tf_op jit(solution)/shard_map/ppermute | solution.py:414
  113.0 2.8 %finish.1 = bf16[512,256]{1,0:T(8,128)(2,1)} custom-call(s32[2,16]{1,0:T(2,128)S(1)} %get-tuple-element.44.send_ref, f32[512,256]{1,0:T(8,128)S(1)} %get-tuple-element.72.part_ref, f32[16,256]{1,0:T(8,128)S(1)} %collective-permute-done.6.got0_ref, f32[16,256]{1,0:T(8,128)S(1)} %collective-permute-done.7.got1_ref, bf16[768,256]{1,0:T(8,128)(2,1)S(1)} %get-tuple-element.50.ef_ref), custom_call_target="tpu_custom_call" | custom-call | flops 67108864 | bytes 67108 | tf_op jit(solution)/shard_map/finish/pallas_call | solution.py:397
  115.7 1.3 %all-to-all-done.2 = bf16[64,56,128]{2,1,0:T(8,128)(2,1)S(1)} async-done(((bf16[64,56,128]{2,1,0:T(8,128)(2,1)}), bf16[64,56,128]{2,1,0:T(8,128)(2,1)S(1)}, u32[]{:S(2)}, u32[]{:S(2)}) %all-to-all-start.2) | async-done | bytes 917536 | tf_op jit(solution)/shard_map/all_to_all | solution.py:452
  117.0 1.1 unpack.1
  (14 shorter events, 1.1 us)
Async XLA Ops:
  2.1 21.2 %collective-permute-start = (bf16[16,256]{1,0:T(8,128)(2,1)S(1)}, bf16[16,256]{1,0:T(8,128)(2,1)S(1)}, u32[]{:S(2)}, u32[]{:S(2)}) collective-permute-start(bf16[16,256]{1,0:T(8,128)(2,1)S(1)} %get-tuple-element.47), channel_id=1, source_target_pairs={{4,0},{8,4},{12,8},{16,12},{20,16},{24,20},{28,24},{32,28},{36,32}... | collective-permute-start | bytes 24584 | tf_op jit(solution)/shard_map/ppermute | solution.py:414
  10.8 12.4 %collective-permute-start.1 = (bf16[16,256]{1,0:T(8,128)(2,1)S(1)}, bf16[16,256]{1,0:T(8,128)(2,1)S(1)}, u32[]{:S(2)}, u32[]{:S(2)}) collective-permute-start(bf16[16,256]{1,0:T(8,128)(2,1)S(1)} %get-tuple-element.48), channel_id=1, source_target_pairs={{8,0},{12,4},{16,8},{20,12},{24,16},{28,20},{32,24},{36,28},{40,32... | collective-permute-start | bytes 24584 | tf_op jit(solution)/shard_map/ppermute | solution.py:414
  19.7 3.6 %copy-start = (bf16[256,256]{1,0:T(8,128)(2,1)S(1)}, bf16[256,256]{1,0:T(8,128)(2,1)}, u32[]{:S(2)}) copy-start(bf16[256,256]{1,0:T(8,128)(2,1)} %es_ref.3) | copy-start | bytes 393220
  23.3 14.5 %copy-start.1 = (bf16[1,512,256]{2,1,0:T(8,128)(2,1)S(1)}, bf16[1,512,256]{2,1,0:T(8,128)(2,1)}, u32[]{:S(2)}) copy-start(bf16[1,512,256]{2,1,0:T(8,128)(2,1)} %param.15) | copy-start | bytes 786436
  23.3 14.5 %copy-start.2 = (bf16[512,256]{1,0:T(8,128)(2,1)S(1)}, bf16[512,256]{1,0:T(8,128)(2,1)}, u32[]{:S(2)}) copy-start(bf16[512,256]{1,0:T(8,128)(2,1)} %nf_ref.3) | copy-start | bytes 786436
  23.3 14.5 %copy-start.3 = (bf16[256,256]{1,0:T(8,128)(2,1)S(1)}, bf16[256,256]{1,0:T(8,128)(2,1)}, u32[]{:S(2)}) copy-start(bf16[256,256]{1,0:T(8,128)(2,1)} %ns_ref.1) | copy-start | bytes 393220
  26.5 5.2 %collective-permute-start.2 = (f32[16,256]{1,0:T(8,128)S(1)}, f32[16,256]{1,0:T(8,128)S(1)}, u32[]{:S(2)}, u32[]{:S(2)}) collective-permute-start(f32[16,256]{1,0:T(8,128)S(1)} %get-tuple-element.54), channel_id=1, source_target_pairs={{508,0},{0,4},{4,8},{8,12},{12,16},{16,20},{20,24},{24,28},{28,32}... | collective-permute-start | bytes 49160 | tf_op jit(solution)/shard_map/ppermute | solution.py:414
  29.8 8.0 %collective-permute-start.3 = (f32[16,256]{1,0:T(8,128)S(1)}, f32[16,256]{1,0:T(8,128)S(1)}, u32[]{:S(2)}, u32[]{:S(2)}) collective-permute-start(f32[16,256]{1,0:T(8,128)S(1)} %get-tuple-element.55), channel_id=1, source_target_pairs={{504,0},{508,4},{0,8},{4,12},{8,16},{12,20},{16,24},{20,28},{24,32... | collective-permute-start | bytes 49160 | tf_op jit(solution)/shard_map/ppermute | solution.py:414
  40.5 5.8 %collective-permute-start.4 = (bf16[16,256]{1,0:T(8,128)(2,1)S(1)}, bf16[16,256]{1,0:T(8,128)(2,1)S(1)}, u32[]{:S(2)}, u32[]{:S(2)}) collective-permute-start(bf16[16,256]{1,0:T(8,128)(2,1)S(1)} %get-tuple-element.64), channel_id=1, source_target_pairs={{4,0},{8,4},{12,8},{16,12},{20,16},{24,20},{28,24},{32,28},{36,32}... | collective-permute-start | bytes 24584 | tf_op jit(solution)/shard_map/ppermute | solution.py:414
  42.8 4.4 %collective-permute-start.5 = (bf16[16,256]{1,0:T(8,128)(2,1)S(1)}, bf16[16,256]{1,0:T(8,128)(2,1)S(1)}, u32[]{:S(2)}, u32[]{:S(2)}) collective-permute-start(bf16[16,256]{1,0:T(8,128)(2,1)S(1)} %get-tuple-element.65), channel_id=1, source_target_pairs={{8,0},{12,4},{16,8},{20,12},{24,16},{28,20},{32,24},{36,28},{40,32... | collective-permute-start | bytes 24584 | tf_op jit(solution)/shard_map/ppermute | solution.py:414
  94.0 23.0 %all-to-all-start.2 = ((bf16[64,56,128]{2,1,0:T(8,128)(2,1)}), bf16[64,56,128]{2,1,0:T(8,128)(2,1)S(1)}, u32[]{:S(2)}, u32[]{:S(2)}) async-start(bf16[64,56,128]{2,1,0:T(8,128)(2,1)} %outer_sum.1), calls=%async_computation.2 | async-start | bytes 1835008 | tf_op jit(solution)/shard_map/all_to_all | solution.py:452
  101.3 10.0 %collective-permute-start.6 = (f32[16,256]{1,0:T(8,128)S(1)}, f32[16,256]{1,0:T(8,128)S(1)}, u32[]{:S(2)}, u32[]{:S(2)}) collective-permute-start(f32[16,256]{1,0:T(8,128)S(1)} %get-tuple-element.73), channel_id=1, source_target_pairs={{508,0},{0,4},{4,8},{8,12},{12,16},{16,20},{20,24},{24,28},{28,32}... | collective-permute-start | bytes 49160 | tf_op jit(solution)/shard_map/ppermute | solution.py:414
  104.9 8.1 %collective-permute-start.7 = (f32[16,256]{1,0:T(8,128)S(1)}, f32[16,256]{1,0:T(8,128)S(1)}, u32[]{:S(2)}, u32[]{:S(2)}) collective-permute-start(f32[16,256]{1,0:T(8,128)S(1)} %get-tuple-element.74), channel_id=1, source_target_pairs={{504,0},{508,4},{0,8},{4,12},{8,16},{12,20},{16,24},{20,28},{24,32... | collective-permute-start | bytes 49160 | tf_op jit(solution)/shard_map/ppermute | solution.py:414

commit v4 on v3

--- a/solution.py
+++ b/solution.py
@@ -1,3 +1,5 @@
+import functools
+
 import jax
 import jax.numpy as jnp
 from jax import lax
@@ -8,7 +10,7 @@
 EPS = 1e-05
 BF = jnp.bfloat16
 F32 = jnp.float32
-BLOCK = 512
+BLOCK = 1536
 PATCH_SPLIT = (4, 8, 2, 2)
 PATCH = ("y", "zh", "zl", "c")
 INNER = ("y", "zl", "c", "rep")
@@ -73,17 +75,19 @@
     lax.fori_loop(0, total // BLOCK, step, 0)
 
 
-def seam_pick(send_ref, hop, table):
-    verts = table.shape[0]
-    slots = send_ref.shape[1]
-    pick = one_hot(send_ref[hop : hop + 1, :], (verts, slots), 0).astype(BF)
-    return t_dot(pick, table).astype(BF)
-
-
-def seam_spread(send_ref, hop, verts, rows):
-    slots = send_ref.shape[1]
-    pick = one_hot(send_ref[hop : hop + 1, :], (verts, slots), 0)
-    return jnp.dot(pick, rows, preferred_element_type=F32, precision=lax.Precision.HIGHEST)
+def seam_tables(send_ref, pick_ref, spread_ref):
+    hops, slots = send_ref.shape
+    wide, verts = pick_ref.shape
+    flat = jnp.concatenate([send_ref[hop : hop + 1, :] for hop in range(hops)], axis=1)
+    spread = one_hot(flat, (verts, wide), 0)
+    spread_ref[...] = jnp.concatenate([spread, spread], axis=1).astype(BF)
+    column = jnp.broadcast_to(flat, (8, wide)).T[:, 0:1]
+    pick_ref[...] = one_hot(column, (wide, verts), 1).astype(BF)
+
+
+def seam_spread(spread_ref, rows):
+    high, low = split(rows)
+    return dot(spread_ref[...], jnp.concatenate([high, low], axis=0))
 
 
 def load_kernel(
@@ -94,11 +98,13 @@
     edges_hbm,
     out0_ref,
     out1_ref,
-    send_ref,
     nodes_ref,
     ends_ref,
     ef_ref,
     edges_ref,
+    pick_ref,
+    spread_ref,
+    send_ref,
     sems,
 ):
     sources = (send_hbm, nodes_hbm, ends_hbm, ef_hbm, edges_hbm)
@@ -110,23 +116,32 @@
     for copy in copies:
         copy.start()
     copies[0].wait()
+    seam_tables(send_ref, pick_ref, spread_ref)
     copies[1].wait()
-    table = nodes_ref[...]
-    out0_ref[...] = seam_pick(send_ref, 0, table)
-    out1_ref[...] = seam_pick(send_ref, 1, table)
+    picked = dot(pick_ref[...], nodes_ref[...]).astype(BF)
+    slots = out0_ref.shape[0]
+    out0_ref[...] = picked[:slots]
+    out1_ref[...] = picked[slots:]
     for copy in copies[2:]:
         copy.wait()
 
 
 def load(sources):
     send, nodes = sources[:2]
+    wide = send.shape[0] * send.shape[1]
+    outs = [jax.ShapeDtypeStruct(x.shape, x.dtype) for x in sources[1:]]
+    outs.append(jax.ShapeDtypeStruct((wide, nodes.shape[0]), BF))
+    outs.append(jax.ShapeDtypeStruct((nodes.shape[0], 2 * wide), BF))
     seam = jax.ShapeDtypeStruct((send.shape[1], nodes.shape[1]), BF)
     return pl.pallas_call(
         load_kernel,
-        out_shape=[seam, seam] + [jax.ShapeDtypeStruct(x.shape, x.dtype) for x in sources],
+        out_shape=[seam, seam] + outs,
         in_specs=[pl.BlockSpec(memory_space=pltpu.HBM) for _ in sources],
-        out_specs=[pl.BlockSpec(memory_space=pltpu.VMEM) for _ in range(2 + len(sources))],
-        scratch_shapes=[pltpu.SemaphoreType.DMA((len(sources),))],
+        out_specs=[pl.BlockSpec(memory_space=pltpu.VMEM) for _ in range(2 + len(outs))],
+        scratch_shapes=[
+            pltpu.VMEM(send.shape, send.dtype),
+            pltpu.SemaphoreType.DMA((len(sources),)),
+        ],
         compiler_params=pltpu.CompilerParams(vmem_limit_bytes=24 * 2**20),
         cost_estimate=pl.CostEstimate(flops=10**8, transcendentals=0, bytes_accessed=10**6),
         name="load",
@@ -165,7 +180,22 @@
     loop(edges_ref.shape[0], body)
 
 
+def aggregate_kernel(count_ref, ends_ref, new_ref, agg_ref):
+    verts = agg_ref.shape[0]
+    count = count_ref[0]
+    agg_ref[...] = jnp.zeros_like(agg_ref)
+
+    def body(start):
+        first = live_row(ends_ref, 0, start, count)
+        second = live_row(ends_ref, 1, start, count)
+        spread = one_hot(first, (verts, BLOCK), 0) + one_hot(second, (verts, BLOCK), 0)
+        agg_ref[...] += dot(spread.astype(BF), new_ref[pl.ds(start, BLOCK), :])
+
+    loop(new_ref.shape[0], body)
+
+
 def edge_forward_kernel(
+    verts,
     count_ref,
     ends_ref,
     halo0_ref,
@@ -179,17 +209,15 @@
     hidden_ref,
     normed_ref,
     inv_ref,
-    agg_ref,
+    new_ref,
     back0_ref,
     back1_ref,
     seam_ref,
 ):
     features = edges_ref.shape[1]
-    verts = agg_ref.shape[0]
     slots = halo0_ref.shape[0]
     count = count_ref[0]
     halo = jnp.concatenate([halo0_ref[...], halo1_ref[...]], axis=0)
-    agg_ref[...] = jnp.zeros_like(agg_ref)
     seam_ref[...] = jnp.zeros_like(seam_ref)
 
     def body(start):
@@ -203,10 +231,8 @@
         normed_ref[rows, :] = normed
         inv_ref[rows, :] = inv
         new_edge = (edges_ref[rows, :].astype(F32) + normed).astype(BF)
-        first = live_row(ends_ref, 0, start, count)
+        new_ref[rows, :] = new_edge
         second = live_row(ends_ref, 1, start, count)
-        spread = one_hot(first, (verts, BLOCK), 0) + one_hot(second, (verts, BLOCK), 0)
-        agg_ref[...] += dot(spread.astype(BF), new_edge)
         away = one_hot(second - verts, (2 * slots, BLOCK), 0).astype(BF)
         seam_ref[...] += dot(away, new_edge)
 
@@ -216,7 +242,8 @@
 
 
 def node_kernel(
-    send_ref,
+    pick_ref,
+    spread_ref,
     nodes_ref,
     cot_ref,
     agg_ref,
@@ -234,9 +261,8 @@
     out1_ref,
 ):
     verts, features = nodes_ref.shape
-    total = agg_ref[...] + seam_spread(send_ref, 0, verts, got0_ref[...])
-    total = total + seam_spread(send_ref, 1, verts, got1_ref[...])
-    aggregate = total.astype(BF)
+    got = jnp.concatenate([got0_ref[...], got1_ref[...]], axis=0)
+    aggregate = (agg_ref[...] + seam_spread(spread_ref, got)).astype(BF)
     agg16_ref[...] = aggregate
     node_rows = nodes_ref[...]
     pre = dot(node_rows, nf_ref[:features, :]) + dot(aggregate, nf_ref[features:, :])
@@ -251,8 +277,10 @@
     dpre_ref[...] = d_pre
     d_agg = dot_t(d_pre, nf_ref[features:, :]).astype(BF)
     dagg_ref[...] = d_agg
-    out0_ref[...] = seam_pick(send_ref, 0, d_agg)
-    out1_ref[...] = seam_pick(send_ref, 1, d_agg)
+    picked = dot(pick_ref[...], d_agg).astype(BF)
+    slots = out0_ref.shape[0]
+    out0_ref[...] = picked[:slots]
+    out1_ref[...] = picked[slots:]
 
 
 def fill_kernel(
@@ -348,38 +376,32 @@
         pack_ref[total + begin : total + begin + size, :] = grad[:, half:]
 
     node_rows = nodes_ref[...]
-    first_high, first_low = split(first_ref[...])
-    second_high, second_low = split(second_ref[...])
-    far_high, far_low = split(seam_ref[...])
+    first = first_ref[...].astype(BF)
+    second = second_ref[...].astype(BF)
+    far = seam_ref[...].astype(BF)
     halo = jnp.concatenate([halo0_ref[...], halo1_ref[...]], axis=0)
     put(0, ge1_ref[...])
-    put(features, t_dot(node_rows, first_high) + t_dot(node_rows, first_low))
+    put(features, t_dot(node_rows, first))
     put(
         2 * features,
-        t_dot(node_rows, second_high)
-        + t_dot(node_rows, second_low)
-        + t_dot(halo, far_high)
-        + t_dot(halo, far_low),
+        t_dot(node_rows, second) + t_dot(halo, far),
     )
     put(3 * features, ges_ref[...])
     put(4 * features, nodegrad_ref[...])
     middle = ef_ref[features : 2 * features, :]
     last = ef_ref[2 * features :, :]
     partout_ref[...] = (
-        part_ref[...]
-        + (dot_t(first_high, middle) + dot_t(first_low, middle))
-        + (dot_t(second_high, last) + dot_t(second_low, last))
-    )
-
-
-def finish_kernel(send_ref, part_ref, got0_ref, got1_ref, ef_ref, out_ref):
-    verts, features = part_ref.shape
+        part_ref[...] + dot_t(first, middle) + dot_t(second, last)
+    )
+
+
+def finish_kernel(spread_ref, part_ref, got0_ref, got1_ref, ef_ref, out_ref):
+    features = part_ref.shape[1]
+    got = jnp.concatenate([got0_ref[...], got1_ref[...]], axis=0)
+    high, low = split(got)
     last = ef_ref[2 * features :, :]
-    total = part_ref[...]
-    for hop, ref in enumerate((got0_ref, got1_ref)):
-        high, low = split(ref[...])
-        total = total + seam_spread(send_ref, hop, verts, dot_t(high, last) + dot_t(low, last))
-    out_ref[...] = total.astype(BF)
+    ends = dot_t(high, last) + dot_t(low, last)
+    out_ref[...] = (part_ref[...] + seam_spread(spread_ref, ends)).astype(BF)
 
 
 def unpack_kernel(pack_ref, gef_ref, ges_ref, gnf_ref, gns_ref):
@@ -418,9 +440,11 @@
     return lax.axis_size(axes)
 
 
-def sum_kernel(pieces_ref, out_ref):
+def sum_kernel(pieces_ref, side0_ref, side1_ref, out_ref, pass0_ref, pass1_ref):
     count = pieces_ref.shape[0]
     copies = out_ref.shape[0]
+    pass0_ref[...] = side0_ref[...]
+    pass1_ref[...] = side1_ref[...]
     total = lax.fori_loop(
         1,
         count,
@@ -436,21 +460,32 @@
     lax.fori_loop(0, copies, store, 0, unroll=8)
 
 
-def sum_and_copy(pieces, copies, name):
-    (out,) = call(
-        sum_kernel, [((copies,) + pieces.shape[1:], BF)], (pieces,), flops=pieces.size, name=name
-    )
-    return out
-
-
-def sum_everywhere(pack):
+def sum_and_copy(pieces, side0, side1, copies, name):
+    return call(
+        sum_kernel,
+        [
+            ((copies,) + pieces.shape[1:], BF),
+            (side0.shape, side0.dtype),
+            (side1.shape, side1.dtype),
+        ],
+        (pieces, side0, side1),
+        flops=pieces.size,
+        name=name,
+    )
+
+
+def sum_everywhere(pack, back0, back1):
     inner = group_size(INNER)
     outer = group_size(OUTER)
     rows, lanes = pack.shape
     pieces = lax.all_to_all(pack.reshape(inner, rows // inner, lanes), INNER, 0, 0)
-    pieces = lax.all_to_all(sum_and_copy(pieces, outer, "inner_sum"), OUTER, 0, 0)
-    pieces = lax.all_to_all(sum_and_copy(pieces, inner, "outer_sum"), INNER, 0, 0)
-    return pieces.reshape(rows, lanes)
+    pieces, back0, back1 = sum_and_copy(pieces, back0, back1, outer, "inner_sum")
+    pieces = lax.all_to_all(pieces, OUTER, 0, 0)
+    got0 = shift(back0, 1)
+    got1 = shift(back1, 2)
+    pieces, got0, got1 = sum_and_copy(pieces, got0, got1, inner, "outer_sum")
+    pieces = lax.all_to_all(pieces, INNER, 0, 0)
+    return pieces.reshape(rows, lanes), got0, got1
 
 
 def local(
@@ -477,7 +512,7 @@
     seam32 = ((seam, features), F32)
     unit = 2 * features * features
 
-    out0, out1, send_rows, node_rows, ends, edge_first, edge_rows = load(
+    out0, out1, node_rows, ends, edge_first, edge_rows, pick, spread = load(
         (send_rows, node_rows, ends, edge_first, edge_rows)
     )
     halo0 = shift(out0, -1)
@@ -490,14 +525,14 @@
         flops=7 * slots * unit,
         name="edge_local",
     )
-    pre, hidden, normed, inv, agg, back0, back1 = call(
-        edge_forward_kernel,
+    pre, hidden, normed, inv, new_edge, back0, back1 = call(
+        functools.partial(edge_forward_kernel, verts),
         [
             ((slots, features), F32),
             ((slots, features), BF),
             ((slots, features), F32),
             ((slots, 1), F32),
-            ((verts, features), F32),
+            ((slots, features), BF),
             seam32,
             seam32,
         ],
@@ -510,10 +545,18 @@
     got0 = shift(back0, 1)
     got1 = shift(back1, 2)
     tall = (verts, features)
+    (agg,) = call(
+        aggregate_kernel,
+        [(tall, F32)],
+        (edge_count, ends, new_edge),
+        scalars=1,
+        flops=4 * slots * unit,
+        name="aggregate",
+    )
     new_nodes, agg16, node_hidden, d_out, d_pre, d_agg, out0, out1 = call(
         node_kernel,
         [(tall, BF)] * 6 + [seam16, seam16],
-        (send_rows, node_rows, cot, agg, got0, got1, node_first, node_second),
+        (pick, spread, node_rows, cot, agg, got0, got1, node_first, node_second),
         flops=8 * verts * unit,
         name="node",
     )
@@ -560,13 +603,11 @@
         flops=12 * slots * unit,
         name="edge_backward",
     )
-    got0 = shift(back0, 1)
-    got1 = shift(back1, 2)
-    pack = sum_everywhere(pack)
+    pack, got0, got1 = sum_everywhere(pack, back0, back1)
     (grad_nodes,) = call(
         finish_kernel,
         [(tall, BF)],
-        (send_rows, grad_part, got0, got1, edge_first),
+        (spread, grad_part, got0, got1, edge_first),
         flops=verts * unit,
         name="finish",
     )

time: 119 us -> 116 us (0.975)
  blocking collectives: 40.8 us -> 22.7 us
  waiting for transfers between devices: 14.4 us -> 26.3 us
  starting transfers between devices: 39.3 us -> 47.4 us
  Pallas kernels: 22.1 us -> 17.2 us
    all_to_all x1 -> x0, blocking collectives: 18.2 us -> none  [sum_everywhere(): lax.all_to_all(sum_and_copy(pieces, outer, 'inner_sum'), OUTER, 0, 0)]
    all_to_all x1 -> x2, waiting for transfers between devices: 1.26 us -> 16.3 us  [the longest x1 14.5 us: sum_everywhere(): pieces = lax.all_to_all(pieces, INNER, 0, 0)]
    pallas_call x9 -> x10, Pallas kernels: 20.7 us -> 15.8 us  [call(): pl.pallas_call(kernel, out_shape=[jax.ShapeDtypeStruct(shape, kind) for s...]
    all_to_all x1 -> x2, starting transfers between devices: 7.34 us -> 12.2 us  [the longest x1 7.34 us: sum_everywhere(): pieces = lax.all_to_all(pieces, INNER, 0, 0)]
    ppermute x8, starting transfers between devices: 32 us -> 35.2 us  [shift(): lax.ppermute(block, PATCH, [((i - distance) % count, i) for i in range(co...]
    ppermute x8, waiting for transfers between devices: 13.1 us -> 9.99 us  [shift(): lax.ppermute(block, PATCH, [((i - distance) % count, i) for i in range(co...]
  transfers between devices with their start and end apart: 9 -> 10, of which waited for: 5 -> 5; matrix products, arithmetic and copies ran while one was open for 0% -> 0% of each run, Pallas kernels for 6% -> 5%
where the time goes in v4:
time: 116 us; the launch traced here: 115 us
  starting transfers between devices  47.4 us (41%)
  waiting for transfers between devices  26.3 us (23%)
  blocking collectives  22.7 us (20%)
  Pallas kernels  17.2 us (15%)
  between operations  1.46 us (1%)
    ppermute x8, starting transfers between devices, shift(): lax.ppermute(block, PATCH, [((i - distance) % count, i) for i in range(co...  35.2 us
    all_to_all x1, blocking collectives, sum_everywhere(): lax.all_to_all(pack.reshape(inner, rows // inner, lanes), INNER, 0, 0)  22.7 us
    pallas_call x10, Pallas kernels, call(): pl.pallas_call(kernel, out_shape=[jax.ShapeDtypeStruct(shape, kind) for s...  15.8 us
    all_to_all x1, waiting for transfers between devices, sum_everywhere(): pieces = lax.all_to_all(pieces, INNER, 0, 0)  14.5 us
    ppermute x8, waiting for transfers between devices, shift(): lax.ppermute(block, PATCH, [((i - distance) % count, i) for i in range(co...  9.99 us
    all_to_all x1, starting transfers between devices, sum_everywhere(): pieces = lax.all_to_all(pieces, INNER, 0, 0)  7.34 us
    all_to_all x1, starting transfers between devices, sum_everywhere(): pieces = lax.all_to_all(pieces, OUTER, 0, 0)  4.82 us
  transfers between devices with their start and end apart: 10, of which 5 were waited for; matrix products, arithmetic and copies ran while one was open for 0% of the time, Pallas kernels for 5%

profile of v4, /device:TPU:1, one launch (start us, length us, event | category | flops | bytes accessed | tf_op | source)
XLA Modules:
  0.0 115.1 jit_solution(1328647600497499719)
XLA Ops:
  0.6 1.4 %load.1 = (bf16[16,256]{1,0:T(8,128)(2,1)S(1)}, bf16[16,256]{1,0:T(8,128)(2,1)S(1)}, bf16[512,256]{1,0:T(8,128)(2,1)S(1)}, s32[2,1536]{1,0:T(2,128)S(1)}, bf16[7...) custom-call(s32[2,16]{1,0:T(2,128)} %send_hbm.1, ...), custom_call_target="tpu_custom_call" | custom-call | flops 100000000 | bytes 1000000 | tf_op jit(solution)/shard_map/load/pallas_call | solution.py:136
  2.1 8.7 %collective-permute-start = (bf16[16,256]{1,0:T(8,128)(2,1)S(1)}, bf16[16,256]{1,0:T(8,128)(2,1)S(1)}, u32[]{:S(2)}, u32[]{:S(2)}) collective-permute-start(bf16[16,256]{1,0:T(8,128)(2,1)S(1)} %get-tuple-element.55), channel_id=1, source_target_pairs={{4,0},{8,4},{12,8},{16,12},{20,16},{24,20},{28,24},{32,28},{36,32}... | collective-permute-start | bytes 24584 | tf_op jit(solution)/shard_map/ppermute | solution.py:436
  10.8 8.2 %collective-permute-start.1 = (bf16[16,256]{1,0:T(8,128)(2,1)S(1)}, bf16[16,256]{1,0:T(8,128)(2,1)S(1)}, u32[]{:S(2)}, u32[]{:S(2)}) collective-permute-start(bf16[16,256]{1,0:T(8,128)(2,1)S(1)} %get-tuple-element.56), channel_id=1, source_target_pairs={{8,0},{12,4},{16,8},{20,12},{24,16},{28,20},{32,24},{36,28},{40,32... | collective-permute-start | bytes 24584 | tf_op jit(solution)/shard_map/ppermute | solution.py:436
  19.7 2.7 %edge_local.1 = (f32[1536,256]{1,0:T(8,128)S(1)}, bf16[1536,512]{1,0:T(8,128)(2,1)S(1)}, bf16[1536,32]{1,0:T(8,128)(2,1)S(1)}) custom-call(s32[1]{0:T(128)S(6)} %copy.17.count_ref, s32[2,1536]{1,0:T(2,128)S(1)} %get-tuple-element.54.ends_ref, bf16[512,256]{1,0:T(8,128)(2,1)S(1)} %get-tuple-element.53.nodes_ref, ...), custom_call_target="tpu_custom_call" | custom-call | flops 1409286144 | bytes 1409286 | tf_op jit(solution)/shard_map/edge_local/pallas_call | solution.py:419
  22.4 1.4 %edge_forward.1 = (f32[1536,256]{1,0:T(8,128)S(1)}, bf16[1536,256]{1,0:T(8,128)(2,1)S(1)}, f32[1536,256]{1,0:T(8,128)S(1)}, f32[1536,1]{1,0:T(8,128)S(1)}, bf16[...) custom-call(s32[1]{0:T(128)S(6)} %copy.17.count_ref, ...), custom_call_target="tpu_custom_call" | custom-call | flops 805306368 | bytes 805306 | tf_op jit(solution)/shard_map/edge_forward/pallas_call | solution.py:419
  23.8 3.4 %collective-permute-start.2 = (f32[16,256]{1,0:T(8,128)S(1)}, f32[16,256]{1,0:T(8,128)S(1)}, u32[]{:S(2)}, u32[]{:S(2)}) collective-permute-start(f32[16,256]{1,0:T(8,128)S(1)} %get-tuple-element.62), channel_id=1, source_target_pairs={{508,0},{0,4},{4,8},{8,12},{12,16},{16,20},{20,24},{24,28},{28,32}... | collective-permute-start | bytes 49160 | tf_op jit(solution)/shard_map/ppermute | solution.py:436
  27.2 1.9 %collective-permute-start.3 = (f32[16,256]{1,0:T(8,128)S(1)}, f32[16,256]{1,0:T(8,128)S(1)}, u32[]{:S(2)}, u32[]{:S(2)}) collective-permute-start(f32[16,256]{1,0:T(8,128)S(1)} %get-tuple-element.63), channel_id=1, source_target_pairs={{504,0},{508,4},{0,8},{4,12},{8,16},{12,20},{16,24},{20,28},{24,32... | collective-permute-start | bytes 49160 | tf_op jit(solution)/shard_map/ppermute | solution.py:436
  30.0 5.2 %collective-permute-done.3.got1_ref = f32[16,256]{1,0:T(8,128)S(1)} collective-permute-done((f32[16,256]{1,0:T(8,128)S(1)}, f32[16,256]{1,0:T(8,128)S(1)}, u32[]{:S(2)}, u32[]{:S(2)}) %collective-permute-start.3) | collective-permute-done | bytes 16416 | tf_op jit(solution)/shard_map/ppermute | solution.py:436
  35.2 2.0 %node.1 = (bf16[512,256]{1,0:T(8,128)(2,1)}, bf16[512,256]{1,0:T(8,128)(2,1)S(1)}, bf16[512,256]{1,0:T(8,128)(2,1)S(1)}, bf16[512,256]{1,0:T(8,128)(2,1)S(1)}, b...) custom-call(bf16[32,512]{1,0:T(8,128)(2,1)S(1)} %get-tuple-element.5, ...), custom_call_target="tpu_custom_call" | custom-call | flops 536870912 | bytes 536870 | tf_op jit(solution)/shard_map/node/pallas_call | solution.py:419
  37.2 2.3 %collective-permute-start.4 = (bf16[16,256]{1,0:T(8,128)(2,1)S(1)}, bf16[16,256]{1,0:T(8,128)(2,1)S(1)}, u32[]{:S(2)}, u32[]{:S(2)}) collective-permute-start(bf16[16,256]{1,0:T(8,128)(2,1)S(1)} %get-tuple-element.72), channel_id=1, source_target_pairs={{4,0},{8,4},{12,8},{16,12},{20,16},{24,20},{28,24},{32,28},{36,32}... | collective-permute-start | bytes 24584 | tf_op jit(solution)/shard_map/ppermute | solution.py:436
  39.5 2.1 %collective-permute-start.5 = (bf16[16,256]{1,0:T(8,128)(2,1)S(1)}, bf16[16,256]{1,0:T(8,128)(2,1)S(1)}, u32[]{:S(2)}, u32[]{:S(2)}) collective-permute-start(bf16[16,256]{1,0:T(8,128)(2,1)S(1)} %get-tuple-element.73), channel_id=1, source_target_pairs={{8,0},{12,4},{16,8},{20,12},{24,16},{28,20},{32,24},{36,28},{40,32... | collective-permute-start | bytes 24584 | tf_op jit(solution)/shard_map/ppermute | solution.py:436
  42.5 1.4 %collective-permute-done.5.dhalo1_ref = bf16[16,256]{1,0:T(8,128)(2,1)S(1)} collective-permute-done((bf16[16,256]{1,0:T(8,128)(2,1)S(1)}, bf16[16,256]{1,0:T(8,128)(2,1)S(1)}, u32[]{:S(2)}, u32[]{:S(2)}) %collective-permute-start.5) | collective-permute-done | bytes 8224 | tf_op jit(solution)/shard_map/ppermute | solution.py:436
  43.9 4.0 %edge_backward.1 = (bf16[1536,256]{1,0:T(8,128)(2,1)}, bf16[3584,128]{1,0:T(8,128)(2,1)S(1)}, f32[512,256]{1,0:T(8,128)S(1)}, f32[16,256]{1,0:T(8,128)S(1)}, f32[16,256]{1,0:T(8,128)S(1)}) custom-call(s32[1]{0:T(128)S(6)} %copy.17.count_ref, s32[2,1536]{1,0:T(2,128)S(1)} %get-tuple-element.54.ends_ref, bf16[512,256]{1,0:T(8,128)(2,1)S(1)} %get-tuple-element.53.nodes_ref, ...), custom_call_target="tpu_custom_call" | custom-call | flops 2415919104 | bytes 2415919 | tf_op jit(solution)/shard_map/edge_backward/pallas_call | solution.py:419
  47.9 22.7 %all_to_all.15.pieces_ref = bf16[64,56,128]{2,1,0:T(8,128)(2,1)S(1)} all-to-all(bf16[64,56,128]{2,1,0:T(8,128)(2,1)S(1)} %bitcast.10), channel_id=1, replica_groups=mesh['y'=4,'zh'=8,'zl'=2,'c'=2,'rep'=4] {'y','zl','c','rep'}, dimensions={0} | all-to-all | bytes 1835008 | tf_op jit(solution)/shard_map/all_to_all | solution.py:481
  71.3 4.8 %all-to-all-start.1 = ((bf16[8,56,128]{2,1,0:T(8,128)(2,1)}), bf16[8,56,128]{2,1,0:T(8,128)(2,1)S(1)}, u32[]{:S(2)}, u32[]{:S(2)}) async-start(bf16[8,56,128]{2,1,0:T(8,128)(2,1)} %get-tuple-element.84), calls=%async_computation.1 | async-start | bytes 229376 | tf_op jit(solution)/shard_map/all_to_all | solution.py:483
  76.2 3.7 %collective-permute-start.6 = (f32[16,256]{1,0:T(8,128)S(1)}, f32[16,256]{1,0:T(8,128)S(1)}, u32[]{:S(2)}, u32[]{:S(2)}) collective-permute-start(f32[16,256]{1,0:T(8,128)S(1)} %get-tuple-element.85), channel_id=1, source_target_pairs={{508,0},{0,4},{4,8},{8,12},{12,16},{16,20},{20,24},{24,28},{28,32}... | collective-permute-start | bytes 49160 | tf_op jit(solution)/shard_map/ppermute | solution.py:436
  79.9 4.8 %collective-permute-start.7 = (f32[16,256]{1,0:T(8,128)S(1)}, f32[16,256]{1,0:T(8,128)S(1)}, u32[]{:S(2)}, u32[]{:S(2)}) collective-permute-start(f32[16,256]{1,0:T(8,128)S(1)} %get-tuple-element.86), channel_id=1, source_target_pairs={{504,0},{508,4},{0,8},{4,12},{8,16},{12,20},{16,24},{20,28},{24,32... | collective-permute-start | bytes 49160 | tf_op jit(solution)/shard_map/ppermute | solution.py:436
  84.7 3.3 %collective-permute-done.7.side1_ref = f32[16,256]{1,0:T(8,128)S(1)} collective-permute-done((f32[16,256]{1,0:T(8,128)S(1)}, f32[16,256]{1,0:T(8,128)S(1)}, u32[]{:S(2)}, u32[]{:S(2)}) %collective-permute-start.7) | collective-permute-done | bytes 16416 | tf_op jit(solution)/shard_map/ppermute | solution.py:436
  88.1 1.8 %all-to-all-done.1.pieces_ref = bf16[8,56,128]{2,1,0:T(8,128)(2,1)S(1)} async-done(((bf16[8,56,128]{2,1,0:T(8,128)(2,1)}), bf16[8,56,128]{2,1,0:T(8,128)(2,1)S(1)}, u32[]{:S(2)}, u32[]{:S(2)}) %all-to-all-start.1) | async-done | bytes 114720 | tf_op jit(solution)/shard_map/all_to_all | solution.py:483
  89.9 1.0 outer_sum.1
  90.9 7.3 %all-to-all-start.2 = ((bf16[64,56,128]{2,1,0:T(8,128)(2,1)}), bf16[64,56,128]{2,1,0:T(8,128)(2,1)S(1)}, u32[]{:S(2)}, u32[]{:S(2)}) async-start(bf16[64,56,128]{2,1,0:T(8,128)(2,1)} %get-tuple-element.90), calls=%async_computation.2 | async-start | bytes 1835008 | tf_op jit(solution)/shard_map/all_to_all | solution.py:487
  98.3 1.2 %finish.1 = bf16[512,256]{1,0:T(8,128)(2,1)} custom-call(bf16[512,64]{1,0:T(8,128)(2,1)S(1)} %get-tuple-element.52.spread_ref, f32[512,256]{1,0:T(8,128)S(1)} %get-tuple-element.80.part_ref, f32[16,256]{1,0:T(8,128)S(1)} %get-tuple-element.87.got0_ref, f32[16,256]{1,0:T(8,128)S(1)} %get-tuple-element.88.got1_ref, bf16[768,256]{1,0:T(8,128)(2,1)S(1)} %get-tuple-element.58.ef_ref), custom_call_target="tpu_custom_call" | custom-call | flops 67108864 | bytes 67108 | tf_op jit(solution)/shard_map/finish/pallas_call | solution.py:419
  99.5 14.5 %all-to-all-done.2 = bf16[64,56,128]{2,1,0:T(8,128)(2,1)S(1)} async-done(((bf16[64,56,128]{2,1,0:T(8,128)(2,1)}), bf16[64,56,128]{2,1,0:T(8,128)(2,1)S(1)}, u32[]{:S(2)}, u32[]{:S(2)}) %all-to-all-start.2) | async-done | bytes 917536 | tf_op jit(solution)/shard_map/all_to_all | solution.py:487
  114.0 1.1 unpack.1
  (16 shorter events, 2.5 us)
Async XLA Ops:
  2.1 20.4 %collective-permute-start = (bf16[16,256]{1,0:T(8,128)(2,1)S(1)}, bf16[16,256]{1,0:T(8,128)(2,1)S(1)}, u32[]{:S(2)}, u32[]{:S(2)}) collective-permute-start(bf16[16,256]{1,0:T(8,128)(2,1)S(1)} %get-tuple-element.55), channel_id=1, source_target_pairs={{4,0},{8,4},{12,8},{16,12},{20,16},{24,20},{28,24},{32,28},{36,32}... | collective-permute-start | bytes 24584 | tf_op jit(solution)/shard_map/ppermute | solution.py:436
  10.8 11.6 %collective-permute-start.1 = (bf16[16,256]{1,0:T(8,128)(2,1)S(1)}, bf16[16,256]{1,0:T(8,128)(2,1)S(1)}, u32[]{:S(2)}, u32[]{:S(2)}) collective-permute-start(bf16[16,256]{1,0:T(8,128)(2,1)S(1)} %get-tuple-element.56), channel_id=1, source_target_pairs={{8,0},{12,4},{16,8},{20,12},{24,16},{28,20},{32,24},{36,28},{40,32... | collective-permute-start | bytes 24584 | tf_op jit(solution)/shard_map/ppermute | solution.py:436
  19.7 2.7 %copy-start = (bf16[256,256]{1,0:T(8,128)(2,1)S(1)}, bf16[256,256]{1,0:T(8,128)(2,1)}, u32[]{:S(2)}) copy-start(bf16[256,256]{1,0:T(8,128)(2,1)} %es_ref.3) | copy-start | bytes 393220
  23.8 11.4 %copy-start.1 = (bf16[1,512,256]{2,1,0:T(8,128)(2,1)S(1)}, bf16[1,512,256]{2,1,0:T(8,128)(2,1)}, u32[]{:S(2)}) copy-start(bf16[1,512,256]{2,1,0:T(8,128)(2,1)} %param.15) | copy-start | bytes 786436
  23.8 11.4 %copy-start.2 = (bf16[512,256]{1,0:T(8,128)(2,1)S(1)}, bf16[512,256]{1,0:T(8,128)(2,1)}, u32[]{:S(2)}) copy-start(bf16[512,256]{1,0:T(8,128)(2,1)} %nf_ref.3) | copy-start | bytes 786436
  23.8 11.4 %copy-start.3 = (bf16[256,256]{1,0:T(8,128)(2,1)S(1)}, bf16[256,256]{1,0:T(8,128)(2,1)}, u32[]{:S(2)}) copy-start(bf16[256,256]{1,0:T(8,128)(2,1)} %ns_ref.1) | copy-start | bytes 393220
  23.8 6.1 %collective-permute-start.2 = (f32[16,256]{1,0:T(8,128)S(1)}, f32[16,256]{1,0:T(8,128)S(1)}, u32[]{:S(2)}, u32[]{:S(2)}) collective-permute-start(f32[16,256]{1,0:T(8,128)S(1)} %get-tuple-element.62), channel_id=1, source_target_pairs={{508,0},{0,4},{4,8},{8,12},{12,16},{16,20},{20,24},{24,28},{28,32}... | collective-permute-start | bytes 49160 | tf_op jit(solution)/shard_map/ppermute | solution.py:436
  27.2 7.9 %collective-permute-start.3 = (f32[16,256]{1,0:T(8,128)S(1)}, f32[16,256]{1,0:T(8,128)S(1)}, u32[]{:S(2)}, u32[]{:S(2)}) collective-permute-start(f32[16,256]{1,0:T(8,128)S(1)} %get-tuple-element.63), channel_id=1, source_target_pairs={{504,0},{508,4},{0,8},{4,12},{8,16},{12,20},{16,24},{20,28},{24,32... | collective-permute-start | bytes 49160 | tf_op jit(solution)/shard_map/ppermute | solution.py:436
  37.2 5.3 %collective-permute-start.4 = (bf16[16,256]{1,0:T(8,128)(2,1)S(1)}, bf16[16,256]{1,0:T(8,128)(2,1)S(1)}, u32[]{:S(2)}, u32[]{:S(2)}) collective-permute-start(bf16[16,256]{1,0:T(8,128)(2,1)S(1)} %get-tuple-element.72), channel_id=1, source_target_pairs={{4,0},{8,4},{12,8},{16,12},{20,16},{24,20},{28,24},{32,28},{36,32}... | collective-permute-start | bytes 24584 | tf_op jit(solution)/shard_map/ppermute | solution.py:436
  39.5 4.4 %collective-permute-start.5 = (bf16[16,256]{1,0:T(8,128)(2,1)S(1)}, bf16[16,256]{1,0:T(8,128)(2,1)S(1)}, u32[]{:S(2)}, u32[]{:S(2)}) collective-permute-start(bf16[16,256]{1,0:T(8,128)(2,1)S(1)} %get-tuple-element.73), channel_id=1, source_target_pairs={{8,0},{12,4},{16,8},{20,12},{24,16},{28,20},{32,24},{36,28},{40,32... | collective-permute-start | bytes 24584 | tf_op jit(solution)/shard_map/ppermute | solution.py:436
  71.3 18.6 %all-to-all-start.1 = ((bf16[8,56,128]{2,1,0:T(8,128)(2,1)}), bf16[8,56,128]{2,1,0:T(8,128)(2,1)S(1)}, u32[]{:S(2)}, u32[]{:S(2)}) async-start(bf16[8,56,128]{2,1,0:T(8,128)(2,1)} %get-tuple-element.84), calls=%async_computation.1 | async-start | bytes 229376 | tf_op jit(solution)/shard_map/all_to_all | solution.py:483
  76.2 8.6 %collective-permute-start.6 = (f32[16,256]{1,0:T(8,128)S(1)}, f32[16,256]{1,0:T(8,128)S(1)}, u32[]{:S(2)}, u32[]{:S(2)}) collective-permute-start(f32[16,256]{1,0:T(8,128)S(1)} %get-tuple-element.85), channel_id=1, source_target_pairs={{508,0},{0,4},{4,8},{8,12},{12,16},{16,20},{20,24},{24,28},{28,32}... | collective-permute-start | bytes 49160 | tf_op jit(solution)/shard_map/ppermute | solution.py:436
  79.9 8.2 %collective-permute-start.7 = (f32[16,256]{1,0:T(8,128)S(1)}, f32[16,256]{1,0:T(8,128)S(1)}, u32[]{:S(2)}, u32[]{:S(2)}) collective-permute-start(f32[16,256]{1,0:T(8,128)S(1)} %get-tuple-element.86), channel_id=1, source_target_pairs={{504,0},{508,4},{0,8},{4,12},{8,16},{12,20},{16,24},{20,28},{24,32... | collective-permute-start | bytes 49160 | tf_op jit(solution)/shard_map/ppermute | solution.py:436
  90.9 23.1 %all-to-all-start.2 = ((bf16[64,56,128]{2,1,0:T(8,128)(2,1)}), bf16[64,56,128]{2,1,0:T(8,128)(2,1)S(1)}, u32[]{:S(2)}, u32[]{:S(2)}) async-start(bf16[64,56,128]{2,1,0:T(8,128)(2,1)} %get-tuple-element.90), calls=%async_computation.2 | async-start | bytes 1835008 | tf_op jit(solution)/shard_map/all_to_all | solution.py:487

commit v5 on v4

--- a/solution.py
+++ b/solution.py
@@ -13,7 +13,7 @@
 BLOCK = 1536
 PATCH_SPLIT = (4, 8, 2, 2)
 PATCH = ("y", "zh", "zl", "c")
-INNER = ("y", "zl", "c", "rep")
+INNER = ("y", "zl", "rep")
 OUTER = ("zh",)
 
 
@@ -313,6 +313,7 @@
 
 def edge_backward_kernel(
     count_ref,
+    core_ref,
     ends_ref,
     nodes_ref,
     halo0_ref,
@@ -331,7 +332,8 @@
     nodegrad_ref,
     part_ref,
     gedges_ref,
-    pack_ref,
+    keep_ref,
+    give_ref,
     partout_ref,
     back0_ref,
     back1_ref,
@@ -342,7 +344,6 @@
     ge1_ref,
 ):
     features = edges_ref.shape[1]
-    half = features // 2
     verts = nodes_ref.shape[0]
     slots = halo0_ref.shape[0]
     count = count_ref[0]
@@ -367,13 +368,16 @@
     loop(edges_ref.shape[0], body)
     back0_ref[...] = seam_ref[:slots, :]
     back1_ref[...] = seam_ref[slots:, :]
-    total = pack_ref.shape[0] // 2
+    half = features // 2
+    low_core = core_ref[0] == 0
 
     def put(begin, grad):
         grad = grad.astype(BF)
         size = grad.shape[0]
-        pack_ref[begin : begin + size, :] = grad[:, :half]
-        pack_ref[total + begin : total + begin + size, :] = grad[:, half:]
+        left = grad[:, :half]
+        right = grad[:, half:]
+        keep_ref[begin : begin + size, :] = jnp.where(low_core, left, right)
+        give_ref[begin : begin + size, :] = jnp.where(low_core, right, left)
 
     node_rows = nodes_ref[...]
     first = first_ref[...].astype(BF)
@@ -404,14 +408,16 @@
     out_ref[...] = (part_ref[...] + seam_spread(spread_ref, ends)).astype(BF)
 
 
-def unpack_kernel(pack_ref, gef_ref, ges_ref, gnf_ref, gns_ref):
-    total = pack_ref.shape[0] // 2
-    half = pack_ref.shape[1]
+def unpack_kernel(core_ref, mine_ref, other_ref, gef_ref, ges_ref, gnf_ref, gns_ref):
+    half = mine_ref.shape[1]
+    low_core = core_ref[0] == 0
     begin = 0
     for ref in (gef_ref, ges_ref, gnf_ref, gns_ref):
         size = ref.shape[0]
-        ref[:, :half] = pack_ref[begin : begin + size, :]
-        ref[:, half:] = pack_ref[total + begin : total + begin + size, :]
+        mine = mine_ref[begin : begin + size, :]
+        other = other_ref[begin : begin + size, :]
+        ref[:, :half] = jnp.where(low_core, mine, other)
+        ref[:, half:] = jnp.where(low_core, other, mine)
         begin += size
 
 
@@ -474,18 +480,30 @@
     )
 
 
-def sum_everywhere(pack, back0, back1):
+def add_kernel(keep_ref, got_ref, out_ref):
+    out_ref[...] = (keep_ref[...].astype(F32) + got_ref[...].astype(F32)).astype(BF)
+
+
+def swap_cores(block):
+    count = lax.axis_size("c")
+    return lax.ppermute(block, "c", [((i + 1) % count, i) for i in range(count)])
+
+
+def sum_everywhere(keep, give, back0, back1):
     inner = group_size(INNER)
     outer = group_size(OUTER)
-    rows, lanes = pack.shape
-    pieces = lax.all_to_all(pack.reshape(inner, rows // inner, lanes), INNER, 0, 0)
+    rows, lanes = keep.shape
+    (pair,) = call(
+        add_kernel, [(keep.shape, BF)], (keep, swap_cores(give)), flops=keep.size, name="core_sum"
+    )
+    pieces = lax.all_to_all(pair.reshape(inner, rows // inner, lanes), INNER, 0, 0)
     pieces, back0, back1 = sum_and_copy(pieces, back0, back1, outer, "inner_sum")
     pieces = lax.all_to_all(pieces, OUTER, 0, 0)
     got0 = shift(back0, 1)
     got1 = shift(back1, 2)
     pieces, got0, got1 = sum_and_copy(pieces, got0, got1, inner, "outer_sum")
-    pieces = lax.all_to_all(pieces, INNER, 0, 0)
-    return pieces.reshape(rows, lanes), got0, got1
+    mine = lax.all_to_all(pieces, INNER, 0, 0).reshape(rows, lanes)
+    return mine, swap_cores(mine), got0, got1
 
 
 def local(
@@ -508,6 +526,7 @@
     hops, seam = send_rows.shape
     assert hops == 2
     ends = edge_ends.T
+    core = lax.axis_index("c").astype(jnp.int32).reshape(1)
     seam16 = ((seam, features), BF)
     seam32 = ((seam, features), F32)
     unit = 2 * features * features
@@ -569,17 +588,19 @@
         flops=4 * slots * unit,
         name="fill",
     )
-    grad_edges, pack, grad_part, back0, back1 = call(
+    grad_edges, keep, give, grad_part, back0, back1 = call(
         edge_backward_kernel,
         [
             ((slots, features), BF),
-            ((2 * 7 * features, features // 2), BF),
+            ((7 * features, features // 2), BF),
+            ((7 * features, features // 2), BF),
             (tall, F32),
             seam32,
             seam32,
         ],
         (
             edge_count,
+            core,
             ends,
             node_rows,
             halo0,
@@ -598,12 +619,12 @@
             node_grads,
             grad_part,
         ),
-        scalars=1,
+        scalars=2,
         scratch=[tall, tall, (hops * seam, features), (features, features), (features, features)],
         flops=12 * slots * unit,
         name="edge_backward",
     )
-    pack, got0, got1 = sum_everywhere(pack, back0, back1)
+    mine, other, got0, got1 = sum_everywhere(keep, give, back0, back1)
     (grad_nodes,) = call(
         finish_kernel,
         [(tall, BF)],
@@ -619,7 +640,8 @@
             ((2 * features, features), BF),
             ((features, features), BF),
         ],
-        (pack,),
+        (core, mine, other),
+        scalars=1,
         flops=1000,
         name="unpack",
     )

time: 116 us -> 114 us (0.983)
  waiting for transfers between devices: 26.3 us -> 12.4 us
  blocking collectives: 22.7 us -> 28.5 us
  local copies, waits for them, and re-layouts: 0.02 us -> 3.24 us
  starting transfers between devices: 47.4 us -> 49.4 us
  Pallas kernels: 17.2 us -> 18.4 us
    all_to_all x1 -> x0, waiting for transfers between devices: 14.5 us -> none  [sum_everywhere(): pieces = lax.all_to_all(pieces, INNER, 0, 0)]
    ppermute x0 -> x2, starting transfers between devices: none -> 8.92 us  [swap_cores(): lax.ppermute(block, 'c', [((i + 1) % count, i) for i in range(count)])]
    all_to_all x1 -> x0, starting transfers between devices: 7.34 us -> none  [sum_everywhere(): pieces = lax.all_to_all(pieces, INNER, 0, 0)]
    all_to_all x1 -> x2, blocking collectives: 22.7 us -> 28.5 us  [the longest x1 14.4 us: sum_everywhere(): lax.all_to_all(pair.reshape(inner, rows // inner, lanes), INNER, 0, 0)]
    unnamed x8 -> x22, local copies, waits for them, and re-layouts: 0.02 us -> 3.24 us
    all_to_all x1, waiting for transfers between devices: 1.83 us -> 0.01 us  [sum_everywhere(): pieces = lax.all_to_all(pieces, OUTER, 0, 0)]
    ppermute x0 -> x2, waiting for transfers between devices: none -> 1.62 us  [swap_cores(): lax.ppermute(block, 'c', [((i + 1) % count, i) for i in range(count)])]
    pallas_call x10 -> x11, Pallas kernels: 15.8 us -> 16.3 us  [call(): pl.pallas_call(kernel, out_shape=[jax.ShapeDtypeStruct(shape, kind) for s...]
  transfers between devices with their start and end apart: 10 -> 11, of which waited for: 5 -> 5; matrix products, arithmetic and copies ran while one was open for 0% -> 0% of each run, Pallas kernels for 5% -> 5%
where the time goes in v5:
time: 114 us; the launch traced here: 113 us
  starting transfers between devices  49.4 us (43%)
  blocking collectives  28.5 us (25%)
  Pallas kernels  18.4 us (16%)
  waiting for transfers between devices  12.4 us (11%)
  local copies, waits for them, and re-layouts  3.24 us (3%)
  between operations  1.54 us (1%)
    ppermute x8, starting transfers between devices, shift(): lax.ppermute(block, PATCH, [((i - distance) % count, i) for i in range(co...  35.9 us
    pallas_call x11, Pallas kernels, call(): pl.pallas_call(kernel, out_shape=[jax.ShapeDtypeStruct(shape, kind) for s...  16.3 us
    all_to_all x1, blocking collectives, sum_everywhere(): lax.all_to_all(pair.reshape(inner, rows // inner, lanes), INNER, 0, 0)  14.4 us
    all_to_all x1, blocking collectives, sum_everywhere(): mine = lax.all_to_all(pieces, INNER, 0, 0).reshape(rows, lanes)  14.1 us
    ppermute x8, waiting for transfers between devices, shift(): lax.ppermute(block, PATCH, [((i - distance) % count, i) for i in range(co...  10.8 us
    ppermute x2, starting transfers between devices, swap_cores(): lax.ppermute(block, 'c', [((i + 1) % count, i) for i in range(count)])  8.92 us
    all_to_all x1, starting transfers between devices, sum_everywhere(): pieces = lax.all_to_all(pieces, OUTER, 0, 0)  4.62 us
    unnamed x22, local copies, waits for them, and re-layouts  3.24 us
  transfers between devices with their start and end apart: 11, of which 5 were waited for; matrix products, arithmetic and copies ran while one was open for 0% of the time, Pallas kernels for 5%

profile of v5, /device:TPU:1, one launch (start us, length us, event | category | flops | bytes accessed | tf_op | source)
XLA Modules:
  0.0 113.5 jit_solution(12874096152432942552)
XLA Ops:
  0.6 2.0 %load.1 = (bf16[16,256]{1,0:T(8,128)(2,1)}, bf16[16,256]{1,0:T(8,128)(2,1)}, bf16[512,256]{1,0:T(8,128)(2,1)S(1)}, s32[2,1536]{1,0:T(2,128)S(1)}, bf16[768,256]{...) custom-call(s32[2,16]{1,0:T(2,128)} %send_hbm.1, ...), custom_call_target="tpu_custom_call" | custom-call | flops 100000000 | bytes 1000000 | tf_op jit(solution)/shard_map/load/pallas_call | solution.py:136
  3.3 8.7 %collective-permute-start = (bf16[16,256]{1,0:T(8,128)(2,1)}, bf16[16,256]{1,0:T(8,128)(2,1)}, u32[]{:S(2)}, u32[]{:S(2)}) collective-permute-start(bf16[16,256]{1,0:T(8,128)(2,1)} %get-tuple-element.56), channel_id=1, source_target_pairs={{4,0},{8,4},{12,8},{16,12},{20,16},{24,20},{28,24},{32,28},{36,32}... | collective-permute-start | bytes 24584 | tf_op jit(solution)/shard_map/ppermute | solution.py:442
  12.0 8.2 %collective-permute-start.1 = (bf16[16,256]{1,0:T(8,128)(2,1)}, bf16[16,256]{1,0:T(8,128)(2,1)}, u32[]{:S(2)}, u32[]{:S(2)}) collective-permute-start(bf16[16,256]{1,0:T(8,128)(2,1)} %get-tuple-element.57), channel_id=1, source_target_pairs={{8,0},{12,4},{16,8},{20,12},{24,16},{28,20},{32,24},{36,28},{40,32... | collective-permute-start | bytes 24584 | tf_op jit(solution)/shard_map/ppermute | solution.py:442
  20.9 2.7 %edge_local.1 = (f32[1536,256]{1,0:T(8,128)S(1)}, bf16[1536,512]{1,0:T(8,128)(2,1)S(1)}, bf16[1536,32]{1,0:T(8,128)(2,1)S(1)}) custom-call(s32[1]{0:T(128)S(6)} %copy.17.count_ref, s32[2,1536]{1,0:T(2,128)S(1)} %get-tuple-element.55.ends_ref, bf16[512,256]{1,0:T(8,128)(2,1)S(1)} %get-tuple-element.54.nodes_ref, ...), custom_call_target="tpu_custom_call" | custom-call | flops 1409286144 | bytes 1409286 | tf_op jit(solution)/shard_map/edge_local/pallas_call | solution.py:425
  24.8 1.4 %copy-done.1 = f32[1536,256]{1,0:T(8,128)S(1)} copy-done((f32[1536,256]{1,0:T(8,128)S(1)}, f32[1536,256]{1,0:T(8,128)}, u32[]{:S(2)}) %copy-start.1) | copy-done | bytes 1572888
  26.2 2.1 %edge_forward.1 = (f32[1536,256]{1,0:T(8,128)S(1)}, bf16[1536,256]{1,0:T(8,128)(2,1)S(1)}, f32[1536,256]{1,0:T(8,128)S(1)}, f32[1536,1]{1,0:T(8,128)S(1)}, bf16[...) custom-call(s32[1]{0:T(128)S(6)} %copy.17.count_ref, ...), custom_call_target="tpu_custom_call" | custom-call | flops 805306368 | bytes 805306 | tf_op jit(solution)/shard_map/edge_forward/pallas_call | solution.py:425
  28.3 3.4 %collective-permute-start.2 = (f32[16,256]{1,0:T(8,128)S(1)}, f32[16,256]{1,0:T(8,128)S(1)}, u32[]{:S(2)}, u32[]{:S(2)}) collective-permute-start(f32[16,256]{1,0:T(8,128)S(1)} %get-tuple-element.63), channel_id=1, source_target_pairs={{508,0},{0,4},{4,8},{8,12},{12,16},{16,20},{20,24},{24,28},{28,32}... | collective-permute-start | bytes 49160 | tf_op jit(solution)/shard_map/ppermute | solution.py:442
  31.7 1.9 %collective-permute-start.3 = (f32[16,256]{1,0:T(8,128)S(1)}, f32[16,256]{1,0:T(8,128)S(1)}, u32[]{:S(2)}, u32[]{:S(2)}) collective-permute-start(f32[16,256]{1,0:T(8,128)S(1)} %get-tuple-element.64), channel_id=1, source_target_pairs={{504,0},{508,4},{0,8},{4,12},{8,16},{12,20},{16,24},{20,28},{24,32... | collective-permute-start | bytes 49160 | tf_op jit(solution)/shard_map/ppermute | solution.py:442
  34.5 5.2 %collective-permute-done.3.got1_ref = f32[16,256]{1,0:T(8,128)S(1)} collective-permute-done((f32[16,256]{1,0:T(8,128)S(1)}, f32[16,256]{1,0:T(8,128)S(1)}, u32[]{:S(2)}, u32[]{:S(2)}) %collective-permute-start.3) | collective-permute-done | bytes 16416 | tf_op jit(solution)/shard_map/ppermute | solution.py:442
  39.7 2.0 %node.1 = (bf16[512,256]{1,0:T(8,128)(2,1)}, bf16[512,256]{1,0:T(8,128)(2,1)S(1)}, bf16[512,256]{1,0:T(8,128)(2,1)S(1)}, bf16[512,256]{1,0:T(8,128)(2,1)S(1)}, b...) custom-call(bf16[32,512]{1,0:T(8,128)(2,1)S(1)} %copy-done.10, ...), custom_call_target="tpu_custom_call" | custom-call | flops 536870912 | bytes 536870 | tf_op jit(solution)/shard_map/node/pallas_call | solution.py:425
  41.7 2.3 %collective-permute-start.4 = (bf16[16,256]{1,0:T(8,128)(2,1)S(1)}, bf16[16,256]{1,0:T(8,128)(2,1)S(1)}, u32[]{:S(2)}, u32[]{:S(2)}) collective-permute-start(bf16[16,256]{1,0:T(8,128)(2,1)S(1)} %get-tuple-element.73), channel_id=1, source_target_pairs={{4,0},{8,4},{12,8},{16,12},{20,16},{24,20},{28,24},{32,28},{36,32}... | collective-permute-start | bytes 24584 | tf_op jit(solution)/shard_map/ppermute | solution.py:442
  44.0 2.1 %collective-permute-start.5 = (bf16[16,256]{1,0:T(8,128)(2,1)S(1)}, bf16[16,256]{1,0:T(8,128)(2,1)S(1)}, u32[]{:S(2)}, u32[]{:S(2)}) collective-permute-start(bf16[16,256]{1,0:T(8,128)(2,1)S(1)} %get-tuple-element.74), channel_id=1, source_target_pairs={{8,0},{12,4},{16,8},{20,12},{24,16},{28,20},{32,24},{36,28},{40,32... | collective-permute-start | bytes 24584 | tf_op jit(solution)/shard_map/ppermute | solution.py:442
  47.0 1.4 %collective-permute-done.5.dhalo1_ref = bf16[16,256]{1,0:T(8,128)(2,1)S(1)} collective-permute-done((bf16[16,256]{1,0:T(8,128)(2,1)S(1)}, bf16[16,256]{1,0:T(8,128)(2,1)S(1)}, u32[]{:S(2)}, u32[]{:S(2)}) %collective-permute-start.5) | collective-permute-done | bytes 8224 | tf_op jit(solution)/shard_map/ppermute | solution.py:442
  48.4 4.8 %edge_backward.1 = (bf16[1536,256]{1,0:T(8,128)(2,1)}, bf16[1792,128]{1,0:T(8,128)(2,1)S(1)}, bf16[1792,128]{1,0:T(8,128)(2,1)S(1)}, f32[512,256]{1,0:T(8,128)S(...) custom-call(s32[1]{0:T(128)S(6)} %copy.17.count_ref, s32[1]{0:T(128)} %bitcast.5.core_ref, ...), custom_call_target="tpu_custom_call" | custom-call | flops 2415919104 | bytes 2415919 | tf_op jit(solution)/shard_map/edge_backward/pallas_call | solution.py:425
  53.2 3.6 %collective-permute-start.6 = (bf16[1792,128]{1,0:T(8,128)(2,1)S(1)}, bf16[1792,128]{1,0:T(8,128)(2,1)S(1)}, u32[]{:S(2)}, u32[]{:S(2)}) collective-permute-start(bf16[1792,128]{1,0:T(8,128)(2,1)S(1)} %get-tuple-element.83), channel_id=1, source_target_pairs={{4,0},{0,4},{5,1},{1,5},{6,2},{2,6},{7,3},{3,7},{12,8},{8,12},{13,... | collective-permute-start | bytes 1376264 | tf_op jit(solution)/shard_map/ppermute | solution.py:489
  56.8 1.4 %collective-permute-done.6.got_ref = bf16[1792,128]{1,0:T(8,128)(2,1)S(1)} collective-permute-done((bf16[1792,128]{1,0:T(8,128)(2,1)S(1)}, bf16[1792,128]{1,0:T(8,128)(2,1)S(1)}, u32[]{:S(2)}, u32[]{:S(2)}) %collective-permute-start.6) | collective-permute-done | bytes 458784 | tf_op jit(solution)/shard_map/ppermute | solution.py:489
  58.4 14.4 %all_to_all.15.pieces_ref = bf16[32,56,128]{2,1,0:T(8,128)(2,1)S(1)} all-to-all(bf16[32,56,128]{2,1,0:T(8,128)(2,1)S(1)} %bitcast.12), channel_id=1, replica_groups=mesh['y'=4,'zh'=8,'zl'=2,'c'=2,'rep'=4] {'y','zl','rep'}, dimensions={0} | all-to-all | bytes 917504 | tf_op jit(solution)/shard_map/all_to_all | solution.py:499
  73.5 4.6 %all-to-all-start.1 = ((bf16[8,56,128]{2,1,0:T(8,128)(2,1)}), bf16[8,56,128]{2,1,0:T(8,128)(2,1)S(1)}, u32[]{:S(2)}, u32[]{:S(2)}) async-start(bf16[8,56,128]{2,1,0:T(8,128)(2,1)} %get-tuple-element.86), calls=%async_computation.1 | async-start | bytes 229376 | tf_op jit(solution)/shard_map/all_to_all | solution.py:501
  78.1 5.0 %collective-permute-start.7 = (f32[16,256]{1,0:T(8,128)S(1)}, f32[16,256]{1,0:T(8,128)S(1)}, u32[]{:S(2)}, u32[]{:S(2)}) collective-permute-start(f32[16,256]{1,0:T(8,128)S(1)} %get-tuple-element.87), channel_id=1, source_target_pairs={{508,0},{0,4},{4,8},{8,12},{12,16},{16,20},{20,24},{24,28},{28,32}... | collective-permute-start | bytes 49160 | tf_op jit(solution)/shard_map/ppermute | solution.py:442
  83.1 4.2 %collective-permute-start.8 = (f32[16,256]{1,0:T(8,128)S(1)}, f32[16,256]{1,0:T(8,128)S(1)}, u32[]{:S(2)}, u32[]{:S(2)}) collective-permute-start(f32[16,256]{1,0:T(8,128)S(1)} %get-tuple-element.88), channel_id=1, source_target_pairs={{504,0},{508,4},{0,8},{4,12},{8,16},{12,20},{16,24},{20,28},{24,32... | collective-permute-start | bytes 49160 | tf_op jit(solution)/shard_map/ppermute | solution.py:442
  87.4 4.2 %collective-permute-done.8.side1_ref = f32[16,256]{1,0:T(8,128)S(1)} collective-permute-done((f32[16,256]{1,0:T(8,128)S(1)}, f32[16,256]{1,0:T(8,128)S(1)}, u32[]{:S(2)}, u32[]{:S(2)}) %collective-permute-start.8) | collective-permute-done | bytes 16416 | tf_op jit(solution)/shard_map/ppermute | solution.py:442
  91.6 14.1 %all_to_all.16 = bf16[32,56,128]{2,1,0:T(8,128)(2,1)S(1)} all-to-all(bf16[32,56,128]{2,1,0:T(8,128)(2,1)S(1)} %get-tuple-element.92), channel_id=1, replica_groups=mesh['y'=4,'zh'=8,'zl'=2,'c'=2,'rep'=4] {'y','zl','rep'}, dimensions={0} | all-to-all | bytes 917504 | tf_op jit(solution)/shard_map/all_to_all | solution.py:505
  105.7 5.3 %collective-permute-start.9 = (bf16[1792,128]{1,0:T(8,128)(2,1)S(1)}, bf16[1792,128]{1,0:T(8,128)(2,1)S(1)}, u32[]{:S(2)}, u32[]{:S(2)}) collective-permute-start(bf16[1792,128]{1,0:T(8,128)(2,1)S(1)} %bitcast.10), channel_id=1, source_target_pairs={{4,0},{0,4},{5,1},{1,5},{6,2},{2,6},{7,3},{3,7},{12,8},{8,12},{13,... | collective-permute-start | bytes 1376264 | tf_op jit(solution)/shard_map/ppermute | solution.py:489
  111.0 1.2 %finish.1 = bf16[512,256]{1,0:T(8,128)(2,1)} custom-call(bf16[512,64]{1,0:T(8,128)(2,1)S(1)} %copy-done.7, f32[512,256]{1,0:T(8,128)S(1)} %get-tuple-element.81.part_ref, f32[16,256]{1,0:T(8,128)S(1)} %get-tuple-element.89.got0_ref, f32[16,256]{1,0:T(8,128)S(1)} %get-tuple-element.90.got1_ref, bf16[768,256]{1,0:T(8,128)(2,1)S(1)} %get-tuple-element.59.ef_ref), custom_call_target="tpu_custom_call" | custom-call | flops 67108864 | bytes 67108 | tf_op jit(solution)/shard_map/finish/pallas_call | solution.py:425
  (34 shorter events, 5.7 us)
Async XLA Ops:
  2.7 0.6 copy-start.9
  3.3 20.3 %copy-start.5 = (bf16[512,64]{1,0:T(8,128)(2,1)}, bf16[512,64]{1,0:T(8,128)(2,1)S(1)}, u32[]{:S(2)}) copy-start(bf16[512,64]{1,0:T(8,128)(2,1)S(1)} %get-tuple-element.53.spread_ref) | copy-start | bytes 196612
  3.3 21.5 %collective-permute-start = (bf16[16,256]{1,0:T(8,128)(2,1)}, bf16[16,256]{1,0:T(8,128)(2,1)}, u32[]{:S(2)}, u32[]{:S(2)}) collective-permute-start(bf16[16,256]{1,0:T(8,128)(2,1)} %get-tuple-element.56), channel_id=1, source_target_pairs={{4,0},{8,4},{12,8},{16,12},{20,16},{24,20},{28,24},{32,28},{36,32}... | collective-permute-start | bytes 24584 | tf_op jit(solution)/shard_map/ppermute | solution.py:442
  12.0 12.8 %collective-permute-start.1 = (bf16[16,256]{1,0:T(8,128)(2,1)}, bf16[16,256]{1,0:T(8,128)(2,1)}, u32[]{:S(2)}, u32[]{:S(2)}) collective-permute-start(bf16[16,256]{1,0:T(8,128)(2,1)} %get-tuple-element.57), channel_id=1, source_target_pairs={{8,0},{12,4},{16,8},{20,12},{24,16},{28,20},{32,24},{36,28},{40,32... | collective-permute-start | bytes 24584 | tf_op jit(solution)/shard_map/ppermute | solution.py:442
  20.9 3.9 %copy-start.2 = (bf16[256,256]{1,0:T(8,128)(2,1)S(1)}, bf16[256,256]{1,0:T(8,128)(2,1)}, u32[]{:S(2)}) copy-start(bf16[256,256]{1,0:T(8,128)(2,1)} %es_ref.3) | copy-start | bytes 393220
  23.6 1.2 %copy-start = (f32[1536,256]{1,0:T(8,128)}, f32[1536,256]{1,0:T(8,128)S(1)}, u32[]{:S(2)}) copy-start(f32[1536,256]{1,0:T(8,128)S(1)} %get-tuple-element.60.part_ref) | copy-start | bytes 4718596
  24.8 1.4 %copy-start.1 = (f32[1536,256]{1,0:T(8,128)S(1)}, f32[1536,256]{1,0:T(8,128)}, u32[]{:S(2)}) copy-start(f32[1536,256]{1,0:T(8,128)} %copy-done) | copy-start | bytes 4718596
  28.3 11.4 %copy-start.3 = (bf16[1,512,256]{2,1,0:T(8,128)(2,1)S(1)}, bf16[1,512,256]{2,1,0:T(8,128)(2,1)}, u32[]{:S(2)}) copy-start(bf16[1,512,256]{2,1,0:T(8,128)(2,1)} %param.15) | copy-start | bytes 786436
  28.3 11.4 %copy-start.4 = (bf16[512,256]{1,0:T(8,128)(2,1)S(1)}, bf16[512,256]{1,0:T(8,128)(2,1)}, u32[]{:S(2)}) copy-start(bf16[512,256]{1,0:T(8,128)(2,1)} %nf_ref.3) | copy-start | bytes 786436
  28.3 11.4 %copy-start.6 = (bf16[512,64]{1,0:T(8,128)(2,1)S(1)}, bf16[512,64]{1,0:T(8,128)(2,1)}, u32[]{:S(2)}) copy-start(bf16[512,64]{1,0:T(8,128)(2,1)} %copy-done.5) | copy-start | bytes 196612
  28.3 11.4 %copy-start.8 = (bf16[256,256]{1,0:T(8,128)(2,1)S(1)}, bf16[256,256]{1,0:T(8,128)(2,1)}, u32[]{:S(2)}) copy-start(bf16[256,256]{1,0:T(8,128)(2,1)} %ns_ref.1) | copy-start | bytes 393220
  28.3 11.4 %copy-start.10 = (bf16[32,512]{1,0:T(8,128)(2,1)S(1)}, bf16[32,512]{1,0:T(8,128)(2,1)}, u32[]{:S(2)}) copy-start(bf16[32,512]{1,0:T(8,128)(2,1)} %copy-done.9) | copy-start | bytes 98308
  28.3 6.1 %collective-permute-start.2 = (f32[16,256]{1,0:T(8,128)S(1)}, f32[16,256]{1,0:T(8,128)S(1)}, u32[]{:S(2)}, u32[]{:S(2)}) collective-permute-start(f32[16,256]{1,0:T(8,128)S(1)} %get-tuple-element.63), channel_id=1, source_target_pairs={{508,0},{0,4},{4,8},{8,12},{12,16},{16,20},{20,24},{24,28},{28,32}... | collective-permute-start | bytes 49160 | tf_op jit(solution)/shard_map/ppermute | solution.py:442
  31.7 7.9 %collective-permute-start.3 = (f32[16,256]{1,0:T(8,128)S(1)}, f32[16,256]{1,0:T(8,128)S(1)}, u32[]{:S(2)}, u32[]{:S(2)}) collective-permute-start(f32[16,256]{1,0:T(8,128)S(1)} %get-tuple-element.64), channel_id=1, source_target_pairs={{504,0},{508,4},{0,8},{4,12},{8,16},{12,20},{16,24},{20,28},{24,32... | collective-permute-start | bytes 49160 | tf_op jit(solution)/shard_map/ppermute | solution.py:442
  41.7 5.3 %collective-permute-start.4 = (bf16[16,256]{1,0:T(8,128)(2,1)S(1)}, bf16[16,256]{1,0:T(8,128)(2,1)S(1)}, u32[]{:S(2)}, u32[]{:S(2)}) collective-permute-start(bf16[16,256]{1,0:T(8,128)(2,1)S(1)} %get-tuple-element.73), channel_id=1, source_target_pairs={{4,0},{8,4},{12,8},{16,12},{20,16},{24,20},{28,24},{32,28},{36,32}... | collective-permute-start | bytes 24584 | tf_op jit(solution)/shard_map/ppermute | solution.py:442
  44.0 4.4 %collective-permute-start.5 = (bf16[16,256]{1,0:T(8,128)(2,1)S(1)}, bf16[16,256]{1,0:T(8,128)(2,1)S(1)}, u32[]{:S(2)}, u32[]{:S(2)}) collective-permute-start(bf16[16,256]{1,0:T(8,128)(2,1)S(1)} %get-tuple-element.74), channel_id=1, source_target_pairs={{8,0},{12,4},{16,8},{20,12},{24,16},{28,20},{32,24},{36,28},{40,32... | collective-permute-start | bytes 24584 | tf_op jit(solution)/shard_map/ppermute | solution.py:442
  53.2 5.0 %collective-permute-start.6 = (bf16[1792,128]{1,0:T(8,128)(2,1)S(1)}, bf16[1792,128]{1,0:T(8,128)(2,1)S(1)}, u32[]{:S(2)}, u32[]{:S(2)}) collective-permute-start(bf16[1792,128]{1,0:T(8,128)(2,1)S(1)} %get-tuple-element.83), channel_id=1, source_target_pairs={{4,0},{0,4},{5,1},{1,5},{6,2},{2,6},{7,3},{3,7},{12,8},{8,12},{13,... | collective-permute-start | bytes 1376264 | tf_op jit(solution)/shard_map/ppermute | solution.py:489
  58.3 52.7 %copy-start.7 = (bf16[512,64]{1,0:T(8,128)(2,1)S(1)}, bf16[512,64]{1,0:T(8,128)(2,1)}, u32[]{:S(2)}) copy-start(bf16[512,64]{1,0:T(8,128)(2,1)} %copy-done.5) | copy-start | bytes 196612
  73.5 18.0 %all-to-all-start.1 = ((bf16[8,56,128]{2,1,0:T(8,128)(2,1)}), bf16[8,56,128]{2,1,0:T(8,128)(2,1)S(1)}, u32[]{:S(2)}, u32[]{:S(2)}) async-start(bf16[8,56,128]{2,1,0:T(8,128)(2,1)} %get-tuple-element.86), calls=%async_computation.1 | async-start | bytes 229376 | tf_op jit(solution)/shard_map/all_to_all | solution.py:501
  78.1 9.3 %collective-permute-start.7 = (f32[16,256]{1,0:T(8,128)S(1)}, f32[16,256]{1,0:T(8,128)S(1)}, u32[]{:S(2)}, u32[]{:S(2)}) collective-permute-start(f32[16,256]{1,0:T(8,128)S(1)} %get-tuple-element.87), channel_id=1, source_target_pairs={{508,0},{0,4},{4,8},{8,12},{12,16},{16,20},{20,24},{24,28},{28,32}... | collective-permute-start | bytes 49160 | tf_op jit(solution)/shard_map/ppermute | solution.py:442
  83.1 8.4 %collective-permute-start.8 = (f32[16,256]{1,0:T(8,128)S(1)}, f32[16,256]{1,0:T(8,128)S(1)}, u32[]{:S(2)}, u32[]{:S(2)}) collective-permute-start(f32[16,256]{1,0:T(8,128)S(1)} %get-tuple-element.88), channel_id=1, source_target_pairs={{504,0},{508,4},{0,8},{4,12},{8,16},{12,20},{16,24},{20,28},{24,32... | collective-permute-start | bytes 49160 | tf_op jit(solution)/shard_map/ppermute | solution.py:442
  105.7 6.7 %collective-permute-start.9 = (bf16[1792,128]{1,0:T(8,128)(2,1)S(1)}, bf16[1792,128]{1,0:T(8,128)(2,1)S(1)}, u32[]{:S(2)}, u32[]{:S(2)}) collective-permute-start(bf16[1792,128]{1,0:T(8,128)(2,1)S(1)} %bitcast.10), channel_id=1, source_target_pairs={{4,0},{0,4},{5,1},{1,5},{6,2},{2,6},{7,3},{3,7},{12,8},{8,12},{13,... | collective-permute-start | bytes 1376264 | tf_op jit(solution)/shard_map/ppermute | solution.py:489

commit v6 on v5

--- a/solution.py
+++ b/solution.py
@@ -313,7 +313,6 @@
 
 def edge_backward_kernel(
     count_ref,
-    core_ref,
     ends_ref,
     nodes_ref,
     halo0_ref,
@@ -332,8 +331,7 @@
     nodegrad_ref,
     part_ref,
     gedges_ref,
-    keep_ref,
-    give_ref,
+    pack_ref,
     partout_ref,
     back0_ref,
     back1_ref,
@@ -369,15 +367,14 @@
     back0_ref[...] = seam_ref[:slots, :]
     back1_ref[...] = seam_ref[slots:, :]
     half = features // 2
-    low_core = core_ref[0] == 0
 
     def put(begin, grad):
         grad = grad.astype(BF)
         size = grad.shape[0]
         left = grad[:, :half]
         right = grad[:, half:]
-        keep_ref[begin : begin + size, :] = jnp.where(low_core, left, right)
-        give_ref[begin : begin + size, :] = jnp.where(low_core, right, left)
+        pack_ref[0, begin : begin + size, :] = left
+        pack_ref[1, begin : begin + size, :] = right
 
     node_rows = nodes_ref[...]
     first = first_ref[...].astype(BF)
@@ -480,8 +477,8 @@
     )
 
 
-def add_kernel(keep_ref, got_ref, out_ref):
-    out_ref[...] = (keep_ref[...].astype(F32) + got_ref[...].astype(F32)).astype(BF)
+def add_kernel(pieces_ref, out_ref):
+    out_ref[...] = (pieces_ref[0].astype(F32) + pieces_ref[1].astype(F32)).astype(BF)
 
 
 def swap_cores(block):
@@ -489,12 +486,16 @@
     return lax.ppermute(block, "c", [((i + 1) % count, i) for i in range(count)])
 
 
-def sum_everywhere(keep, give, back0, back1):
+def sum_everywhere(pack, back0, back1):
     inner = group_size(INNER)
     outer = group_size(OUTER)
-    rows, lanes = keep.shape
+    rows, lanes = pack.shape[1:]
     (pair,) = call(
-        add_kernel, [(keep.shape, BF)], (keep, swap_cores(give)), flops=keep.size, name="core_sum"
+        add_kernel,
+        [((rows, lanes), BF)],
+        (lax.all_to_all(pack, "c", 0, 0),),
+        flops=pack.size,
+        name="core_sum",
     )
     pieces = lax.all_to_all(pair.reshape(inner, rows // inner, lanes), INNER, 0, 0)
     pieces, back0, back1 = sum_and_copy(pieces, back0, back1, outer, "inner_sum")
@@ -588,19 +589,17 @@
         flops=4 * slots * unit,
         name="fill",
     )
-    grad_edges, keep, give, grad_part, back0, back1 = call(
+    grad_edges, pack, grad_part, back0, back1 = call(
         edge_backward_kernel,
         [
             ((slots, features), BF),
-            ((7 * features, features // 2), BF),
-            ((7 * features, features // 2), BF),
+            ((2, 7 * features, features // 2), BF),
             (tall, F32),
             seam32,
             seam32,
         ],
         (
             edge_count,
-            core,
             ends,
             node_rows,
             halo0,
@@ -619,12 +618,12 @@
             node_grads,
             grad_part,
         ),
-        scalars=2,
+        scalars=1,
         scratch=[tall, tall, (hops * seam, features), (features, features), (features, features)],
         flops=12 * slots * unit,
         name="edge_backward",
     )
-    mine, other, got0, got1 = sum_everywhere(keep, give, back0, back1)
+    mine, other, got0, got1 = sum_everywhere(pack, back0, back1)
     (grad_nodes,) = call(
         finish_kernel,
         [(tall, BF)],

time: 114 us -> 110 us (0.965)
  blocking collectives: 28.5 us -> 34.2 us
  starting transfers between devices: 49.4 us -> 46 us
  local copies, waits for them, and re-layouts: 3.24 us -> 0.02 us
  Pallas kernels: 18.4 us -> 16.3 us
  waiting for transfers between devices: 12.4 us -> 11 us
    all_to_all x0 -> x1, blocking collectives: none -> 5.8 us  [sum_everywhere(): lax.all_to_all(pack, 'c', 0, 0)]
    ppermute x2 -> x1, starting transfers between devices: 8.92 us -> 5.3 us  [swap_cores(): lax.ppermute(block, 'c', [((i + 1) % count, i) for i in range(count)])]
    unnamed x22 -> x8, local copies, waits for them, and re-layouts: 3.24 us -> 0.02 us
    pallas_call x11, Pallas kernels: 16.3 us -> 14.9 us  [call(): pl.pallas_call(kernel, out_shape=[jax.ShapeDtypeStruct(shape, kind) for s...]
    ppermute x2 -> x1, waiting for transfers between devices: 1.62 us -> 0.2 us  [swap_cores(): lax.ppermute(block, 'c', [((i + 1) % count, i) for i in range(count)])]
  transfers between devices with their start and end apart: 11 -> 10, of which waited for: 5 -> 4; matrix products, arithmetic and copies ran while one was open for 0% -> 0% of each run, Pallas kernels for 5% -> 5%
where the time goes in v6:
time: 110 us; the launch traced here: 109 us
  starting transfers between devices  46 us (42%)
  blocking collectives  34.2 us (31%)
  Pallas kernels  16.3 us (15%)
  waiting for transfers between devices  11 us (10%)
  between operations  1.47 us (1%)
    ppermute x8, starting transfers between devices, shift(): lax.ppermute(block, PATCH, [((i - distance) % count, i) for i in range(co...  35.9 us
    pallas_call x11, Pallas kernels, call(): pl.pallas_call(kernel, out_shape=[jax.ShapeDtypeStruct(shape, kind) for s...  14.9 us
    all_to_all x1, blocking collectives, sum_everywhere(): lax.all_to_all(pair.reshape(inner, rows // inner, lanes), INNER, 0, 0)  14.3 us
    all_to_all x1, blocking collectives, sum_everywhere(): mine = lax.all_to_all(pieces, INNER, 0, 0).reshape(rows, lanes)  14.1 us
    ppermute x8, waiting for transfers between devices, shift(): lax.ppermute(block, PATCH, [((i - distance) % count, i) for i in range(co...  10.8 us
    all_to_all x1, blocking collectives, sum_everywhere(): lax.all_to_all(pack, 'c', 0, 0)  5.8 us
    ppermute x1, starting transfers between devices, swap_cores(): lax.ppermute(block, 'c', [((i + 1) % count, i) for i in range(count)])  5.3 us
    all_to_all x1, starting transfers between devices, sum_everywhere(): pieces = lax.all_to_all(pieces, OUTER, 0, 0)  4.82 us
  transfers between devices with their start and end apart: 10, of which 4 were waited for; matrix products, arithmetic and copies ran while one was open for 0% of the time, Pallas kernels for 5%

profile of v6, /device:TPU:1, one launch (start us, length us, event | category | flops | bytes accessed | tf_op | source)
XLA Modules:
  0.0 109.0 jit_solution(16654756029546772655)
XLA Ops:
  0.6 1.4 %load.1 = (bf16[16,256]{1,0:T(8,128)(2,1)S(1)}, bf16[16,256]{1,0:T(8,128)(2,1)S(1)}, bf16[512,256]{1,0:T(8,128)(2,1)S(1)}, s32[2,1536]{1,0:T(2,128)S(1)}, bf16[7...) custom-call(s32[2,16]{1,0:T(2,128)} %send_hbm.1, ...), custom_call_target="tpu_custom_call" | custom-call | flops 100000000 | bytes 1000000 | tf_op jit(solution)/shard_map/load/pallas_call | solution.py:136
  2.1 8.7 %collective-permute-start = (bf16[16,256]{1,0:T(8,128)(2,1)S(1)}, bf16[16,256]{1,0:T(8,128)(2,1)S(1)}, u32[]{:S(2)}, u32[]{:S(2)}) collective-permute-start(bf16[16,256]{1,0:T(8,128)(2,1)S(1)} %get-tuple-element.55), channel_id=1, source_target_pairs={{4,0},{8,4},{12,8},{16,12},{20,16},{24,20},{28,24},{32,28},{36,32}... | collective-permute-start | bytes 24584 | tf_op jit(solution)/shard_map/ppermute | solution.py:439
  10.8 8.2 %collective-permute-start.1 = (bf16[16,256]{1,0:T(8,128)(2,1)S(1)}, bf16[16,256]{1,0:T(8,128)(2,1)S(1)}, u32[]{:S(2)}, u32[]{:S(2)}) collective-permute-start(bf16[16,256]{1,0:T(8,128)(2,1)S(1)} %get-tuple-element.56), channel_id=1, source_target_pairs={{8,0},{12,4},{16,8},{20,12},{24,16},{28,20},{32,24},{36,28},{40,32... | collective-permute-start | bytes 24584 | tf_op jit(solution)/shard_map/ppermute | solution.py:439
  19.7 2.7 %edge_local.1 = (f32[1536,256]{1,0:T(8,128)S(1)}, bf16[1536,512]{1,0:T(8,128)(2,1)S(1)}, bf16[1536,32]{1,0:T(8,128)(2,1)S(1)}) custom-call(s32[1]{0:T(128)S(6)} %copy.17.count_ref, s32[2,1536]{1,0:T(2,128)S(1)} %get-tuple-element.54.ends_ref, bf16[512,256]{1,0:T(8,128)(2,1)S(1)} %get-tuple-element.53.nodes_ref, ...), custom_call_target="tpu_custom_call" | custom-call | flops 1409286144 | bytes 1409286 | tf_op jit(solution)/shard_map/edge_local/pallas_call | solution.py:422
  22.4 1.4 %edge_forward.1 = (f32[1536,256]{1,0:T(8,128)S(1)}, bf16[1536,256]{1,0:T(8,128)(2,1)S(1)}, f32[1536,256]{1,0:T(8,128)S(1)}, f32[1536,1]{1,0:T(8,128)S(1)}, bf16[...) custom-call(s32[1]{0:T(128)S(6)} %copy.17.count_ref, ...), custom_call_target="tpu_custom_call" | custom-call | flops 805306368 | bytes 805306 | tf_op jit(solution)/shard_map/edge_forward/pallas_call | solution.py:422
  23.8 3.4 %collective-permute-start.2 = (f32[16,256]{1,0:T(8,128)S(1)}, f32[16,256]{1,0:T(8,128)S(1)}, u32[]{:S(2)}, u32[]{:S(2)}) collective-permute-start(f32[16,256]{1,0:T(8,128)S(1)} %get-tuple-element.62), channel_id=1, source_target_pairs={{508,0},{0,4},{4,8},{8,12},{12,16},{16,20},{20,24},{24,28},{28,32}... | collective-permute-start | bytes 49160 | tf_op jit(solution)/shard_map/ppermute | solution.py:439
  27.2 1.9 %collective-permute-start.3 = (f32[16,256]{1,0:T(8,128)S(1)}, f32[16,256]{1,0:T(8,128)S(1)}, u32[]{:S(2)}, u32[]{:S(2)}) collective-permute-start(f32[16,256]{1,0:T(8,128)S(1)} %get-tuple-element.63), channel_id=1, source_target_pairs={{504,0},{508,4},{0,8},{4,12},{8,16},{12,20},{16,24},{20,28},{24,32... | collective-permute-start | bytes 49160 | tf_op jit(solution)/shard_map/ppermute | solution.py:439
  30.0 5.2 %collective-permute-done.3.got1_ref = f32[16,256]{1,0:T(8,128)S(1)} collective-permute-done((f32[16,256]{1,0:T(8,128)S(1)}, f32[16,256]{1,0:T(8,128)S(1)}, u32[]{:S(2)}, u32[]{:S(2)}) %collective-permute-start.3) | collective-permute-done | bytes 16416 | tf_op jit(solution)/shard_map/ppermute | solution.py:439
  35.2 2.0 %node.1 = (bf16[512,256]{1,0:T(8,128)(2,1)}, bf16[512,256]{1,0:T(8,128)(2,1)S(1)}, bf16[512,256]{1,0:T(8,128)(2,1)S(1)}, bf16[512,256]{1,0:T(8,128)(2,1)S(1)}, b...) custom-call(bf16[32,512]{1,0:T(8,128)(2,1)S(1)} %get-tuple-element.5, ...), custom_call_target="tpu_custom_call" | custom-call | flops 536870912 | bytes 536870 | tf_op jit(solution)/shard_map/node/pallas_call | solution.py:422
  37.2 2.3 %collective-permute-start.4 = (bf16[16,256]{1,0:T(8,128)(2,1)S(1)}, bf16[16,256]{1,0:T(8,128)(2,1)S(1)}, u32[]{:S(2)}, u32[]{:S(2)}) collective-permute-start(bf16[16,256]{1,0:T(8,128)(2,1)S(1)} %get-tuple-element.72), channel_id=1, source_target_pairs={{4,0},{8,4},{12,8},{16,12},{20,16},{24,20},{28,24},{32,28},{36,32}... | collective-permute-start | bytes 24584 | tf_op jit(solution)/shard_map/ppermute | solution.py:439
  39.5 2.1 %collective-permute-start.5 = (bf16[16,256]{1,0:T(8,128)(2,1)S(1)}, bf16[16,256]{1,0:T(8,128)(2,1)S(1)}, u32[]{:S(2)}, u32[]{:S(2)}) collective-permute-start(bf16[16,256]{1,0:T(8,128)(2,1)S(1)} %get-tuple-element.73), channel_id=1, source_target_pairs={{8,0},{12,4},{16,8},{20,12},{24,16},{28,20},{32,24},{36,28},{40,32... | collective-permute-start | bytes 24584 | tf_op jit(solution)/shard_map/ppermute | solution.py:439
  41.6 0.9 fill.1
  42.5 1.4 %collective-permute-done.5.dhalo1_ref = bf16[16,256]{1,0:T(8,128)(2,1)S(1)} collective-permute-done((bf16[16,256]{1,0:T(8,128)(2,1)S(1)}, bf16[16,256]{1,0:T(8,128)(2,1)S(1)}, u32[]{:S(2)}, u32[]{:S(2)}) %collective-permute-start.5) | collective-permute-done | bytes 8224 | tf_op jit(solution)/shard_map/ppermute | solution.py:439
  43.9 4.0 %edge_backward.1 = (bf16[1536,256]{1,0:T(8,128)(2,1)}, bf16[2,1792,128]{2,1,0:T(8,128)(2,1)S(1)}, f32[512,256]{1,0:T(8,128)S(1)}, f32[16,256]{1,0:T(8,128)S(1)}, f32[16,256]{1,0:T(8,128)S(1)}) custom-call(s32[1]{0:T(128)S(6)} %copy.17.count_ref, s32[2,1536]{1,0:T(2,128)S(1)} %get-tuple-element.54.ends_ref, bf16[512,256]{1,0:T(8,128)(2,1)S(1)} %get-tuple-element.53.nodes_ref, ...), custom_call_target="tpu_custom_call" | custom-call | flops 2415919104 | bytes 2415919 | tf_op jit(solution)/shard_map/edge_backward/pallas_call | solution.py:422
  47.9 5.8 %all_to_all.20.pieces_ref = bf16[2,1792,128]{2,1,0:T(8,128)(2,1)S(1)} all-to-all(bf16[2,1792,128]{2,1,0:T(8,128)(2,1)S(1)} %get-tuple-element.81), channel_id=1, replica_groups=mesh['y'=4,'zh'=8,'zl'=2,'c'=2,'rep'=4] {'c'}, dimensions={0} | all-to-all | bytes 1835008 | tf_op jit(solution)/shard_map/all_to_all | solution.py:496
  53.8 14.3 %all_to_all.21.pieces_ref = bf16[32,56,128]{2,1,0:T(8,128)(2,1)S(1)} all-to-all(bf16[32,56,128]{2,1,0:T(8,128)(2,1)S(1)} %bitcast.12), channel_id=1, replica_groups=mesh['y'=4,'zh'=8,'zl'=2,'c'=2,'rep'=4] {'y','zl','rep'}, dimensions={0} | all-to-all | bytes 917504 | tf_op jit(solution)/shard_map/all_to_all | solution.py:500
  68.8 4.8 %all-to-all-start.2 = ((bf16[8,56,128]{2,1,0:T(8,128)(2,1)}), bf16[8,56,128]{2,1,0:T(8,128)(2,1)S(1)}, u32[]{:S(2)}, u32[]{:S(2)}) async-start(bf16[8,56,128]{2,1,0:T(8,128)(2,1)} %get-tuple-element.84), calls=%async_computation.2 | async-start | bytes 229376 | tf_op jit(solution)/shard_map/all_to_all | solution.py:502
  73.7 5.0 %collective-permute-start.6 = (f32[16,256]{1,0:T(8,128)S(1)}, f32[16,256]{1,0:T(8,128)S(1)}, u32[]{:S(2)}, u32[]{:S(2)}) collective-permute-start(f32[16,256]{1,0:T(8,128)S(1)} %get-tuple-element.85), channel_id=1, source_target_pairs={{508,0},{0,4},{4,8},{8,12},{12,16},{16,20},{20,24},{24,28},{28,32}... | collective-permute-start | bytes 49160 | tf_op jit(solution)/shard_map/ppermute | solution.py:439
  78.7 4.2 %collective-permute-start.7 = (f32[16,256]{1,0:T(8,128)S(1)}, f32[16,256]{1,0:T(8,128)S(1)}, u32[]{:S(2)}, u32[]{:S(2)}) collective-permute-start(f32[16,256]{1,0:T(8,128)S(1)} %get-tuple-element.86), channel_id=1, source_target_pairs={{504,0},{508,4},{0,8},{4,12},{8,16},{12,20},{16,24},{20,28},{24,32... | collective-permute-start | bytes 49160 | tf_op jit(solution)/shard_map/ppermute | solution.py:439
  82.9 4.2 %collective-permute-done.7.side1_ref = f32[16,256]{1,0:T(8,128)S(1)} collective-permute-done((f32[16,256]{1,0:T(8,128)S(1)}, f32[16,256]{1,0:T(8,128)S(1)}, u32[]{:S(2)}, u32[]{:S(2)}) %collective-permute-start.7) | collective-permute-done | bytes 16416 | tf_op jit(solution)/shard_map/ppermute | solution.py:439
  87.1 14.1 %all_to_all.22 = bf16[32,56,128]{2,1,0:T(8,128)(2,1)S(1)} all-to-all(bf16[32,56,128]{2,1,0:T(8,128)(2,1)S(1)} %get-tuple-element.90), channel_id=1, replica_groups=mesh['y'=4,'zh'=8,'zl'=2,'c'=2,'rep'=4] {'y','zl','rep'}, dimensions={0} | all-to-all | bytes 917504 | tf_op jit(solution)/shard_map/all_to_all | solution.py:506
  101.2 5.3 %collective-permute-start.8 = (bf16[1792,128]{1,0:T(8,128)(2,1)S(1)}, bf16[1792,128]{1,0:T(8,128)(2,1)S(1)}, u32[]{:S(2)}, u32[]{:S(2)}) collective-permute-start(bf16[1792,128]{1,0:T(8,128)(2,1)S(1)} %bitcast.10), channel_id=1, source_target_pairs={{4,0},{0,4},{5,1},{1,5},{6,2},{2,6},{7,3},{3,7},{12,8},{8,12},{13,... | collective-permute-start | bytes 1376264 | tf_op jit(solution)/shard_map/ppermute | solution.py:486
  106.5 1.2 %finish.1 = bf16[512,256]{1,0:T(8,128)(2,1)} custom-call(bf16[512,64]{1,0:T(8,128)(2,1)S(1)} %get-tuple-element.52.spread_ref, f32[512,256]{1,0:T(8,128)S(1)} %get-tuple-element.80.part_ref, f32[16,256]{1,0:T(8,128)S(1)} %get-tuple-element.87.got0_ref, f32[16,256]{1,0:T(8,128)S(1)} %get-tuple-element.88.got1_ref, bf16[768,256]{1,0:T(8,128)(2,1)S(1)} %get-tuple-element.58.ef_ref), custom_call_target="tpu_custom_call" | custom-call | flops 67108864 | bytes 67108 | tf_op jit(solution)/shard_map/finish/pallas_call | solution.py:422
  108.0 1.1 unpack.1
  (19 shorter events, 1.9 us)
Async XLA Ops:
  2.1 20.4 %collective-permute-start = (bf16[16,256]{1,0:T(8,128)(2,1)S(1)}, bf16[16,256]{1,0:T(8,128)(2,1)S(1)}, u32[]{:S(2)}, u32[]{:S(2)}) collective-permute-start(bf16[16,256]{1,0:T(8,128)(2,1)S(1)} %get-tuple-element.55), channel_id=1, source_target_pairs={{4,0},{8,4},{12,8},{16,12},{20,16},{24,20},{28,24},{32,28},{36,32}... | collective-permute-start | bytes 24584 | tf_op jit(solution)/shard_map/ppermute | solution.py:439
  10.8 11.6 %collective-permute-start.1 = (bf16[16,256]{1,0:T(8,128)(2,1)S(1)}, bf16[16,256]{1,0:T(8,128)(2,1)S(1)}, u32[]{:S(2)}, u32[]{:S(2)}) collective-permute-start(bf16[16,256]{1,0:T(8,128)(2,1)S(1)} %get-tuple-element.56), channel_id=1, source_target_pairs={{8,0},{12,4},{16,8},{20,12},{24,16},{28,20},{32,24},{36,28},{40,32... | collective-permute-start | bytes 24584 | tf_op jit(solution)/shard_map/ppermute | solution.py:439
  19.7 2.7 %copy-start = (bf16[256,256]{1,0:T(8,128)(2,1)S(1)}, bf16[256,256]{1,0:T(8,128)(2,1)}, u32[]{:S(2)}) copy-start(bf16[256,256]{1,0:T(8,128)(2,1)} %es_ref.3) | copy-start | bytes 393220
  23.8 11.4 %copy-start.1 = (bf16[1,512,256]{2,1,0:T(8,128)(2,1)S(1)}, bf16[1,512,256]{2,1,0:T(8,128)(2,1)}, u32[]{:S(2)}) copy-start(bf16[1,512,256]{2,1,0:T(8,128)(2,1)} %param.15) | copy-start | bytes 786436
  23.8 11.4 %copy-start.2 = (bf16[512,256]{1,0:T(8,128)(2,1)S(1)}, bf16[512,256]{1,0:T(8,128)(2,1)}, u32[]{:S(2)}) copy-start(bf16[512,256]{1,0:T(8,128)(2,1)} %nf_ref.3) | copy-start | bytes 786436
  23.8 11.4 %copy-start.3 = (bf16[256,256]{1,0:T(8,128)(2,1)S(1)}, bf16[256,256]{1,0:T(8,128)(2,1)}, u32[]{:S(2)}) copy-start(bf16[256,256]{1,0:T(8,128)(2,1)} %ns_ref.1) | copy-start | bytes 393220
  23.8 6.1 %collective-permute-start.2 = (f32[16,256]{1,0:T(8,128)S(1)}, f32[16,256]{1,0:T(8,128)S(1)}, u32[]{:S(2)}, u32[]{:S(2)}) collective-permute-start(f32[16,256]{1,0:T(8,128)S(1)} %get-tuple-element.62), channel_id=1, source_target_pairs={{508,0},{0,4},{4,8},{8,12},{12,16},{16,20},{20,24},{24,28},{28,32}... | collective-permute-start | bytes 49160 | tf_op jit(solution)/shard_map/ppermute | solution.py:439
  27.2 7.9 %collective-permute-start.3 = (f32[16,256]{1,0:T(8,128)S(1)}, f32[16,256]{1,0:T(8,128)S(1)}, u32[]{:S(2)}, u32[]{:S(2)}) collective-permute-start(f32[16,256]{1,0:T(8,128)S(1)} %get-tuple-element.63), channel_id=1, source_target_pairs={{504,0},{508,4},{0,8},{4,12},{8,16},{12,20},{16,24},{20,28},{24,32... | collective-permute-start | bytes 49160 | tf_op jit(solution)/shard_map/ppermute | solution.py:439
  37.2 5.3 %collective-permute-start.4 = (bf16[16,256]{1,0:T(8,128)(2,1)S(1)}, bf16[16,256]{1,0:T(8,128)(2,1)S(1)}, u32[]{:S(2)}, u32[]{:S(2)}) collective-permute-start(bf16[16,256]{1,0:T(8,128)(2,1)S(1)} %get-tuple-element.72), channel_id=1, source_target_pairs={{4,0},{8,4},{12,8},{16,12},{20,16},{24,20},{28,24},{32,28},{36,32}... | collective-permute-start | bytes 24584 | tf_op jit(solution)/shard_map/ppermute | solution.py:439
  39.5 4.4 %collective-permute-start.5 = (bf16[16,256]{1,0:T(8,128)(2,1)S(1)}, bf16[16,256]{1,0:T(8,128)(2,1)S(1)}, u32[]{:S(2)}, u32[]{:S(2)}) collective-permute-start(bf16[16,256]{1,0:T(8,128)(2,1)S(1)} %get-tuple-element.73), channel_id=1, source_target_pairs={{8,0},{12,4},{16,8},{20,12},{24,16},{28,20},{32,24},{36,28},{40,32... | collective-permute-start | bytes 24584 | tf_op jit(solution)/shard_map/ppermute | solution.py:439
  68.8 18.2 %all-to-all-start.2 = ((bf16[8,56,128]{2,1,0:T(8,128)(2,1)}), bf16[8,56,128]{2,1,0:T(8,128)(2,1)S(1)}, u32[]{:S(2)}, u32[]{:S(2)}) async-start(bf16[8,56,128]{2,1,0:T(8,128)(2,1)} %get-tuple-element.84), calls=%async_computation.2 | async-start | bytes 229376 | tf_op jit(solution)/shard_map/all_to_all | solution.py:502
  73.7 9.3 %collective-permute-start.6 = (f32[16,256]{1,0:T(8,128)S(1)}, f32[16,256]{1,0:T(8,128)S(1)}, u32[]{:S(2)}, u32[]{:S(2)}) collective-permute-start(f32[16,256]{1,0:T(8,128)S(1)} %get-tuple-element.85), channel_id=1, source_target_pairs={{508,0},{0,4},{4,8},{8,12},{12,16},{16,20},{20,24},{24,28},{28,32}... | collective-permute-start | bytes 49160 | tf_op jit(solution)/shard_map/ppermute | solution.py:439
  78.7 8.4 %collective-permute-start.7 = (f32[16,256]{1,0:T(8,128)S(1)}, f32[16,256]{1,0:T(8,128)S(1)}, u32[]{:S(2)}, u32[]{:S(2)}) collective-permute-start(f32[16,256]{1,0:T(8,128)S(1)} %get-tuple-element.86), channel_id=1, source_target_pairs={{504,0},{508,4},{0,8},{4,12},{8,16},{12,20},{16,24},{20,28},{24,32... | collective-permute-start | bytes 49160 | tf_op jit(solution)/shard_map/ppermute | solution.py:439
  101.2 6.7 %collective-permute-start.8 = (bf16[1792,128]{1,0:T(8,128)(2,1)S(1)}, bf16[1792,128]{1,0:T(8,128)(2,1)S(1)}, u32[]{:S(2)}, u32[]{:S(2)}) collective-permute-start(bf16[1792,128]{1,0:T(8,128)(2,1)S(1)} %bitcast.10), channel_id=1, source_target_pairs={{4,0},{0,4},{5,1},{1,5},{6,2},{2,6},{7,3},{3,7},{12,8},{8,12},{13,... | collective-permute-start | bytes 1376264 | tf_op jit(solution)/shard_map/ppermute | solution.py:486
